TPU v7x, 128 devices: a whole 4x4x4 slice. The times are simulated.
128 devices in a mesh: gx: 4 (over x), gy: 32 (over z, y, core).
Axes of the slice: x: 4, y: 4, z: 4, core: 2. Of those that a mesh axis runs over, the one named last changes fastest.
Arguments:
- schur_blocks: float32 [128, 2048, 2048], P(('gx', 'gy')), may hold values from -1 to 11, as said below
- offsets: int32 [128], P(('gx', 'gy')), may hold values from 256 to 768, as said below
- right_side: float32 [131072, 128], P(('gx', 'gy')), may hold values from -20 to 20
- coarse_basis: float32 [131072, 128], P(('gx', 'gy')), may hold values from -0.015625 to 0.015625
- coarse_load: float32 [128, 128], replicated, may hold values from -6 to 6
Outputs:
- multipliers: float32 [131072, 128], P(('gx', 'gy'))
- amplitudes: float32 [128, 128], replicated
Inputs may be any that keep to these rules, and one draw needn't show every extreme that they name: `schur_blocks`: each block is symmetric positive definite. `offsets`: both ends of the range are taken by some subdomain.
All inputs are finite; a program needn't handle non-finite values.
Results may differ from a plain program's by a relative error of at most 0.0003.
Values sent between devices are 32-bit elements; how exact they have to be, the bound alone decides.
No kernel may reach another device: no remote copies, remote signals or barrier semaphores. Data moves between devices by JAX's collectives and lax.ppermute only.
A program may use at most 128 MiB of HBM per device.

v0:
```python
import jax
import jax.numpy as jnp
from jax import lax
from jax.sharding import Mesh
from jax.sharding import PartitionSpec as P

ITERS = 3
GX_GY = ("gx", "gy_0", "gy_1", "gy_2")


HIGHEST = lax.Precision.HIGHEST


def extended_2(shard, sides, width):
    edges = {}
    for axis, dim in sides:
        peers, length = (lax.axis_size(axis), shard.shape[dim])
        up = [(i, (i + 1) % peers) for i in range(peers - 1)]
        last = lax.slice_in_dim(shard, length - width, length, axis=dim)
        initial = lax.slice_in_dim(shard, 0, width, axis=dim)
        edges[dim] = (
            lax.ppermute(last, axis, up),
            lax.ppermute(initial, axis, [(b, a) for a, b in up]),
        )
    done = []
    for _, dim in sides:
        low, high = edges[dim]
        around = [(width, width) if d in done else (0, 0) for d in range(shard.ndim)]
        shard = jnp.concatenate([jnp.pad(low, around), shard, jnp.pad(high, around)], axis=dim)
        done.append(dim)
    return shard


def cut_along(shard, dim, peers):
    shape = shard.shape
    pieces = shard.reshape(*shape[:dim], peers, shape[dim] // peers, *shape[dim + 1 :])
    return jnp.moveaxis(pieces, dim, 0)


def sum_at_owner(shard, axis, dim):
    peers = lax.axis_size(axis)
    pieces = lax.all_to_all(cut_along(shard, dim, peers), axis, 0, 0, tiled=True)
    return jnp.sum(pieces, axis=0)


def sum_in_two_steps(shard, axes, dim):
    far, near = axes
    own = sum_at_owner(cut_along(shard, dim, lax.axis_size(far)), near, dim + 1)
    return jnp.sum(lax.all_to_all(own, far, 0, 0, tiled=True), axis=0)


def filled_up(lines, peers):
    spare = -lines.shape[0] % peers
    if not spare:
        return lines
    return jnp.concatenate([lines, jnp.zeros((spare, *lines.shape[1:]), lines.dtype)])


def sent_to_all(shard, axis):
    copies = jnp.broadcast_to(shard, (lax.axis_size(axis), *shard.shape))
    return lax.all_to_all(copies, axis, split_axis=0, concat_axis=0, tiled=True)


def in_order(pieces, dim):
    shape = list(pieces.shape[1:])
    shape[dim] *= pieces.shape[0]
    return jnp.moveaxis(pieces, 0, dim).reshape(shape)


def gathered_by_axis(shard, axes, dim):
    far, near = axes
    initial = sent_to_all(shard, far)
    pieces = jnp.swapaxes(sent_to_all(initial, near), 0, 1)
    return in_order(pieces.reshape(-1, *shard.shape), dim)


def nested_sum(shard, axes):
    lines = shard.reshape(-1, shard.shape[-1])
    own = sum_in_two_steps(
        filled_up(lines, lax.axis_size(axes[0]) * lax.axis_size(axes[1])), axes, 0
    )
    whole = gathered_by_axis(own, axes, 0)
    return whole[: len(lines)].reshape(shard.shape)


def taken_together(shard, axis):
    everything = sent_to_all(shard, axis)
    return jnp.sum(everything, axis=0)


def over_axes(shard, axes):
    far, near = axes
    nearer = taken_together(shard, near)
    return taken_together(nearer, far)


def apply_local(vector, schur_block, start_row):
    slab_rows = vector.shape[0]
    window_rows = schur_block.shape[0]
    reach_rows = 3 * slab_rows // 4
    skip_rows = slab_rows - reach_rows
    extended = extended_2(vector, ((GX_GY, 0),), reach_rows)
    first_row = start_row - skip_rows
    window = lax.dynamic_slice_in_dim(extended, first_row, window_rows, 0)
    product_block = jnp.dot(
        schur_block, window, precision=HIGHEST, preferred_element_type=jnp.float32
    )
    spread = jnp.zeros((3 * slab_rows, vector.shape[1]), jnp.float32)
    spread = lax.dynamic_update_slice_in_dim(spread, product_block, start_row, 0)
    to_left = spread[:slab_rows]
    own_part = spread[slab_rows : 2 * slab_rows]
    to_right = spread[2 * slab_rows :]
    packed = jnp.concatenate([to_left, to_right], axis=0)
    arrived = extended_2(packed, ((GX_GY, 0),), slab_rows)
    result = own_part + arrived[:slab_rows] + arrived[3 * slab_rows :]
    return result


def project_sum(residual, coarse_basis, gram_factor):
    local_coarse = jnp.dot(
        coarse_basis.T, residual, precision=HIGHEST, preferred_element_type=jnp.float32
    )
    coarse_part = nested_sum(local_coarse, (("gx", "gy_0", "gy_1"), "gy_2"))
    amplitudes = jax.scipy.linalg.cho_solve((gram_factor, True), coarse_part)
    projected = residual - jnp.dot(
        coarse_basis, amplitudes, precision=HIGHEST, preferred_element_type=jnp.float32
    )
    energy = over_axes(jnp.sum(projected * projected, axis=0), (("gx", "gy_0", "gy_1"), "gy_2"))
    return (projected, amplitudes, energy)


def local(schur_blocks, offsets, right_side, coarse_basis, coarse_load):
    schur_block = schur_blocks[0]
    start_row = offsets[0]
    local_gram = jnp.dot(
        coarse_basis.T, coarse_basis, precision=HIGHEST, preferred_element_type=jnp.float32
    )
    gram_matrix = nested_sum(local_gram, (("gx", "gy_0", "gy_1"), "gy_2"))
    gram_factor = jnp.linalg.cholesky(gram_matrix)
    start_load = jax.scipy.linalg.cho_solve((gram_factor, True), coarse_load)
    multipliers = jnp.dot(
        coarse_basis, start_load, precision=HIGHEST, preferred_element_type=jnp.float32
    )
    residual = right_side - apply_local(multipliers, schur_block, start_row)
    projected, amplitudes, energy_now = project_sum(residual, coarse_basis, gram_factor)
    direction = projected
    for iteration in range(ITERS):
        operator_image = apply_local(direction, schur_block, start_row)
        curvature = over_axes(
            jnp.sum(direction * operator_image, axis=0), (("gx", "gy_0", "gy_1"), "gy_2")
        )
        step_length = energy_now / curvature
        multipliers = multipliers + step_length * direction
        residual = residual - step_length * operator_image
        projected, amplitudes, energy_next = project_sum(residual, coarse_basis, gram_factor)
        direction = projected + energy_next / energy_now * direction
        energy_now = energy_next
    return (multipliers, amplitudes)


def solution(mesh):
    split = Mesh(mesh.devices.reshape(mesh.shape["gx"], 4, 4, 2), ("gx", "gy_0", "gy_1", "gy_2"))
    in_specs = (P(GX_GY, None, None), P(GX_GY), P(GX_GY, None), P(GX_GY, None), P())
    out_specs = (P(GX_GY, None), P())
    return jax.shard_map(local, mesh=split, in_specs=in_specs, out_specs=out_specs, check_vma=False)
```

profile of v0, /device:TPU:1, one launch (start us, length us, event | category | flops | bytes accessed | tf_op | source)
XLA Modules:
  0.0 609.1 jit_solution(10132944279101455514)
XLA Ops:
  9.1 19.5 %all_to_all.203 = f32[64,1,128]{2,1,0:T(1,128)S(1)} all-to-all(f32[64,1,128]{2,1,0:T(1,128)S(1)} %bitcast.188), channel_id=1, replica_groups=mesh['gx'=4,'gy_0'=4,'gy_1'=4,'gy_2'=2] {'gx','gy_0','gy_1'}, dimensions={0} | all-to-all | bytes 65536 | tf_op jit(solution)/shard_map/all_to_all | solution.py:49
  28.6 12.9 %all_to_all.187 = f32[64,1,128]{2,1,0:T(1,128)S(1)} all-to-all(f32[64,1,128]{2,1,0:T(1,128)S(1)} %broadcast_in_dim.76), channel_id=1, replica_groups=mesh['gx'=4,'gy_0'=4,'gy_1'=4,'gy_2'=2] {'gx','gy_0','gy_1'}, dimensions={0} | all-to-all | bytes 65536 | tf_op jit(solution)/shard_map/all_to_all | solution.py:61
  41.6 6.6 %all_to_all.188 = f32[2,64,1,128]{3,1,2,0:T(8,128)S(1)} all-to-all(f32[2,64,1,128]{3,1,2,0:T(8,128)S(1)} %broadcast_in_dim.77), channel_id=1, replica_groups=mesh['gx'=4,'gy_0'=4,'gy_1'=4,'gy_2'=2] {'gy_2'}, dimensions={0} | all-to-all | bytes 131072 | tf_op jit(solution)/shard_map/all_to_all | solution.py:61
  48.4 11.7 %cholesky.18 = f32[128,128]{1,0:T(8,128)S(1)} custom-call(f32[128,128]{1,0:T(8,128)S(1)} %fusion.65), custom_call_target="Cholesky" | custom-call | tf_op jit(solution)/shard_map/jit(cholesky)/cholesky | solution.py:139
  61.4 9.8 %custom-call.12 = f32[1,128,128]{1,2,0:T(8,128)S(1)} custom-call(f32[1,128,128]{2,1,0:T(8,128)S(1)} %fusion.44), custom_call_target="InvertDiagBlocksLowerTriangular" | custom-call | tf_op jit(solution)/shard_map/jit(_cho_solve)/triangular_solve | solution.py:140
  84.0 20.9 %fusion.8 = f32[2048,128]{0,1:T(8,128)} fusion(f32[1,2048,2048]{2,1,0:T(8,128)} %param.7, s32[]{:T(128)S(6)} %select_n.9, f32[768,128]{0,1:T(8,128)S(1)} %collective-permute-done, f32[1024,128]{0,1:T(8,128)S(1)} %convolution_bitcast_fusion.3, f32[768,128]{0,1:T(8,128)S(1)} %collective-permute-done.1), kind=kOutput, calls=%fused_computation.8 | convolution fusion | flops 6442975232 | bytes 19136516 | tf_op jit(solution)/shard_map/dot_general | solution.py:105
  105.0 5.3 dynamic_update_slice.12
  130.2 25.0 %all_to_all.204 = f32[64,1,128]{2,1,0:T(1,128)S(1)} all-to-all(f32[64,1,128]{2,1,0:T(1,128)S(1)} %bitcast.190), channel_id=1, replica_groups=mesh['gx'=4,'gy_0'=4,'gy_1'=4,'gy_2'=2] {'gx','gy_0','gy_1'}, dimensions={0} | all-to-all | bytes 65536 | tf_op jit(solution)/shard_map/all_to_all | solution.py:49
  155.4 12.9 %all_to_all.190 = f32[64,1,128]{2,1,0:T(1,128)S(1)} all-to-all(f32[64,1,128]{2,1,0:T(1,128)S(1)} %broadcast_in_dim.78), channel_id=1, replica_groups=mesh['gx'=4,'gy_0'=4,'gy_1'=4,'gy_2'=2] {'gx','gy_0','gy_1'}, dimensions={0} | all-to-all | bytes 65536 | tf_op jit(solution)/shard_map/all_to_all | solution.py:61
  168.3 6.6 %all_to_all.191 = f32[2,64,1,128]{3,1,2,0:T(8,128)S(1)} all-to-all(f32[2,64,1,128]{3,1,2,0:T(8,128)S(1)} %broadcast_in_dim.79), channel_id=1, replica_groups=mesh['gx'=4,'gy_0'=4,'gy_1'=4,'gy_2'=2] {'gy_2'}, dimensions={0} | all-to-all | bytes 131072 | tf_op jit(solution)/shard_map/all_to_all | solution.py:61
  187.8 20.9 %fusion.11 = f32[2048,128]{0,1:T(8,128)} fusion(f32[1,2048,2048]{2,1,0:T(8,128)} %param.7, s32[]{:T(128)S(6)} %select_n.9, f32[768,128]{0,1:T(8,128)S(1)} %collective-permute-done.4, f32[1024,128]{0,1:T(8,128)S(1)} %fusion.20, f32[768,128]{0,1:T(8,128)S(1)} %collective-permute-done.5), kind=kOutput, calls=%fused_computation.9 | convolution fusion | flops 6442975232 | bytes 19136516 | tf_op jit(solution)/shard_map/dot_general | solution.py:105
  236.4 16.8 %all-to-all-start.9 = ((f32[64,1,128]{2,1,0:T(1,128)}), f32[64,1,128]{2,1,0:T(1,128)S(1)}, u32[]{:S(2)}, u32[]{:S(2)}) async-start(f32[64,1,128]{2,1,0:T(1,128)} %broadcast_in_dim.81), calls=%async_computation.9 | async-start | bytes 65536 | tf_op jit(solution)/shard_map/all_to_all | solution.py:61
  253.2 8.3 %all-to-all-done.9 = f32[64,1,128]{2,1,0:T(1,128)S(1)} async-done(((f32[64,1,128]{2,1,0:T(1,128)}), f32[64,1,128]{2,1,0:T(1,128)S(1)}, u32[]{:S(2)}, u32[]{:S(2)}) %all-to-all-start.9) | async-done | bytes 32800 | tf_op jit(solution)/shard_map/all_to_all | solution.py:61
  266.9 8.3 %all-to-all-done.11 = f32[64,1,128]{2,1,0:T(1,128)S(1)} async-done(((f32[64,1,128]{2,1,0:T(1,128)}), f32[64,1,128]{2,1,0:T(1,128)S(1)}, u32[]{:S(2)}, u32[]{:S(2)}) %all-to-all-start.11) | async-done | bytes 32800 | tf_op jit(solution)/shard_map/all_to_all | solution.py:61
  278.6 6.8 %all_to_all.193 = f32[2,64,1,128]{3,1,2,0:T(8,128)S(1)} all-to-all(f32[2,64,1,128]{3,1,2,0:T(8,128)S(1)} %bitcast.181), channel_id=1, replica_groups=mesh['gx'=4,'gy_0'=4,'gy_1'=4,'gy_2'=2] {'gy_2'}, dimensions={0} | all-to-all | bytes 131072 | tf_op jit(solution)/shard_map/all_to_all | solution.py:42
  285.4 12.9 %all_to_all.205 = f32[64,1,128]{2,1,0:T(1,128)S(1)} all-to-all(f32[64,1,128]{2,1,0:T(1,128)S(1)} %bitcast.192), channel_id=1, replica_groups=mesh['gx'=4,'gy_0'=4,'gy_1'=4,'gy_2'=2] {'gx','gy_0','gy_1'}, dimensions={0} | all-to-all | bytes 65536 | tf_op jit(solution)/shard_map/all_to_all | solution.py:49
  298.4 12.9 %all_to_all.206 = f32[64,1,128]{2,1,0:T(1,128)S(1)} all-to-all(f32[64,1,128]{2,1,0:T(1,128)S(1)} %broadcast_in_dim.84), channel_id=1, replica_groups=mesh['gx'=4,'gy_0'=4,'gy_1'=4,'gy_2'=2] {'gx','gy_0','gy_1'}, dimensions={0} | all-to-all | bytes 65536 | tf_op jit(solution)/shard_map/all_to_all | solution.py:61
  311.3 6.6 %all_to_all.194 = f32[2,64,1,128]{3,1,2,0:T(8,128)S(1)} all-to-all(f32[2,64,1,128]{3,1,2,0:T(8,128)S(1)} %broadcast_in_dim.85), channel_id=1, replica_groups=mesh['gx'=4,'gy_0'=4,'gy_1'=4,'gy_2'=2] {'gy_2'}, dimensions={0} | all-to-all | bytes 131072 | tf_op jit(solution)/shard_map/all_to_all | solution.py:61
  323.0 12.9 %all_to_all.207 = f32[64,1,128]{2,1,0:T(1,128)S(1)} all-to-all(f32[64,1,128]{2,1,0:T(1,128)S(1)} %broadcast_in_dim.87), channel_id=1, replica_groups=mesh['gx'=4,'gy_0'=4,'gy_1'=4,'gy_2'=2] {'gx','gy_0','gy_1'}, dimensions={0} | all-to-all | bytes 65536 | tf_op jit(solution)/shard_map/all_to_all | solution.py:61
  349.1 20.8 %fusion.14 = f32[2048,128]{0,1:T(8,128)} fusion(f32[1,2048,2048]{2,1,0:T(8,128)} %param.7, s32[]{:T(128)S(6)} %select_n.9, f32[768,128]{0,1:T(8,128)S(1)} %collective-permute-done.8, f32[1024,128]{0,1:T(8,128)S(1)} %multiply_add_fusion.2, f32[768,128]{0,1:T(8,128)S(1)} %collective-permute-done.9), kind=kOutput, calls=%fused_computation.10 | convolution fusion | flops 6442975232 | bytes 19136516 | tf_op jit(solution)/shard_map/dot_general | solution.py:105
  371.2 6.3 %dynamic_update_slice.14 = f32[3072,128]{0,1:T(8,128)} dynamic-update-slice(f32[3072,128]{0,1:T(8,128)} %broadcast.113.clone.2, f32[2048,128]{0,1:T(8,128)} %fusion.14, s32[]{:T(128)S(6)} %select_n.18, s32[]{:T(128)} %constant.55.clone.1) | dynamic-update-slice | bytes 2097156 | tf_op jit(solution)/shard_map/dynamic_update_slice | solution.py:109
  396.6 24.9 %all_to_all.208 = f32[64,1,128]{2,1,0:T(1,128)S(1)} all-to-all(f32[64,1,128]{2,1,0:T(1,128)S(1)} %broadcast_in_dim.89), channel_id=1, replica_groups=mesh['gx'=4,'gy_0'=4,'gy_1'=4,'gy_2'=2] {'gx','gy_0','gy_1'}, dimensions={0} | all-to-all | bytes 65536 | tf_op jit(solution)/shard_map/all_to_all | solution.py:61
  429.3 12.9 %all_to_all.209 = f32[64,1,128]{2,1,0:T(1,128)S(1)} all-to-all(f32[64,1,128]{2,1,0:T(1,128)S(1)} %bitcast.194), channel_id=1, replica_groups=mesh['gx'=4,'gy_0'=4,'gy_1'=4,'gy_2'=2] {'gx','gy_0','gy_1'}, dimensions={0} | all-to-all | bytes 65536 | tf_op jit(solution)/shard_map/all_to_all | solution.py:49
  442.3 12.9 %all_to_all.210 = f32[64,1,128]{2,1,0:T(1,128)S(1)} all-to-all(f32[64,1,128]{2,1,0:T(1,128)S(1)} %broadcast_in_dim.90), channel_id=1, replica_groups=mesh['gx'=4,'gy_0'=4,'gy_1'=4,'gy_2'=2] {'gx','gy_0','gy_1'}, dimensions={0} | all-to-all | bytes 65536 | tf_op jit(solution)/shard_map/all_to_all | solution.py:61
  455.2 6.6 %all_to_all.198 = f32[2,64,1,128]{3,1,2,0:T(8,128)S(1)} all-to-all(f32[2,64,1,128]{3,1,2,0:T(8,128)S(1)} %broadcast_in_dim.91), channel_id=1, replica_groups=mesh['gx'=4,'gy_0'=4,'gy_1'=4,'gy_2'=2] {'gy_2'}, dimensions={0} | all-to-all | bytes 131072 | tf_op jit(solution)/shard_map/all_to_all | solution.py:61
  467.6 12.9 %all_to_all.211 = f32[64,1,128]{2,1,0:T(1,128)S(1)} all-to-all(f32[64,1,128]{2,1,0:T(1,128)S(1)} %broadcast_in_dim.93), channel_id=1, replica_groups=mesh['gx'=4,'gy_0'=4,'gy_1'=4,'gy_2'=2] {'gx','gy_0','gy_1'}, dimensions={0} | all-to-all | bytes 65536 | tf_op jit(solution)/shard_map/all_to_all | solution.py:61
  494.7 20.8 %fusion.17 = f32[2048,128]{0,1:T(8,128)} fusion(f32[1,2048,2048]{2,1,0:T(8,128)} %param.7, s32[]{:T(128)S(6)} %select_n.9, f32[768,128]{0,1:T(8,128)S(1)} %collective-permute-done.12, f32[1024,128]{0,1:T(8,128)S(1)} %multiply_add_fusion.1, f32[768,128]{0,1:T(8,128)S(1)} %collective-permute-done.13), kind=kOutput, calls=%fused_computation.11 | convolution fusion | flops 6442975232 | bytes 19136516 | tf_op jit(solution)/shard_map/dot_general | solution.py:105
  516.9 6.3 %dynamic_update_slice.15 = f32[3072,128]{0,1:T(8,128)} dynamic-update-slice(f32[3072,128]{0,1:T(8,128)} %broadcast.113, f32[2048,128]{0,1:T(8,128)} %fusion.17, s32[]{:T(128)S(6)} %select_n.18, s32[]{:T(128)} %constant.55.clone.1) | dynamic-update-slice | bytes 2097156 | tf_op jit(solution)/shard_map/dynamic_update_slice | solution.py:109
  541.7 24.9 %all_to_all.212 = f32[64,1,128]{2,1,0:T(1,128)S(1)} all-to-all(f32[64,1,128]{2,1,0:T(1,128)S(1)} %broadcast_in_dim.95), channel_id=1, replica_groups=mesh['gx'=4,'gy_0'=4,'gy_1'=4,'gy_2'=2] {'gx','gy_0','gy_1'}, dimensions={0} | all-to-all | bytes 65536 | tf_op jit(solution)/shard_map/all_to_all | solution.py:61
  574.2 12.9 %all_to_all.213 = f32[64,1,128]{2,1,0:T(1,128)S(1)} all-to-all(f32[64,1,128]{2,1,0:T(1,128)S(1)} %bitcast.196), channel_id=1, replica_groups=mesh['gx'=4,'gy_0'=4,'gy_1'=4,'gy_2'=2] {'gx','gy_0','gy_1'}, dimensions={0} | all-to-all | bytes 65536 | tf_op jit(solution)/shard_map/all_to_all | solution.py:49
  593.7 7.1 %all-to-all-done.30 = f32[64,1,128]{2,1,0:T(1,128)S(1)} async-done(((f32[64,1,128]{2,1,0:T(1,128)}), f32[64,1,128]{2,1,0:T(1,128)S(1)}, u32[]{:S(2)}, u32[]{:S(2)}) %all-to-all-start.30) | async-done | bytes 32800 | tf_op jit(solution)/shard_map/all_to_all | solution.py:61
  600.9 6.6 %all_to_all.202 = f32[2,64,1,128]{3,1,2,0:T(8,128)S(1)} all-to-all(f32[2,64,1,128]{3,1,2,0:T(8,128)S(1)} %broadcast_in_dim.97), channel_id=1, replica_groups=mesh['gx'=4,'gy_0'=4,'gy_1'=4,'gy_2'=2] {'gy_2'}, dimensions={0} | all-to-all | bytes 131072 | tf_op jit(solution)/shard_map/all_to_all | solution.py:61
  (177 shorter events, 193.2 us)
Async XLA Ops:
  0.6 1.0 copy-start
  0.6 70.6 %copy-start.11 = (f32[128,128]{1,0:T(8,128)S(1)}, f32[128,128]{1,0:T(8,128)}, u32[]{:S(2)}) copy-start(f32[128,128]{1,0:T(8,128)} %param.11) | copy-start | bytes 196612
  3.3 5.7 all-to-all-start
  72.5 7.1 %collective-permute-start = (f32[768,128]{0,1:T(8,128)S(1)}, f32[768,128]{0,1:T(8,128)S(1)}, u32[]{:S(2)}, u32[]{:S(2)}) collective-permute-start(f32[768,128]{0,1:T(8,128)S(1)} %get-tuple-element.30), channel_id=1, source_target_pairs={{0,1},{1,2},{2,3},{3,4},{4,5},{5,6},{6,7},{7,8},{8,9},{9,10},{10,1... | collective-permute-start | bytes 1179656 | tf_op jit(solution)/shard_map/ppermute | solution.py:22
  74.9 9.1 %collective-permute-start.1 = (f32[768,128]{0,1:T(8,128)S(1)}, f32[768,128]{0,1:T(8,128)S(1)}, u32[]{:S(2)}, u32[]{:S(2)}) collective-permute-start(f32[768,128]{0,1:T(8,128)S(1)} %get-tuple-element.29), channel_id=1, source_target_pairs={{1,0},{2,1},{3,2},{4,3},{5,4},{6,5},{7,6},{8,7},{9,8},{10,9},{11,1... | collective-permute-start | bytes 1179656 | tf_op jit(solution)/shard_map/ppermute | solution.py:23
  110.4 7.5 %copy-start.4 = (f32[3072,128]{0,1:T(8,128)}, f32[3072,128]{0,1:T(8,128)S(1)}, u32[]{:S(2)}) copy-start(f32[3072,128]{0,1:T(8,128)S(1)} %dynamic_update_slice.12) | copy-start | bytes 4718596
  111.5 8.3 %collective-permute-start.2 = (f32[1024,128]{0,1:T(8,128)}, f32[1024,128]{0,1:T(8,128)}, u32[]{:S(2)}, u32[]{:S(2)}) collective-permute-start(f32[1024,128]{0,1:T(8,128)} %get-tuple-element.21), channel_id=1, source_target_pairs={{0,1},{1,2},{2,3},{3,4},{4,5},{5,6},{6,7},{7,8},{8,9},{9,10},{10,1... | collective-permute-start | bytes 1572872 | tf_op jit(solution)/shard_map/ppermute | solution.py:22
  113.4 10.8 %collective-permute-start.3 = (f32[1024,128]{0,1:T(8,128)}, f32[1024,128]{0,1:T(8,128)}, u32[]{:S(2)}, u32[]{:S(2)}) collective-permute-start(f32[1024,128]{0,1:T(8,128)} %get-tuple-element.22), channel_id=1, source_target_pairs={{1,0},{2,1},{3,2},{4,3},{5,4},{6,5},{7,6},{8,7},{9,8},{10,9},{11,1... | collective-permute-start | bytes 1572872 | tf_op jit(solution)/shard_map/ppermute | solution.py:23
  125.8 50.4 %copy-start.1 = (f32[1024,128]{0,1:T(8,128)}, f32[1024,128]{0,1:T(8,128)S(1)}, u32[]{:S(2)}) copy-start(f32[1024,128]{0,1:T(8,128)S(1)} %fusion.39) | copy-start | bytes 1572868
  176.2 7.1 %collective-permute-start.4 = (f32[768,128]{0,1:T(8,128)S(1)}, f32[768,128]{0,1:T(8,128)S(1)}, u32[]{:S(2)}, u32[]{:S(2)}) collective-permute-start(f32[768,128]{0,1:T(8,128)S(1)} %get-tuple-element.28), channel_id=1, source_target_pairs={{0,1},{1,2},{2,3},{3,4},{4,5},{5,6},{6,7},{7,8},{8,9},{9,10},{10,1... | collective-permute-start | bytes 1179656 | tf_op jit(solution)/shard_map/ppermute | solution.py:22
  178.7 9.1 %collective-permute-start.5 = (f32[768,128]{0,1:T(8,128)S(1)}, f32[768,128]{0,1:T(8,128)S(1)}, u32[]{:S(2)}, u32[]{:S(2)}) collective-permute-start(f32[768,128]{0,1:T(8,128)S(1)} %get-tuple-element.27), channel_id=1, source_target_pairs={{1,0},{2,1},{3,2},{4,3},{5,4},{6,5},{7,6},{8,7},{9,8},{10,9},{11,1... | collective-permute-start | bytes 1179656 | tf_op jit(solution)/shard_map/ppermute | solution.py:23
  214.2 8.0 %collective-permute-start.6 = (f32[1024,128]{0,1:T(8,128)S(1)}, f32[1024,128]{0,1:T(8,128)S(1)}, u32[]{:S(2)}, u32[]{:S(2)}) collective-permute-start(f32[1024,128]{0,1:T(8,128)S(1)} %get-tuple-element.19), channel_id=1, source_target_pairs={{0,1},{1,2},{2,3},{3,4},{4,5},{5,6},{6,7},{7,8},{8,9},{9,10},{10,1... | collective-permute-start | bytes 1572872 | tf_op jit(solution)/shard_map/ppermute | solution.py:22
  216.1 10.5 %collective-permute-start.7 = (f32[1024,128]{0,1:T(8,128)S(1)}, f32[1024,128]{0,1:T(8,128)S(1)}, u32[]{:S(2)}, u32[]{:S(2)}) collective-permute-start(f32[1024,128]{0,1:T(8,128)S(1)} %get-tuple-element.20), channel_id=1, source_target_pairs={{1,0},{2,1},{3,2},{4,3},{5,4},{6,5},{7,6},{8,7},{9,8},{10,9},{11,1... | collective-permute-start | bytes 1572872 | tf_op jit(solution)/shard_map/ppermute | solution.py:23
  222.2 4.4 copy-start.9
  231.3 4.5 all-to-all-start.10
  236.4 25.2 %all-to-all-start.9 = ((f32[64,1,128]{2,1,0:T(1,128)}), f32[64,1,128]{2,1,0:T(1,128)S(1)}, u32[]{:S(2)}, u32[]{:S(2)}) async-start(f32[64,1,128]{2,1,0:T(1,128)} %broadcast_in_dim.81), calls=%async_computation.9 | async-start | bytes 65536 | tf_op jit(solution)/shard_map/all_to_all | solution.py:61
  262.2 13.0 %all-to-all-start.11 = ((f32[64,1,128]{2,1,0:T(1,128)}), f32[64,1,128]{2,1,0:T(1,128)S(1)}, u32[]{:S(2)}, u32[]{:S(2)}) async-start(f32[64,1,128]{2,1,0:T(1,128)} %broadcast_in_dim.83), calls=%async_computation.11 | async-start | bytes 65536 | tf_op jit(solution)/shard_map/all_to_all | solution.py:61
  276.8 0.8 copy-start.2
  278.6 39.9 %copy-start.3 = (f32[1024,128]{0,1:T(8,128)S(1)}, f32[1024,128]{0,1:T(8,128)}, u32[]{:S(2)}) copy-start(f32[1024,128]{0,1:T(8,128)} %copy-done.2) | copy-start | bytes 1572868
  336.1 8.6 %collective-permute-start.8 = (f32[768,128]{0,1:T(8,128)S(1)}, f32[768,128]{0,1:T(8,128)S(1)}, u32[]{:S(2)}, u32[]{:S(2)}) collective-permute-start(f32[768,128]{0,1:T(8,128)S(1)} %get-tuple-element.26), channel_id=1, source_target_pairs={{0,1},{1,2},{2,3},{3,4},{4,5},{5,6},{6,7},{7,8},{8,9},{9,10},{10,1... | collective-permute-start | bytes 1179656 | tf_op jit(solution)/shard_map/ppermute | solution.py:22
  340.0 9.1 %collective-permute-start.9 = (f32[768,128]{0,1:T(8,128)S(1)}, f32[768,128]{0,1:T(8,128)S(1)}, u32[]{:S(2)}, u32[]{:S(2)}) collective-permute-start(f32[768,128]{0,1:T(8,128)S(1)} %get-tuple-element.25), channel_id=1, source_target_pairs={{1,0},{2,1},{3,2},{4,3},{5,4},{6,5},{7,6},{8,7},{9,8},{10,9},{11,1... | collective-permute-start | bytes 1179656 | tf_op jit(solution)/shard_map/ppermute | solution.py:23
  378.8 8.0 %collective-permute-start.10 = (f32[1024,128]{0,1:T(8,128)S(1)}, f32[1024,128]{0,1:T(8,128)S(1)}, u32[]{:S(2)}, u32[]{:S(2)}) collective-permute-start(f32[1024,128]{0,1:T(8,128)S(1)} %get-tuple-element.17), channel_id=1, source_target_pairs={{0,1},{1,2},{2,3},{3,4},{4,5},{5,6},{6,7},{7,8},{8,9},{9,10},{10,1... | collective-permute-start | bytes 1572872 | tf_op jit(solution)/shard_map/ppermute | solution.py:22
  380.7 10.5 %collective-permute-start.11 = (f32[1024,128]{0,1:T(8,128)S(1)}, f32[1024,128]{0,1:T(8,128)S(1)}, u32[]{:S(2)}, u32[]{:S(2)}) collective-permute-start(f32[1024,128]{0,1:T(8,128)S(1)} %get-tuple-element.18), channel_id=1, source_target_pairs={{1,0},{2,1},{3,2},{4,3},{5,4},{6,5},{7,6},{8,7},{9,8},{10,9},{11,1... | collective-permute-start | bytes 1572872 | tf_op jit(solution)/shard_map/ppermute | solution.py:23
  386.8 34.7 %copy-start.6 = (f32[1024,128]{0,1:T(8,128)}, f32[1024,128]{0,1:T(8,128)S(1)}, u32[]{:S(2)}) copy-start(f32[1024,128]{0,1:T(8,128)S(1)} %collective-permute-done.10) | copy-start | bytes 1572868
  391.2 0.8 copy-start.8
  481.8 8.6 %collective-permute-start.12 = (f32[768,128]{0,1:T(8,128)S(1)}, f32[768,128]{0,1:T(8,128)S(1)}, u32[]{:S(2)}, u32[]{:S(2)}) collective-permute-start(f32[768,128]{0,1:T(8,128)S(1)} %get-tuple-element.24), channel_id=1, source_target_pairs={{0,1},{1,2},{2,3},{3,4},{4,5},{5,6},{6,7},{7,8},{8,9},{9,10},{10,1... | collective-permute-start | bytes 1179656 | tf_op jit(solution)/shard_map/ppermute | solution.py:22
  485.6 9.1 %collective-permute-start.13 = (f32[768,128]{0,1:T(8,128)S(1)}, f32[768,128]{0,1:T(8,128)S(1)}, u32[]{:S(2)}, u32[]{:S(2)}) collective-permute-start(f32[768,128]{0,1:T(8,128)S(1)} %get-tuple-element.23), channel_id=1, source_target_pairs={{1,0},{2,1},{3,2},{4,3},{5,4},{6,5},{7,6},{8,7},{9,8},{10,9},{11,1... | collective-permute-start | bytes 1179656 | tf_op jit(solution)/shard_map/ppermute | solution.py:23
  524.4 8.0 %collective-permute-start.14 = (f32[1024,128]{0,1:T(8,128)S(1)}, f32[1024,128]{0,1:T(8,128)S(1)}, u32[]{:S(2)}, u32[]{:S(2)}) collective-permute-start(f32[1024,128]{0,1:T(8,128)S(1)} %get-tuple-element.15), channel_id=1, source_target_pairs={{0,1},{1,2},{2,3},{3,4},{4,5},{5,6},{6,7},{7,8},{8,9},{9,10},{10,1... | collective-permute-start | bytes 1572872 | tf_op jit(solution)/shard_map/ppermute | solution.py:22
  526.4 10.5 %collective-permute-start.15 = (f32[1024,128]{0,1:T(8,128)S(1)}, f32[1024,128]{0,1:T(8,128)S(1)}, u32[]{:S(2)}, u32[]{:S(2)}) collective-permute-start(f32[1024,128]{0,1:T(8,128)S(1)} %get-tuple-element.16), channel_id=1, source_target_pairs={{1,0},{2,1},{3,2},{4,3},{5,4},{6,5},{7,6},{8,7},{9,8},{10,9},{11,1... | collective-permute-start | bytes 1572872 | tf_op jit(solution)/shard_map/ppermute | solution.py:23
  532.5 4.4 copy-start.5
  536.9 1.4 copy-start.7
  587.8 13.0 %all-to-all-start.30 = ((f32[64,1,128]{2,1,0:T(1,128)}), f32[64,1,128]{2,1,0:T(1,128)S(1)}, u32[]{:S(2)}, u32[]{:S(2)}) async-start(f32[64,1,128]{2,1,0:T(1,128)} %broadcast_in_dim.96), calls=%async_computation.30 | async-start | bytes 65536 | tf_op jit(solution)/shard_map/all_to_all | solution.py:61
  (1 other events, 0.8 us)
where the time goes:
time: 619 us; the launch traced here: 609 us
  blocking collectives  282 us (46%)
  matrix products  96.3 us (16%)
  waiting for transfers between devices  83.5 us (13%)
  starting transfers between devices  73.7 us (12%)
  local copies, waits for them, and re-layouts  39.3 us (6%)
  other arithmetic  32.4 us (5%)
    all_to_all x18, blocking collectives, sent_to_all(): return lax.all_to_all(copies, axis, split_axis=0, concat_axis=0, tiled=True)  178 us
    dot_general x4, matrix products, apply_local(): jnp.dot(schur_block, window, precision=HIGHEST, preferred_element_type=jn...  83.4 us
    all_to_all x5, blocking collectives, sum_in_two_steps(): return jnp.sum(lax.all_to_all(own, far, 0, 0, tiled=True), axis=0)  83.2 us
    ppermute x8, waiting for transfers between devices, extended_2(): lax.ppermute(initial, axis, [(b, a) for a, b in up])  35.2 us
    all_to_all x4, starting transfers between devices, sent_to_all(): return lax.all_to_all(copies, axis, split_axis=0, concat_axis=0, tiled=True)  29.7 us
    all_to_all x4, waiting for transfers between devices, sent_to_all(): return lax.all_to_all(copies, axis, split_axis=0, concat_axis=0, tiled=True)  24.7 us
    dynamic_update_slice x4, local copies, waits for them, and re-layouts, apply_local(): lax.dynamic_update_slice_in_dim(spread, product_block, start_row, 0)  23.2 us
    ppermute x8, waiting for transfers between devices, extended_2(): lax.ppermute(last, axis, up)  22.5 us
  transfers between devices with their start and end apart: 21, of which 21 were waited for; matrix products, arithmetic and copies ran while one was open for 0% of the time, Pallas kernels for 0%

commit v1 on v0

v1 whole, which is shorter than its diff:
```python
import jax
import jax.numpy as jnp
from jax import lax
from jax.experimental import pallas as pl
from jax.experimental.pallas import tpu as pltpu
from jax.sharding import Mesh
from jax.sharding import PartitionSpec as P

GX_GY = ("gx", "gy_0", "gy_1", "gy_2")
HIGHEST = lax.Precision.HIGHEST
F32 = jnp.float32
BF16 = jnp.bfloat16

SLAB = 1024
WINDOW = 2048
REACH = 768
SKIP = SLAB - REACH
EXT = SLAB + 2 * REACH
R = 128
DEVICES = 128
TILE = 256


def full_dot(a, b):
    return jnp.dot(a, b, precision=HIGHEST, preferred_element_type=F32)


def contract_rows(a, b):
    return lax.dot_general(
        a, b, (((0,), (0,)), ((), ())), precision=HIGHEST, preferred_element_type=F32
    )


def split_bf16(x):
    high = x.astype(BF16)
    return high, (x - high.astype(F32)).astype(BF16)


def operator_kernel(start_ref, ext_ref, left_ref, schur_ref, *refs, spread):
    if spread:
        low_ref, own_ref, up_ref, energy_ref, cross_ref, halves, image = refs
    else:
        energy_ref, halves = refs
    step = pl.program_id(0)
    start = start_ref[0] - SKIP

    @pl.when(step == 0)
    def _():
        high, low = split_bf16(ext_ref[pl.ds(start, WINDOW), :])
        halves[:, :R] = high
        halves[:, R:] = low
        energy_ref[...] = jnp.zeros_like(energy_ref)
        if spread:
            cross_ref[...] = jnp.zeros_like(cross_ref)
            image[: EXT - WINDOW, :] = jnp.zeros((EXT - WINDOW, R), F32)
            image[WINDOW:, :] = jnp.zeros((EXT - WINDOW, R), F32)

    high, low = split_bf16(schur_ref[...])
    both = jnp.dot(high, halves[...], preferred_element_type=F32)
    rest = jnp.dot(low, halves[:, :R], preferred_element_type=F32)
    product = both[:, :R] + both[:, R:] + rest
    rows = pl.ds(start + step * TILE, TILE)
    energy_ref[...] += jnp.sum((ext_ref[rows, :] * product).reshape(TILE // 8, 8, R), axis=0)
    if spread:
        cross_ref[...] += contract_rows(left_ref[rows, :], product)
        image[rows, :] = product

        @pl.when(step == pl.num_programs(0) - 1)
        def _():
            low_ref[...] = image[:REACH, :]
            own_ref[...] = image[REACH : REACH + SLAB, :]
            up_ref[...] = image[REACH + SLAB :, :]


def apply_operator(start, ext, left, schur, spread=True):
    whole = lambda rows: pl.BlockSpec((rows, R), lambda i: (0, 0))
    shapes = [jax.ShapeDtypeStruct((8, R), F32)]
    out_specs = [whole(8)]
    scratch = [pltpu.VMEM((WINDOW, 2 * R), BF16)]
    if spread:
        rows = (REACH, SLAB, REACH)
        shapes = [jax.ShapeDtypeStruct((n, R), F32) for n in rows] + shapes
        shapes += [jax.ShapeDtypeStruct((R, R), F32)]
        out_specs = [whole(n) for n in rows] + out_specs + [whole(R)]
        scratch += [pltpu.VMEM((EXT, R), F32)]
    out = pl.pallas_call(
        lambda *refs: operator_kernel(*refs, spread=spread),
        grid=(WINDOW // TILE,),
        in_specs=[
            pl.BlockSpec(memory_space=pltpu.SMEM),
            whole(EXT),
            whole(EXT),
            pl.BlockSpec((None, TILE, WINDOW), lambda i: (0, i, 0)),
        ],
        out_specs=out_specs,
        out_shape=shapes,
        scratch_shapes=scratch,
        compiler_params=pltpu.CompilerParams(
            dimension_semantics=("arbitrary",), vmem_limit_bytes=32 << 20
        ),
        cost_estimate=pl.CostEstimate(
            flops=6 * WINDOW * WINDOW * R, bytes_accessed=4 * WINDOW * WINDOW, transcendentals=0
        ),
        name="operator",
    )(start, ext, left, schur)
    if spread:
        low, own, up, energy, cross = out
        return (low, own, up), jnp.sum(energy, axis=0), cross
    return jnp.sum(out[0], axis=0)


def inverse_kernel(gram_ref, inverse_ref):
    gram = gram_ref[...]
    row = lax.broadcasted_iota(jnp.int32, (R, R), 0)
    column = lax.broadcasted_iota(jnp.int32, (R, R), 1)
    identity = jnp.where(row == column, 1.0, 0.0).astype(F32)
    diagonal = gram * identity
    across = lax.rsqrt(jnp.sum(diagonal, axis=0, keepdims=True))
    along = lax.rsqrt(jnp.sum(diagonal, axis=1, keepdims=True))
    scaled = gram * across * along
    bound = jnp.max(jnp.sum(jnp.abs(scaled), axis=0, keepdims=True), axis=1, keepdims=True)
    inverse_ref[...] = identity / bound

    def refine():
        current = inverse_ref[...]
        rest = identity - full_dot(scaled, current)
        inverse_ref[...] = current + full_dot(current, rest)
        return jnp.max(jnp.abs(rest))

    def body(carry):
        return carry[0] + 1, refine()

    lax.while_loop(lambda c: (c[0] < 60) & (c[1] > 1e-3), body, (jnp.int32(0), jnp.float32(1.0)))
    refine()
    inverse_ref[...] = inverse_ref[...] * across * along


def inverse_of(gram):
    return pl.pallas_call(
        inverse_kernel,
        out_shape=jax.ShapeDtypeStruct((R, R), F32),
        in_specs=[pl.BlockSpec(memory_space=pltpu.VMEM)],
        out_specs=pl.BlockSpec(memory_space=pltpu.VMEM),
        compiler_params=pltpu.CompilerParams(vmem_limit_bytes=4 << 20),
        cost_estimate=pl.CostEstimate(flops=400 * R * R * R, bytes_accessed=8 * R * R, transcendentals=0),
        name="inverse",
    )(gram)


UP = [(i, i + 1) for i in range(DEVICES - 1)]
DOWN = [(i + 1, i) for i in range(DEVICES - 1)]


def extended(own):
    low = lax.ppermute(own[SKIP:], GX_GY, UP)
    high = lax.ppermute(own[:REACH], GX_GY, DOWN)
    return jnp.concatenate([low, own, high], axis=0)


def gathered_sum(parts):
    to_low, own, to_high = parts
    from_high = lax.ppermute(to_low, GX_GY, DOWN)
    from_low = lax.ppermute(to_high, GX_GY, UP)
    return own + jnp.pad(from_low, ((0, SKIP), (0, 0))) + jnp.pad(from_high, ((SKIP, 0), (0, 0)))


def exchange(*pieces):
    pieces = [jnp.broadcast_to(p, (DEVICES, p.shape[-1])) for p in pieces]
    joined = jnp.concatenate(pieces, axis=1)
    width = joined.shape[1]
    arrived = lax.all_to_all(joined.reshape(DEVICES, 1, width), GX_GY, 0, 0, tiled=True)
    return arrived.reshape(DEVICES, width)


def columns(array, *indices):
    return [array[:, R * i : R * (i + 1)] for i in indices]


def sums(array, *indices):
    return [jnp.sum(array[:, R * i : R * (i + 1)], axis=0, keepdims=True) for i in indices]


def column_sum(a, b):
    return jnp.sum(a * b, axis=0, keepdims=True)


def local(schur, offsets, right_side, basis, load):
    start = offsets

    basis_ext = extended(basis)
    parts, _, stiff = apply_operator(start, basis_ext, basis_ext, schur)
    arrived = exchange(contract_rows(basis, basis), contract_rows(basis, right_side), stiff)
    mine = sums(arrived, 0, 1, 2)
    image = gathered_sum(parts)
    image_ext = extended(image)
    right_ext = extended(right_side)
    arrived = exchange(*mine, contract_rows(image, image))
    gram, coarse, stiff = columns(arrived, 0, 1, 2)
    (mine_square,) = sums(arrived, 3)
    inverse = inverse_of(gram)
    first = full_dot(inverse, load)
    amp = full_dot(inverse, coarse - full_dot(stiff, first))
    r0_ext = right_ext - full_dot(image_ext, first) - full_dot(basis_ext, amp)
    r0 = r0_ext[REACH : REACH + SLAB]

    parts, form, cross = apply_operator(start, r0_ext, image_ext, schur)
    arrived = exchange(column_sum(r0, r0), form[None], mine_square, contract_rows(image, r0), cross)
    w0 = gathered_sum(parts)
    w0_ext = extended(w0)
    energy0, form0 = sums(arrived, 0, 1)
    (square,) = columns(arrived, 2)
    mine = sums(arrived, 3, 4)
    step0 = energy0 / form0
    r1_ext = r0_ext - step0 * w0_ext
    r1 = r1_ext[REACH : REACH + SLAB]

    parts, form, cross = apply_operator(start, r1_ext, image_ext, schur)
    arrived = exchange(column_sum(r1, r1), form[None], *mine, cross)
    w1 = gathered_sum(parts)
    w1_ext = extended(w1)
    norm1, form1 = sums(arrived, 0, 1)
    e0, f0 = columns(arrived, 2, 3)
    mine = sums(arrived, 4)
    c1 = -step0 * e0
    a1 = full_dot(inverse, c1)
    e1 = e0 - step0 * f0
    energy1 = norm1 - column_sum(c1, a1)
    stiff_a1 = full_dot(stiff, a1)
    ratio0 = energy1 / energy0
    curve1 = form1 - 2.0 * column_sum(a1, e1) + column_sum(a1, stiff_a1) - ratio0 * energy1 / step0
    step1 = energy1 / curve1
    d1_image = w1_ext - full_dot(image_ext, a1) + ratio0 * w0_ext
    r2_ext = r1_ext - step1 * d1_image
    r2 = r2_ext[REACH : REACH + SLAB]
    d1 = r1 - full_dot(basis, a1) + ratio0 * r0
    d1_coarse = e1 - stiff_a1 + ratio0 * e0
    c2 = c1 - step1 * d1_coarse
    a2 = full_dot(inverse, c2)
    square_a1 = full_dot(square, a1)

    form = apply_operator(start, r2_ext, image_ext, schur, spread=False)
    arrived = exchange(column_sum(r2, r2), form[None], *mine)
    norm2, form2 = sums(arrived, 0, 1)
    (f1,) = columns(arrived, 2)
    e2 = e1 - step1 * (f1 - square_a1 + ratio0 * f0)
    energy2 = norm2 - column_sum(c2, a2)
    stiff_a2 = full_dot(stiff, a2)
    ratio1 = energy2 / energy1
    curve2 = form2 - 2.0 * column_sum(a2, e2) + column_sum(a2, stiff_a2) - ratio1 * energy2 / step1
    step2 = energy2 / curve2
    d2 = r2 - full_dot(basis, a2) + ratio1 * d1
    c3 = c2 - step2 * (e2 - stiff_a2 + ratio1 * d1_coarse)
    multipliers = full_dot(basis, first) + step0 * r0 + step1 * d1 + step2 * d2
    return multipliers, amp + full_dot(inverse, c3)


def solution(mesh):
    split = Mesh(mesh.devices.reshape(mesh.shape["gx"], 4, 4, 2), GX_GY)
    in_specs = (P(GX_GY, None, None), P(GX_GY), P(GX_GY, None), P(GX_GY, None), P())
    out_specs = (P(GX_GY, None), P())
    return jax.shard_map(local, mesh=split, in_specs=in_specs, out_specs=out_specs, check_vma=False)
```

time: 619 us -> 268 us (0.43); the launches traced: 609 us -> 266 us
  blocking collectives: 282 us -> 0 us
  matrix products: 96.3 us -> 23.5 us
  waiting for transfers between devices: 83.5 us -> 36.9 us
  starting transfers between devices: 73.7 us -> 116 us
  Pallas kernels: 0 us -> 34 us
  other arithmetic: 32.4 us -> 8.51 us
    all_to_all x27 -> x0, blocking collectives: 282 us -> none  [the longest x18 178 us: sent_to_all(): return lax.all_to_all(copies, axis, split_axis=0, concat_axis=0, tiled=True)]
    dot_general x13 -> x19, matrix products: 93.2 us -> 23.5 us  [the longest x15 17.8 us: full_dot(): return jnp.dot(a, b, precision=HIGHEST, preferred_element_type=F32)]
    ppermute x16, waiting for transfers between devices: 57.6 us -> 16.8 us  [the longest x5 11.1 us: extended(): high = lax.ppermute(own[:REACH], GX_GY, DOWN)]
    all_to_all x5, starting transfers between devices: 34.4 us -> 72.5 us  [exchange(): lax.all_to_all(joined.reshape(DEVICES, 1, width), GX_GY, 0, 0, tiled=True)]
    pallas_call x0 -> x5, Pallas kernels: none -> 34 us  [the longest x4 31.5 us: apply_operator(): pl.pallas_call(lambda *refs: operator_kernel(*refs, spread=spread), grid=...]
    unnamed x26 -> x102, local copies, waits for them, and re-layouts: 5.48 us -> 32.5 us
    dynamic_update_slice x4 -> x0, local copies, waits for them, and re-layouts: 23.2 us -> none  [apply_local(): lax.dynamic_update_slice_in_dim(spread, product_block, start_row, 0)]
    another operation x5 -> x0, other arithmetic: 22.9 us -> none  [the longest x3 12.4 us: local(): gram_factor = jnp.linalg.cholesky(gram_matrix)]
  transfers between devices with their start and end apart: 21 -> 21, of which waited for: 21 -> 10; matrix products, arithmetic and copies ran while one was open for 0% -> 9% of each run, Pallas kernels for 0% -> 1%
where the time goes in v1:
time: 268 us; the launch traced here: 266 us
  starting transfers between devices  116 us (43%)
  local copies, waits for them, and re-layouts  44.5 us (17%)
  waiting for transfers between devices  36.9 us (14%)
  Pallas kernels  34 us (13%)
  matrix products  23.5 us (9%)
  other arithmetic  8.51 us (3%)
    all_to_all x5, starting transfers between devices, exchange(): lax.all_to_all(joined.reshape(DEVICES, 1, width), GX_GY, 0, 0, tiled=True)  72.5 us
    unnamed x102, local copies, waits for them, and re-layouts  32.5 us
    pallas_call x4, Pallas kernels, apply_operator(): pl.pallas_call(lambda *refs: operator_kernel(*refs, spread=spread), grid=...  31.5 us
    all_to_all x5, waiting for transfers between devices, exchange(): lax.all_to_all(joined.reshape(DEVICES, 1, width), GX_GY, 0, 0, tiled=True)  20.1 us
    dot_general x15, matrix products, full_dot(): return jnp.dot(a, b, precision=HIGHEST, preferred_element_type=F32)  17.8 us
    ppermute x5, starting transfers between devices, extended(): low = lax.ppermute(own[SKIP:], GX_GY, UP)  16.1 us
    ppermute x5, starting transfers between devices, extended(): high = lax.ppermute(own[:REACH], GX_GY, DOWN)  11.9 us
    ppermute x5, waiting for transfers between devices, extended(): high = lax.ppermute(own[:REACH], GX_GY, DOWN)  11.1 us
  transfers between devices with their start and end apart: 21, of which 10 were waited for; matrix products, arithmetic and copies ran while one was open for 9% of the time, Pallas kernels for 1%

profile of v1, /device:TPU:1, one launch (start us, length us, event | category | flops | bytes accessed | tf_op | source)
XLA Modules:
  0.0 266.1 jit_solution(8915431327511486945)
XLA Ops:
  1.9 3.3 %collective-permute-start.1 = (f32[768,128]{1,0:T(8,128)S(1)}, f32[768,128]{1,0:T(8,128)S(1)}, u32[]{:S(2)}, u32[]{:S(2)}) collective-permute-start(f32[768,128]{1,0:T(8,128)S(1)} %get-tuple-element.65), channel_id=1, source_target_pairs={{1,0},{2,1},{3,2},{4,3},{5,4},{6,5},{7,6},{8,7},{9,8},{10,9},{11,1... | collective-permute-start | bytes 1179656 | tf_op jit(solution)/shard_map/ppermute | solution.py:156
  5.2 3.2 %collective-permute-start = (f32[768,128]{1,0:T(8,128)S(1)}, f32[768,128]{1,0:T(8,128)S(1)}, u32[]{:S(2)}, u32[]{:S(2)}) collective-permute-start(f32[768,128]{1,0:T(8,128)S(1)} %get-tuple-element.66), channel_id=1, source_target_pairs={{0,1},{1,2},{2,3},{3,4},{4,5},{5,6},{6,7},{7,8},{8,9},{9,10},{10,1... | collective-permute-start | bytes 1179656 | tf_op jit(solution)/shard_map/ppermute | solution.py:155
  13.3 5.8 %copy-done.1 = f32[1,2048,2048]{2,1,0:T(8,128)S(1)} copy-done((f32[1,2048,2048]{2,1,0:T(8,128)S(1)}, f32[1,2048,2048]{2,1,0:T(8,128)}, u32[]{:S(2)}) %copy-start.1) | copy-done | bytes 16777240
  19.0 8.7 %operator.4 = (f32[768,128]{1,0:T(8,128)S(1)}, f32[1024,128]{1,0:T(8,128)S(1)}, f32[768,128]{1,0:T(8,128)S(1)}, f32[8,128]{1,0:T(8,128)}, f32[128,128]{1,0:T(8,128)S(1)}) custom-call(s32[1]{0:T(128)S(6)} %copy.55.refs_0_, f32[2560,128]{1,0:T(8,128)S(1)} %constant_dynamic-update-slice_fusion.refs_1_.refs_2_, ...), custom_call_target="tpu_custom_call" | custom-call | flops 3221225472 | bytes 16777216 | tf_op jit(solution)/shard_map/operator/pallas_call | solution.py:86
  28.6 15.3 %all-to-all-start = ((f32[128,1,384]{2,1,0:T(1,128)}), f32[128,1,384]{2,1,0:T(1,128)S(1)}, u32[]{:S(2)}, u32[]{:S(2)}) async-start(f32[128,1,384]{2,1,0:T(1,128)} %copy.16), calls=%async_computation | async-start | bytes 393216 | tf_op jit(solution)/shard_map/all_to_all | solution.py:171
  43.9 3.5 %collective-permute-start.2 = (f32[768,128]{1,0:T(8,128)S(1)}, f32[768,128]{1,0:T(8,128)S(1)}, u32[]{:S(2)}, u32[]{:S(2)}) collective-permute-start(f32[768,128]{1,0:T(8,128)S(1)} %get-tuple-element.18), channel_id=1, source_target_pairs={{0,1},{1,2},{2,3},{3,4},{4,5},{5,6},{6,7},{7,8},{8,9},{9,10},{10,1... | collective-permute-start | bytes 1179656 | tf_op jit(solution)/shard_map/ppermute | solution.py:163
  49.4 4.9 %all-to-all-done = f32[128,1,384]{2,1,0:T(1,128)S(1)} async-done(((f32[128,1,384]{2,1,0:T(1,128)}), f32[128,1,384]{2,1,0:T(1,128)S(1)}, u32[]{:S(2)}, u32[]{:S(2)}) %all-to-all-start) | async-done | bytes 196640 | tf_op jit(solution)/shard_map/all_to_all | solution.py:171
  59.9 12.1 %all-to-all-start.1 = ((f32[128,1,512]{2,1,0:T(1,128)}), f32[128,1,512]{2,1,0:T(1,128)S(1)}, u32[]{:S(2)}, u32[]{:S(2)}) async-start(f32[128,1,512]{2,1,0:T(1,128)} %copy.17), calls=%async_computation.1 | async-start | bytes 524288 | tf_op jit(solution)/shard_map/all_to_all | solution.py:171
  72.9 3.5 %collective-permute-start.4 = (f32[768,128]{1,0:T(8,128)}, f32[768,128]{1,0:T(8,128)}, u32[]{:S(2)}, u32[]{:S(2)}) collective-permute-start(f32[768,128]{1,0:T(8,128)} %get-tuple-element.61), channel_id=1, source_target_pairs={{0,1},{1,2},{2,3},{3,4},{4,5},{5,6},{6,7},{7,8},{8,9},{9,10},{10,1... | collective-permute-start | bytes 1179656 | tf_op jit(solution)/shard_map/ppermute | solution.py:155
  79.3 3.6 %collective-permute-start.6 = (f32[768,128]{1,0:T(8,128)}, f32[768,128]{1,0:T(8,128)S(1)}, u32[]{:S(2)}, u32[]{:S(2)}) collective-permute-start(f32[768,128]{1,0:T(8,128)} %get-tuple-element.63), channel_id=1, source_target_pairs={{0,1},{1,2},{2,3},{3,4},{4,5},{5,6},{6,7},{7,8},{8,9},{9,10},{10,1... | collective-permute-start | bytes 1179656 | tf_op jit(solution)/shard_map/ppermute | solution.py:155
  85.1 2.5 inverse.1
  88.3 3.9 %collective-permute-done.7 = f32[768,128]{1,0:T(8,128)S(1)} collective-permute-done((f32[768,128]{1,0:T(8,128)}, f32[768,128]{1,0:T(8,128)S(1)}, u32[]{:S(2)}, u32[]{:S(2)}) %collective-permute-start.7) | collective-permute-done | bytes 393248 | tf_op jit(solution)/shard_map/ppermute | solution.py:156
  96.8 5.8 %copy-done.2 = f32[1,2048,2048]{2,1,0:T(8,128)S(1)} copy-done((f32[1,2048,2048]{2,1,0:T(8,128)S(1)}, f32[1,2048,2048]{2,1,0:T(8,128)}, u32[]{:S(2)}) %copy-start.2) | copy-done | bytes 16777240
  102.6 8.9 %operator.5 = (f32[768,128]{1,0:T(8,128)}, f32[1024,128]{1,0:T(8,128)S(1)}, f32[768,128]{1,0:T(8,128)}, f32[8,128]{1,0:T(8,128)S(1)}, f32[128,128]{1,0:T(8,128)S(1)}) custom-call(s32[1]{0:T(128)S(6)} %copy.55.refs_0_, f32[2560,128]{1,0:T(8,128)S(1)} %fusion.refs_1_, f32[2560,128]{1,0:T(8,128)S(1)} %pad_maximum_fusion.refs_2_, f32[1,2048,2048]{2,1,0:T(8,128)S(1)} %copy-done.2), custom_call_target="tpu_custom_call" | custom-call | flops 3221225472 | bytes 16777216 | tf_op jit(solution)/shard_map/operator/pallas_call | solution.py:86
  113.5 3.1 %collective-permute-start.9 = (f32[768,128]{1,0:T(8,128)}, f32[768,128]{1,0:T(8,128)}, u32[]{:S(2)}, u32[]{:S(2)}) collective-permute-start(f32[768,128]{1,0:T(8,128)} %get-tuple-element.24), channel_id=1, source_target_pairs={{1,0},{2,1},{3,2},{4,3},{5,4},{6,5},{7,6},{8,7},{9,8},{10,9},{11,1... | collective-permute-start | bytes 1179656 | tf_op jit(solution)/shard_map/ppermute | solution.py:162
  117.9 2.7 %convolution_dynamic-update-slice_fusion = f32[128,640]{1,0:T(8,128)} fusion(f32[128,640]{1,0:T(8,128)} %broadcast_dynamic-update-slice_fusion.4, f32[1024,128]{1,0:T(8,128)} %copy-done.12, f32[2560,128]{1,0:T(8,128)S(1)} %fusion.refs_1_), kind=kOutput, calls=%fused_computation.17 | convolution fusion | flops 201326592 | bytes 1114112 | tf_op jit(solution)/shard_map/dot_general | solution.py:29
  123.3 16.3 %all-to-all-start.2 = ((f32[128,1,640]{2,1,0:T(1,128)}), f32[128,1,640]{2,1,0:T(1,128)}, u32[]{:S(2)}, u32[]{:S(2)}) async-start(f32[128,1,640]{2,1,0:T(1,128)} %copy.20), calls=%async_computation.2 | async-start | bytes 655360 | tf_op jit(solution)/shard_map/all_to_all | solution.py:171
  142.6 3.5 %collective-permute-start.10 = (f32[768,128]{1,0:T(8,128)}, f32[768,128]{1,0:T(8,128)S(1)}, u32[]{:S(2)}, u32[]{:S(2)}) collective-permute-start(f32[768,128]{1,0:T(8,128)} %get-tuple-element.59), channel_id=1, source_target_pairs={{0,1},{1,2},{2,3},{3,4},{4,5},{5,6},{6,7},{7,8},{8,9},{9,10},{10,1... | collective-permute-start | bytes 1179656 | tf_op jit(solution)/shard_map/ppermute | solution.py:155
  148.0 2.7 %all-to-all-done.2 = f32[128,1,640]{2,1,0:T(1,128)} async-done(((f32[128,1,640]{2,1,0:T(1,128)}), f32[128,1,640]{2,1,0:T(1,128)}, u32[]{:S(2)}, u32[]{:S(2)}) %all-to-all-start.2) | async-done | bytes 327712 | tf_op jit(solution)/shard_map/all_to_all | solution.py:171
  152.4 3.0 %collective-permute-done.11 = f32[768,128]{1,0:T(8,128)S(1)} collective-permute-done((f32[768,128]{1,0:T(8,128)}, f32[768,128]{1,0:T(8,128)S(1)}, u32[]{:S(2)}, u32[]{:S(2)}) %collective-permute-start.11) | collective-permute-done | bytes 393248 | tf_op jit(solution)/shard_map/ppermute | solution.py:156
  156.9 6.1 %copy-done.3 = f32[1,2048,2048]{2,1,0:T(8,128)S(1)} copy-done((f32[1,2048,2048]{2,1,0:T(8,128)S(1)}, f32[1,2048,2048]{2,1,0:T(8,128)}, u32[]{:S(2)}) %copy-start.3) | copy-done | bytes 16777240
  163.0 8.0 %operator.6 = (f32[768,128]{1,0:T(8,128)S(1)}, f32[1024,128]{1,0:T(8,128)S(1)}, f32[768,128]{1,0:T(8,128)S(1)}, f32[8,128]{1,0:T(8,128)S(1)}, f32[128,128]{1,0:T(8,128)S(1)}) custom-call(s32[1]{0:T(128)S(6)} %copy.55.refs_0_, f32[2560,128]{1,0:T(8,128)S(1)} %multiply_subtract_fusion.refs_1_, f32[2560,128]{1,0:T(8,128)S(1)} %pad_maximum_fusion.refs_2_, ...), custom_call_target="tpu_custom_call" | custom-call | flops 3221225472 | bytes 16777216 | tf_op jit(solution)/shard_map/operator/pallas_call | solution.py:86
  177.9 12.5 %all-to-all-start.3 = ((f32[128,1,640]{2,1,0:T(1,128)}), f32[128,1,640]{2,1,0:T(1,128)}, u32[]{:S(2)}, u32[]{:S(2)}) async-start(f32[128,1,640]{2,1,0:T(1,128)} %copy.21), calls=%async_computation.3 | async-start | bytes 655360 | tf_op jit(solution)/shard_map/all_to_all | solution.py:171
  192.8 3.5 %collective-permute-start.12 = (f32[768,128]{1,0:T(8,128)}, f32[768,128]{1,0:T(8,128)}, u32[]{:S(2)}, u32[]{:S(2)}) collective-permute-start(f32[768,128]{1,0:T(8,128)} %copy-done.9), channel_id=1, source_target_pairs={{0,1},{1,2},{2,3},{3,4},{4,5},{5,6},{6,7},{7,8},{8,9},{9,10},{10,1... | collective-permute-start | bytes 1179656 | tf_op jit(solution)/shard_map/ppermute | solution.py:163
  198.3 3.2 %all-to-all-done.3 = f32[128,1,640]{2,1,0:T(1,128)} async-done(((f32[128,1,640]{2,1,0:T(1,128)}), f32[128,1,640]{2,1,0:T(1,128)}, u32[]{:S(2)}, u32[]{:S(2)}) %all-to-all-start.3) | async-done | bytes 327712 | tf_op jit(solution)/shard_map/all_to_all | solution.py:171
  209.4 2.6 collective-permute-start.15
  214.3 4.2 %collective-permute-done.15 = f32[768,128]{1,0:T(8,128)S(1)} collective-permute-done((f32[768,128]{1,0:T(8,128)S(1)}, f32[768,128]{1,0:T(8,128)S(1)}, u32[]{:S(2)}, u32[]{:S(2)}) %collective-permute-start.15) | collective-permute-done | bytes 393248 | tf_op jit(solution)/shard_map/ppermute | solution.py:156
  219.9 5.8 %copy-done.4 = f32[1,2048,2048]{2,1,0:T(8,128)S(1)} copy-done((f32[1,2048,2048]{2,1,0:T(8,128)S(1)}, f32[1,2048,2048]{2,1,0:T(8,128)}, u32[]{:S(2)}) %copy-start.4) | copy-done | bytes 16777240
  225.6 5.9 %operator.7 = f32[8,128]{1,0:T(8,128)S(1)} custom-call(s32[1]{0:T(128)S(6)} %copy.55.refs_0_, f32[2560,128]{1,0:T(8,128)S(1)} %fusion.3.refs_1_, f32[2560,128]{1,0:T(8,128)S(1)} %pad_maximum_fusion.refs_2_, f32[1,2048,2048]{2,1,0:T(8,128)S(1)} %copy-done.4), custom_call_target="tpu_custom_call" | custom-call | flops 3221225472 | bytes 16777216 | tf_op jit(solution)/shard_map/operator/pallas_call | solution.py:86
  233.3 16.3 %all-to-all-start.4 = ((f32[128,1,384]{2,1,0:T(1,128)}), f32[128,1,384]{2,1,0:T(1,128)S(1)}, u32[]{:S(2)}, u32[]{:S(2)}) async-start(f32[128,1,384]{2,1,0:T(1,128)} %broadcast.52), calls=%async_computation.4 | async-start | bytes 393216 | tf_op jit(solution)/shard_map/all_to_all | solution.py:171
  250.7 9.3 %all-to-all-done.4 = f32[128,1,384]{2,1,0:T(1,128)S(1)} async-done(((f32[128,1,384]{2,1,0:T(1,128)}), f32[128,1,384]{2,1,0:T(1,128)S(1)}, u32[]{:S(2)}, u32[]{:S(2)}) %all-to-all-start.4) | async-done | bytes 196640 | tf_op jit(solution)/shard_map/all_to_all | solution.py:171
  263.6 2.5 add_add_fusion
  (172 shorter events, 67.5 us)
Async XLA Ops:
  0.6 87.0 %copy-start = (f32[128,128]{1,0:T(8,128)S(1)}, f32[128,128]{1,0:T(8,128)}, u32[]{:S(2)}) copy-start(f32[128,128]{1,0:T(8,128)} %param.9) | copy-start | bytes 196612
  1.9 11.3 %collective-permute-start.1 = (f32[768,128]{1,0:T(8,128)S(1)}, f32[768,128]{1,0:T(8,128)S(1)}, u32[]{:S(2)}, u32[]{:S(2)}) collective-permute-start(f32[768,128]{1,0:T(8,128)S(1)} %get-tuple-element.65), channel_id=1, source_target_pairs={{1,0},{2,1},{3,2},{4,3},{5,4},{6,5},{7,6},{8,7},{9,8},{10,9},{11,1... | collective-permute-start | bytes 1179656 | tf_op jit(solution)/shard_map/ppermute | solution.py:156
  5.2 7.9 %collective-permute-start = (f32[768,128]{1,0:T(8,128)S(1)}, f32[768,128]{1,0:T(8,128)S(1)}, u32[]{:S(2)}, u32[]{:S(2)}) collective-permute-start(f32[768,128]{1,0:T(8,128)S(1)} %get-tuple-element.66), channel_id=1, source_target_pairs={{0,1},{1,2},{2,3},{3,4},{4,5},{5,6},{6,7},{7,8},{8,9},{9,10},{10,1... | collective-permute-start | bytes 1179656 | tf_op jit(solution)/shard_map/ppermute | solution.py:155
  28.6 25.7 %all-to-all-start = ((f32[128,1,384]{2,1,0:T(1,128)}), f32[128,1,384]{2,1,0:T(1,128)S(1)}, u32[]{:S(2)}, u32[]{:S(2)}) async-start(f32[128,1,384]{2,1,0:T(1,128)} %copy.16), calls=%async_computation | async-start | bytes 393216 | tf_op jit(solution)/shard_map/all_to_all | solution.py:171
  43.9 10.5 %collective-permute-start.2 = (f32[768,128]{1,0:T(8,128)S(1)}, f32[768,128]{1,0:T(8,128)S(1)}, u32[]{:S(2)}, u32[]{:S(2)}) collective-permute-start(f32[768,128]{1,0:T(8,128)S(1)} %get-tuple-element.18), channel_id=1, source_target_pairs={{0,1},{1,2},{2,3},{3,4},{4,5},{5,6},{6,7},{7,8},{8,9},{9,10},{10,1... | collective-permute-start | bytes 1179656 | tf_op jit(solution)/shard_map/ppermute | solution.py:163
  47.5 9.2 %collective-permute-start.3 = (f32[768,128]{1,0:T(8,128)S(1)}, f32[768,128]{1,0:T(8,128)}, u32[]{:S(2)}, u32[]{:S(2)}) collective-permute-start(f32[768,128]{1,0:T(8,128)S(1)} %get-tuple-element.19), channel_id=1, source_target_pairs={{1,0},{2,1},{3,2},{4,3},{5,4},{6,5},{7,6},{8,7},{9,8},{10,9},{11,1... | collective-permute-start | bytes 1179656 | tf_op jit(solution)/shard_map/ppermute | solution.py:162
  57.9 38.9 %copy-start.12 = (f32[1024,128]{1,0:T(8,128)}, f32[1024,128]{1,0:T(8,128)S(1)}, u32[]{:S(2)}) copy-start(f32[1024,128]{1,0:T(8,128)S(1)} %pad_add_fusion.2) | copy-start | bytes 1572868
  57.9 14.1 %copy-start.17 = (f32[1024,128]{1,0:T(8,128)S(1)}, f32[1024,128]{1,0:T(8,128)}, u32[]{:S(2)}) copy-start(f32[1024,128]{1,0:T(8,128)} %param.7) | copy-start | bytes 1572868
  59.9 25.2 %all-to-all-start.1 = ((f32[128,1,512]{2,1,0:T(1,128)}), f32[128,1,512]{2,1,0:T(1,128)S(1)}, u32[]{:S(2)}, u32[]{:S(2)}) async-start(f32[128,1,512]{2,1,0:T(1,128)} %copy.17), calls=%async_computation.1 | async-start | bytes 524288 | tf_op jit(solution)/shard_map/all_to_all | solution.py:171
  72.9 20.6 %collective-permute-start.4 = (f32[768,128]{1,0:T(8,128)}, f32[768,128]{1,0:T(8,128)}, u32[]{:S(2)}, u32[]{:S(2)}) collective-permute-start(f32[768,128]{1,0:T(8,128)} %get-tuple-element.61), channel_id=1, source_target_pairs={{0,1},{1,2},{2,3},{3,4},{4,5},{5,6},{6,7},{7,8},{8,9},{9,10},{10,1... | collective-permute-start | bytes 1179656 | tf_op jit(solution)/shard_map/ppermute | solution.py:155
  76.4 17.1 %collective-permute-start.5 = (f32[768,128]{1,0:T(8,128)}, f32[768,128]{1,0:T(8,128)}, u32[]{:S(2)}, u32[]{:S(2)}) collective-permute-start(f32[768,128]{1,0:T(8,128)} %get-tuple-element.62), channel_id=1, source_target_pairs={{1,0},{2,1},{3,2},{4,3},{5,4},{6,5},{7,6},{8,7},{9,8},{10,9},{11,1... | collective-permute-start | bytes 1179656 | tf_op jit(solution)/shard_map/ppermute | solution.py:156
  79.3 9.0 %collective-permute-start.6 = (f32[768,128]{1,0:T(8,128)}, f32[768,128]{1,0:T(8,128)S(1)}, u32[]{:S(2)}, u32[]{:S(2)}) collective-permute-start(f32[768,128]{1,0:T(8,128)} %get-tuple-element.63), channel_id=1, source_target_pairs={{0,1},{1,2},{2,3},{3,4},{4,5},{5,6},{6,7},{7,8},{8,9},{9,10},{10,1... | collective-permute-start | bytes 1179656 | tf_op jit(solution)/shard_map/ppermute | solution.py:155
  82.9 9.3 %collective-permute-start.7 = (f32[768,128]{1,0:T(8,128)}, f32[768,128]{1,0:T(8,128)S(1)}, u32[]{:S(2)}, u32[]{:S(2)}) collective-permute-start(f32[768,128]{1,0:T(8,128)} %get-tuple-element.64), channel_id=1, source_target_pairs={{1,0},{2,1},{3,2},{4,3},{5,4},{6,5},{7,6},{8,7},{9,8},{10,9},{11,1... | collective-permute-start | bytes 1179656 | tf_op jit(solution)/shard_map/ppermute | solution.py:156
  111.5 28.1 %collective-permute-start.8 = (f32[768,128]{1,0:T(8,128)}, f32[768,128]{1,0:T(8,128)}, u32[]{:S(2)}, u32[]{:S(2)}) collective-permute-start(f32[768,128]{1,0:T(8,128)} %get-tuple-element.23), channel_id=1, source_target_pairs={{0,1},{1,2},{2,3},{3,4},{4,5},{5,6},{6,7},{7,8},{8,9},{9,10},{10,1... | collective-permute-start | bytes 1179656 | tf_op jit(solution)/shard_map/ppermute | solution.py:163
  113.5 26.2 %collective-permute-start.9 = (f32[768,128]{1,0:T(8,128)}, f32[768,128]{1,0:T(8,128)}, u32[]{:S(2)}, u32[]{:S(2)}) collective-permute-start(f32[768,128]{1,0:T(8,128)} %get-tuple-element.24), channel_id=1, source_target_pairs={{1,0},{2,1},{3,2},{4,3},{5,4},{6,5},{7,6},{8,7},{9,8},{10,9},{11,1... | collective-permute-start | bytes 1179656 | tf_op jit(solution)/shard_map/ppermute | solution.py:162
  123.3 27.5 %all-to-all-start.2 = ((f32[128,1,640]{2,1,0:T(1,128)}), f32[128,1,640]{2,1,0:T(1,128)}, u32[]{:S(2)}, u32[]{:S(2)}) async-start(f32[128,1,640]{2,1,0:T(1,128)} %copy.20), calls=%async_computation.2 | async-start | bytes 655360 | tf_op jit(solution)/shard_map/all_to_all | solution.py:171
  142.6 9.8 %collective-permute-start.10 = (f32[768,128]{1,0:T(8,128)}, f32[768,128]{1,0:T(8,128)S(1)}, u32[]{:S(2)}, u32[]{:S(2)}) collective-permute-start(f32[768,128]{1,0:T(8,128)} %get-tuple-element.59), channel_id=1, source_target_pairs={{0,1},{1,2},{2,3},{3,4},{4,5},{5,6},{6,7},{7,8},{8,9},{9,10},{10,1... | collective-permute-start | bytes 1179656 | tf_op jit(solution)/shard_map/ppermute | solution.py:155
  146.1 9.3 %collective-permute-start.11 = (f32[768,128]{1,0:T(8,128)}, f32[768,128]{1,0:T(8,128)S(1)}, u32[]{:S(2)}, u32[]{:S(2)}) collective-permute-start(f32[768,128]{1,0:T(8,128)} %get-tuple-element.60), channel_id=1, source_target_pairs={{1,0},{2,1},{3,2},{4,3},{5,4},{6,5},{7,6},{8,7},{9,8},{10,9},{11,1... | collective-permute-start | bytes 1179656 | tf_op jit(solution)/shard_map/ppermute | solution.py:156
  152.4 50.3 %copy-start.38 = (f32[128]{0:T(128)}, f32[128]{0:T(128)S(1)}, u32[]{:S(2)}) copy-start(f32[128]{0:T(128)S(1)} %get-tuple-element.56) | copy-start | bytes 1540
  156.8 14.3 %copy-start.5 = (f32[2560,128]{1,0:T(8,128)}, f32[2560,128]{1,0:T(8,128)S(1)}, u32[]{:S(2)}) copy-start(f32[2560,128]{1,0:T(8,128)S(1)} %multiply_subtract_fusion.refs_1_) | copy-start | bytes 3932164
  172.6 17.8 %copy-start.35 = (f32[128,128]{1,0:T(8,128)S(1)}, f32[128,128]{1,0:T(8,128)}, u32[]{:S(2)}) copy-start(f32[128,128]{1,0:T(8,128)} %copy-done.34) | copy-start | bytes 196612
  177.9 23.6 %all-to-all-start.3 = ((f32[128,1,640]{2,1,0:T(1,128)}), f32[128,1,640]{2,1,0:T(1,128)}, u32[]{:S(2)}, u32[]{:S(2)}) async-start(f32[128,1,640]{2,1,0:T(1,128)} %copy.21), calls=%async_computation.3 | async-start | bytes 655360 | tf_op jit(solution)/shard_map/all_to_all | solution.py:171
  190.4 13.4 %copy-start.40 = (f32[128]{0:T(128)S(1)}, f32[128]{0:T(128)}, u32[]{:S(2)}) copy-start(f32[128]{0:T(128)} %copy-done.39) | copy-start | bytes 1540
  190.4 13.4 %copy-start.42 = (f32[128]{0:T(128)S(1)}, f32[128]{0:T(128)}, u32[]{:S(2)}) copy-start(f32[128]{0:T(128)} %copy-done.41) | copy-start | bytes 1540
  192.8 11.6 %collective-permute-start.12 = (f32[768,128]{1,0:T(8,128)}, f32[768,128]{1,0:T(8,128)}, u32[]{:S(2)}, u32[]{:S(2)}) collective-permute-start(f32[768,128]{1,0:T(8,128)} %copy-done.9), channel_id=1, source_target_pairs={{0,1},{1,2},{2,3},{3,4},{4,5},{5,6},{6,7},{7,8},{8,9},{9,10},{10,1... | collective-permute-start | bytes 1179656 | tf_op jit(solution)/shard_map/ppermute | solution.py:163
  196.4 9.4 %collective-permute-start.13 = (f32[768,128]{1,0:T(8,128)}, f32[768,128]{1,0:T(8,128)}, u32[]{:S(2)}, u32[]{:S(2)}) collective-permute-start(f32[768,128]{1,0:T(8,128)} %copy-done.8), channel_id=1, source_target_pairs={{1,0},{2,1},{3,2},{4,3},{5,4},{6,5},{7,6},{8,7},{9,8},{10,9},{11,1... | collective-permute-start | bytes 1179656 | tf_op jit(solution)/shard_map/ppermute | solution.py:162
  205.8 12.7 %copy-start.31 = (f32[768,128]{1,0:T(8,128)S(1)}, f32[768,128]{1,0:T(8,128)}, u32[]{:S(2)}) copy-start(f32[768,128]{1,0:T(8,128)} %copy-done.30) | copy-start | bytes 1179652
  207.2 7.1 %collective-permute-start.14 = (f32[768,128]{1,0:T(8,128)S(1)}, f32[768,128]{1,0:T(8,128)S(1)}, u32[]{:S(2)}, u32[]{:S(2)}) collective-permute-start(f32[768,128]{1,0:T(8,128)S(1)} %get-tuple-element.57), channel_id=1, source_target_pairs={{0,1},{1,2},{2,3},{3,4},{4,5},{5,6},{6,7},{7,8},{8,9},{9,10},{10,1... | collective-permute-start | bytes 1179656 | tf_op jit(solution)/shard_map/ppermute | solution.py:155
  209.4 9.1 %collective-permute-start.15 = (f32[768,128]{1,0:T(8,128)S(1)}, f32[768,128]{1,0:T(8,128)S(1)}, u32[]{:S(2)}, u32[]{:S(2)}) collective-permute-start(f32[768,128]{1,0:T(8,128)S(1)} %get-tuple-element.58), channel_id=1, source_target_pairs={{1,0},{2,1},{3,2},{4,3},{5,4},{6,5},{7,6},{8,7},{9,8},{10,9},{11,1... | collective-permute-start | bytes 1179656 | tf_op jit(solution)/shard_map/ppermute | solution.py:156
  231.6 32.0 %copy-start.25 = (f32[1024,128]{1,0:T(8,128)S(1)}, f32[1024,128]{1,0:T(8,128)}, u32[]{:S(2)}) copy-start(f32[1024,128]{1,0:T(8,128)} %fusion.5) | copy-start | bytes 1572868
  231.6 32.0 %copy-start.26 = (f32[1024,128]{1,0:T(8,128)S(1)}, f32[1024,128]{1,0:T(8,128)}, u32[]{:S(2)}) copy-start(f32[1024,128]{1,0:T(8,128)} %convolution_bitcast_fusion.2) | copy-start | bytes 1572868
  233.3 26.7 %all-to-all-start.4 = ((f32[128,1,384]{2,1,0:T(1,128)}), f32[128,1,384]{2,1,0:T(1,128)S(1)}, u32[]{:S(2)}, u32[]{:S(2)}) async-start(f32[128,1,384]{2,1,0:T(1,128)} %broadcast.52), calls=%async_computation.4 | async-start | bytes 393216 | tf_op jit(solution)/shard_map/all_to_all | solution.py:171
  (33 other events, 190.6 us)

commit v2 on v0

v2 whole, which is shorter than its diff:
```python
import functools

import jax
import jax.numpy as jnp
from jax import lax
from jax.experimental import pallas as pl
from jax.experimental.pallas import tpu as pltpu
from jax.sharding import Mesh
from jax.sharding import PartitionSpec as P

GX_GY = ("gx", "gy_0", "gy_1", "gy_2")
HIGHEST = lax.Precision.HIGHEST
F32 = jnp.float32
BF16 = jnp.bfloat16

SLAB = 1024
WINDOW = 2048
REACH = 768
SKIP = SLAB - REACH
HIGH = REACH + SLAB
EXT = SLAB + 2 * REACH
R = 128
DEVICES = 128
TILE = 256
STEPS = WINDOW // TILE
OWN = slice(REACH, HIGH)

MATRIX = jax.ShapeDtypeStruct((R, R), F32)
EXTENDED = jax.ShapeDtypeStruct((EXT, R), F32)


def full_dot(a, b):
    return jnp.dot(a, b, precision=HIGHEST, preferred_element_type=F32)


def contract_rows(a, b):
    return lax.dot_general(
        a, b, (((0,), (0,)), ((), ())), precision=HIGHEST, preferred_element_type=F32
    )


def split_bf16(x):
    high = x.astype(BF16)
    return high, (x - high.astype(F32)).astype(BF16)


def column_sum(a, b):
    return jnp.sum(a * b, axis=0, keepdims=True)


def part(arrived, index, count):
    return arrived[pl.ds(index, DEVICES, stride=count), :]


def total(arrived, index, count):
    return jnp.sum(part(arrived, index, count), axis=0, keepdims=True)


def put(joined, index, count, value):
    joined[pl.ds(index, DEVICES, stride=count), :] = jnp.broadcast_to(value, (DEVICES, R))


def sides(parity, scale):
    partner = pl.multiple_of(scale * (1 - parity), 8)
    remote = pl.multiple_of(scale * parity, 8)
    return pl.ds(partner, REACH), pl.ds(remote, REACH)


def assemble(ext, pieces, parity):
    own, partner, remote = pieces
    at_partner, at_remote = sides(parity, HIGH)
    ext[OWN, :] = own[...]
    ext[at_partner, :] = partner[...]
    ext[at_remote, :] = remote[...]


def invert(gram, inverse):
    row = lax.broadcasted_iota(jnp.int32, (R, R), 0)
    column = lax.broadcasted_iota(jnp.int32, (R, R), 1)
    identity = jnp.where(row == column, 1.0, 0.0).astype(F32)
    diagonal = gram * identity
    across = lax.rsqrt(jnp.sum(diagonal, axis=0, keepdims=True))
    along = lax.rsqrt(jnp.sum(diagonal, axis=1, keepdims=True))
    scaled = gram * across * along
    bound = jnp.max(jnp.sum(jnp.abs(scaled), axis=0, keepdims=True), axis=1, keepdims=True)
    inverse[...] = identity / bound

    def refine():
        current = inverse[...]
        rest = identity - full_dot(scaled, current)
        inverse[...] = current + full_dot(current, rest)
        return jnp.max(jnp.abs(rest))

    def body(carry):
        return carry[0] + 1, refine()

    lax.while_loop(lambda c: (c[0] < 60) & (c[1] > 1e-3), body, (jnp.int32(0), jnp.float32(1.0)))
    refine()
    inverse[...] = inverse[...] * across * along


def multiply(start, step, ext, schur, halves):
    @pl.when(step == 0)
    def _():
        high, low = split_bf16(ext[pl.ds(start, WINDOW), :])
        halves[:, :R] = high
        halves[:, R:] = low

    high, low = split_bf16(schur[...])
    both = jnp.dot(high, halves[...], preferred_element_type=F32)
    rest = jnp.dot(low, halves[:, :R], preferred_element_type=F32)
    return both[:, :R] + both[:, R:] + rest


def add_form(form, ext, rows, product):
    form[...] += jnp.sum((ext[rows, :] * product).reshape(TILE // 8, 8, R), axis=0)


def clear(form, cross, image):
    form[...] = jnp.zeros_like(form)
    cross[...] = jnp.zeros_like(cross)
    image[: EXT - WINDOW, :] = jnp.zeros((EXT - WINDOW, R), F32)
    image[WINDOW:, :] = jnp.zeros((EXT - WINDOW, R), F32)


def deliver(image, parity, own, partner, remote):
    at_partner, at_remote = sides(parity, HIGH)
    own[...] = image[OWN, :]
    partner[...] = image[at_partner, :]
    remote[...] = image[at_remote, :]


def first_kernel(
    place, own, partner, remote, gram, coarse, schur,
    out_own, out_partner, out_remote, joined,
    ext, halves, image, form, cross,
):
    step = pl.program_id(0)
    start, parity = place[0] - SKIP, place[1]

    @pl.when(step == 0)
    def _():
        assemble(ext, (own, partner, remote), parity)
        clear(form, cross, image)
        put(joined, 0, 3, gram[...])
        put(joined, 1, 3, coarse[...])

    product = multiply(start, step, ext, schur, halves)
    rows = pl.ds(start + step * TILE, TILE)
    cross[...] += contract_rows(ext[rows, :], product)
    image[rows, :] = product

    @pl.when(step == STEPS - 1)
    def _():
        deliver(image, parity, out_own, out_partner, out_remote)
        put(joined, 2, 3, cross[...])


def start_kernel(
    place, arrived, load, square,
    right_own, right_partner, right_remote,
    basis_own, basis_partner, basis_remote,
    image_own, image_partner, image_remote, schur,
    out_own, out_partner, out_remote, joined,
    residual, z_ext, inverse, first, amp, stiff,
    halves, image, form, cross, early,
):
    step = pl.program_id(0)
    start, parity = place[0] - SKIP, place[1]

    @pl.when(step == 0)
    def _():
        invert(part(arrived, 0, 3), inverse)
        stiff[...] = part(arrived, 2, 3)
        first[...] = full_dot(inverse[...], load[...])
        amp[...] = full_dot(inverse[...], part(arrived, 1, 3) - full_dot(stiff[...], first[...]))
        assemble(z_ext, (image_own, image_partner, image_remote), parity)
        assemble(image, (basis_own, basis_partner, basis_remote), parity)
        assemble(residual, (right_own, right_partner, right_remote), parity)
        residual[...] = (
            residual[...]
            - full_dot(z_ext[...], first[...])
            - full_dot(image[...], amp[...])
        )
        clear(form, cross, image)
        own = residual[OWN, :]
        put(joined, 0, 5, column_sum(own, own))
        put(joined, 4, 5, square[...])
        early[...] = contract_rows(image_own[...], own)
        put(joined, 2, 5, early[...])

    product = multiply(start, step, residual, schur, halves)
    rows = pl.ds(start + step * TILE, TILE)
    add_form(form, residual, rows, product)
    cross[...] += contract_rows(z_ext[rows, :], product)
    image[rows, :] = product

    @pl.when(step == STEPS - 1)
    def _():
        deliver(image, parity, out_own, out_partner, out_remote)
        put(joined, 1, 5, jnp.sum(form[...], axis=0, keepdims=True))
        put(joined, 3, 5, cross[...])


def middle_kernel(
    place, arrived, last, z_ext, own, partner, remote, schur,
    out_own, out_partner, out_remote, joined, residual, w_ext, scalars,
    halves, image, form, cross,
):
    step = pl.program_id(0)
    start, parity = place[0] - SKIP, place[1]

    @pl.when(step == 0)
    def _():
        energy = total(arrived, 0, 5)
        length = energy / total(arrived, 1, 5)
        assemble(w_ext, (own, partner, remote), parity)
        residual[...] = last[...] - length * w_ext[...]
        clear(form, cross, image)
        mine = residual[OWN, :]
        put(joined, 0, 5, column_sum(mine, mine))
        put(joined, 2, 5, total(arrived, 2, 5))
        put(joined, 3, 5, total(arrived, 3, 5))
        scalars[...] = jnp.zeros_like(scalars)
        scalars[0:1, :] = energy
        scalars[1:2, :] = length
        scalars[2:3, :] = total(arrived, 4, 5)

    product = multiply(start, step, residual, schur, halves)
    rows = pl.ds(start + step * TILE, TILE)
    add_form(form, residual, rows, product)
    cross[...] += contract_rows(z_ext[rows, :], product)
    image[rows, :] = product

    @pl.when(step == STEPS - 1)
    def _():
        deliver(image, parity, out_own, out_partner, out_remote)
        put(joined, 1, 5, jnp.sum(form[...], axis=0, keepdims=True))
        put(joined, 4, 5, cross[...])


def last_kernel(
    place, arrived, scalars, last, w_last, z_ext, own, partner, remote, inverse, stiff, schur,
    joined, new_own, numbers, matrices,
    residual, halves, form, w_ext,
):
    step = pl.program_id(0)
    start, parity = place[0] - SKIP, place[1]

    @pl.when(step == 0)
    def _():
        energy0, length0 = scalars[0:1, :], scalars[1:2, :]
        e0, f0 = part(arrived, 2, 5), part(arrived, 3, 5)
        c1 = -length0 * e0
        a1 = full_dot(inverse[...], c1)
        e1 = e0 - length0 * f0
        energy1 = total(arrived, 0, 5) - column_sum(c1, a1)
        stiff_a1 = full_dot(stiff[...], a1)
        ratio0 = energy1 / energy0
        curve1 = (
            total(arrived, 1, 5)
            - 2.0 * column_sum(a1, e1)
            + column_sum(a1, stiff_a1)
            - ratio0 * energy1 / length0
        )
        length1 = energy1 / curve1
        assemble(w_ext, (own, partner, remote), parity)
        residual[...] = last[...] - length1 * (
            w_ext[...] - full_dot(z_ext[...], a1) + ratio0 * w_last[...]
        )
        mine = residual[OWN, :]
        new_own[...] = mine
        put(joined, 0, 4, column_sum(mine, mine))
        put(joined, 2, 4, total(arrived, 4, 5))
        put(joined, 3, 4, scalars[2:3, :])
        numbers[...] = jnp.zeros_like(numbers)
        numbers[0:1, :] = length0
        numbers[1:2, :] = length1
        numbers[2:3, :] = ratio0
        numbers[3:4, :] = energy1
        d_coarse = e1 - stiff_a1 + ratio0 * e0
        matrices[0] = a1
        matrices[1] = c1 - length1 * d_coarse
        matrices[2] = d_coarse
        matrices[3] = e1 - length1 * ratio0 * f0
        form[...] = jnp.zeros_like(form)

    product = multiply(start, step, residual, schur, halves)
    add_form(form, residual, pl.ds(start + step * TILE, TILE), product)

    @pl.when(step == STEPS - 1)
    def _():
        put(joined, 1, 4, jnp.sum(form[...], axis=0, keepdims=True))


def direction_kernel(
    numbers, matrices, inverse, stiff, first, basis, r0, r1, r2,
    base, d1, p2, small,
):
    length0, length1, ratio0 = numbers[0:1, :], numbers[1:2, :], numbers[2:3, :]
    a1 = matrices[0]
    a2 = full_dot(inverse[...], matrices[1])
    d1[...] = r1[...] - full_dot(basis[...], a1) + ratio0 * r0[...]
    p2[...] = r2[...] - full_dot(basis[...], a2)
    base[...] = full_dot(basis[...], first[...]) + length0 * r0[...] + length1 * d1[...]
    small[0] = a2
    small[1] = full_dot(stiff[...], a2)


def final_kernel(
    arrived, numbers, matrices, small, inverse, amp, base, d1, p2,
    multipliers, amplitudes,
):
    length1, energy1 = numbers[1:2, :], numbers[3:4, :]
    a2, stiff_a2 = small[0], small[1]
    f1, square = part(arrived, 2, 4), part(arrived, 3, 4)
    e2 = matrices[3] - length1 * (f1 - full_dot(square, matrices[0]))
    energy2 = total(arrived, 0, 4) - column_sum(matrices[1], a2)
    ratio1 = energy2 / energy1
    curve2 = (
        total(arrived, 1, 4)
        - 2.0 * column_sum(a2, e2)
        + column_sum(a2, stiff_a2)
        - ratio1 * energy2 / length1
    )
    length2 = energy2 / curve2
    multipliers[...] = base[...] + length2 * (p2[...] + ratio1 * d1[...])
    c3 = matrices[1] - length2 * (e2 - stiff_a2 + ratio1 * matrices[2])
    amplitudes[...] = amp[...] + full_dot(inverse[...], c3)


def sum_kernel(place, own, partner, remote, total_own, to_partner, to_remote):
    at_partner, at_remote = sides(place[1], SKIP)
    total_own[...] = own[...]
    total_own[at_partner, :] += partner[...]
    total_own[at_remote, :] += remote[...]
    to_partner[...] = total_own[at_partner, :]
    to_remote[...] = total_own[at_remote, :]


def turn_kernel(arrived, joined, *, count):
    for i in range(count):
        put(joined, i, count, total(arrived, i, count))


def shape(rows):
    return jax.ShapeDtypeStruct((rows, R), F32)


def whole(array):
    zeros = (0,) * len(array.shape)
    return pl.BlockSpec(array.shape, lambda *_: zeros)


def operator(kernel, place, arrays, schur, outs, scratch):
    return pl.pallas_call(
        kernel,
        grid=(STEPS,),
        in_specs=[pl.BlockSpec(memory_space=pltpu.SMEM)]
        + [whole(a) for a in arrays]
        + [pl.BlockSpec((None, TILE, WINDOW), lambda i: (0, i, 0))],
        out_specs=[whole(o) for o in outs],
        out_shape=outs,
        scratch_shapes=scratch,
        compiler_params=pltpu.CompilerParams(
            dimension_semantics=("arbitrary",), vmem_limit_bytes=50 << 20
        ),
        cost_estimate=pl.CostEstimate(
            flops=8 * WINDOW * WINDOW * R, bytes_accessed=4 * WINDOW * WINDOW, transcendentals=0
        ),
    )(place, *arrays, schur)


def small_call(kernel, arrays, outs, place=None):
    head = [] if place is None else [place]
    return pl.pallas_call(
        kernel,
        in_specs=[pl.BlockSpec(memory_space=pltpu.SMEM)] * len(head)
        + [pl.BlockSpec(memory_space=pltpu.VMEM)] * len(arrays),
        out_specs=[pl.BlockSpec(memory_space=pltpu.VMEM)] * len(outs),
        out_shape=outs,
        compiler_params=pltpu.CompilerParams(vmem_limit_bytes=24 << 20),
        cost_estimate=pl.CostEstimate(
            flops=1 << 30, bytes_accessed=1 << 22, transcendentals=0
        ),
    )(*head, *arrays)


REMOTE = [(i, i + 1) for i in range(1, DEVICES - 1, 2)]
REMOTE = REMOTE + [(b, a) for a, b in REMOTE]


def swapped(to_partner, to_remote):
    remote = lax.ppermute(to_remote, GX_GY, REMOTE)
    partner = lax.ppermute(to_partner, "gy_2", [(0, 1), (1, 0)])
    return partner, remote


def halves_of(own, parity):
    at = SKIP * (1 - parity), SKIP * parity
    return [lax.dynamic_slice_in_dim(own, a, REACH, 0) for a in at]


def exchange(joined, count):
    sent = joined.reshape(DEVICES, 1, count * R)
    arrived = lax.all_to_all(sent, GX_GY, 0, 0, tiled=True)
    return arrived.reshape(DEVICES * count, R)


def summed(ends, place):
    own, *rest = ends
    arrived = swapped(*rest)
    own, *rest = small_call(
        sum_kernel, (own, *arrived), [shape(SLAB), shape(REACH), shape(REACH)], place
    )
    return own, *swapped(*rest)


def local(schur, offsets, right_side, basis, load):
    parity = lax.axis_index("gy_2").astype(jnp.int32)
    place = jnp.concatenate([offsets, parity[None]])
    ends = [shape(SLAB), shape(REACH), shape(REACH)]
    halves = pltpu.VMEM((WINDOW, 2 * R), BF16)
    ext = pltpu.VMEM((EXT, R), F32)
    rows = pltpu.VMEM((8, R), F32)
    square = pltpu.VMEM((R, R), F32)

    basis_sides = swapped(*halves_of(basis, parity))
    right_sides = swapped(*halves_of(right_side, parity))
    gram, coarse = contract_rows(basis, basis), contract_rows(basis, right_side)
    *image, joined = operator(
        first_kernel, place, (basis, *basis_sides, gram, coarse), schur,
        ends + [shape(3 * DEVICES)], [ext, halves, ext, rows, square],
    )
    arrived = exchange(joined, 3)
    image = summed(image, place)
    (joined,) = small_call(
        functools.partial(turn_kernel, count=3), (arrived,), [shape(3 * DEVICES)]
    )
    arrived = exchange(joined, 3)

    *w0, joined, r0, z_ext, inverse, first, amp, stiff = operator(
        start_kernel, place,
        (
            arrived, load, contract_rows(image[0], image[0]),
            right_side, *right_sides, basis, *basis_sides, *image,
        ),
        schur,
        ends + [shape(5 * DEVICES), EXTENDED, EXTENDED] + [MATRIX] * 4,
        [halves, ext, rows, square, square],
    )
    arrived = exchange(joined, 5)
    w0 = summed(w0, place)

    *w1, joined, r1, w0_ext, scalars = operator(
        middle_kernel, place, (arrived, r0, z_ext, *w0), schur,
        ends + [shape(5 * DEVICES), EXTENDED, EXTENDED, shape(8)], [halves, ext, rows, square],
    )
    arrived = exchange(joined, 5)
    w1 = summed(w1, place)

    joined, r2, numbers, matrices = operator(
        last_kernel, place,
        (arrived, scalars, r1, w0_ext, z_ext, *w1, inverse, stiff),
        schur,
        [shape(4 * DEVICES), shape(SLAB), shape(8), jax.ShapeDtypeStruct((4, R, R), F32)],
        [ext, halves, rows, ext],
    )
    arrived = exchange(joined, 4)
    base, d1, p2, small = small_call(
        direction_kernel,
        (numbers, matrices, inverse, stiff, first, basis, r0[OWN], r1[OWN], r2),
        [shape(SLAB)] * 3 + [jax.ShapeDtypeStruct((2, R, R), F32)],
    )
    return tuple(
        small_call(
            final_kernel,
            (arrived, numbers, matrices, small, inverse, amp, base, d1, p2),
            [shape(SLAB), MATRIX],
        )
    )


def solution(mesh):
    split = Mesh(mesh.devices.reshape(mesh.shape["gx"], 4, 4, 2), GX_GY)
    in_specs = (P(GX_GY, None, None), P(GX_GY), P(GX_GY, None), P(GX_GY, None), P())
    out_specs = (P(GX_GY, None), P())
    return jax.shard_map(local, mesh=split, in_specs=in_specs, out_specs=out_specs, check_vma=False)
```

time: 619 us -> 218 us (0.35); the launches traced: 609 us -> 217 us
  blocking collectives: 282 us -> 44.7 us
  matrix products: 96.3 us -> 3.01 us
  Pallas kernels: 0 us -> 68.8 us
  waiting for transfers between devices: 83.5 us -> 33.1 us
  other arithmetic: 32.4 us -> 0.08 us
  local copies, waits for them, and re-layouts: 39.3 us -> 8.71 us
  starting transfers between devices: 73.7 us -> 57.3 us
    all_to_all x27 -> x2, blocking collectives: 282 us -> 44.7 us  [exchange(): arrived = lax.all_to_all(sent, GX_GY, 0, 0, tiled=True)]
    dot_general x13 -> x3, matrix products: 93.2 us -> 3.01 us  [contract_rows(): lax.dot_general(a, b, (((0,), (0,)), ((), ())), precision=HIGHEST, prefer...]
    pallas_call x0 -> x10, Pallas kernels: none -> 68.8 us  [the longest x4 62.3 us: operator(): pl.pallas_call(kernel, grid=(STEPS,), in_specs=[pl.BlockSpec(memory_space...]
    ppermute x16, waiting for transfers between devices: 57.6 us -> 17.3 us  [the longest x8 17.3 us: swapped(): remote = lax.ppermute(to_remote, GX_GY, REMOTE)]
    dynamic_update_slice x4 -> x0, local copies, waits for them, and re-layouts: 23.2 us -> none  [apply_local(): lax.dynamic_update_slice_in_dim(spread, product_block, start_row, 0)]
    another operation x5 -> x0, other arithmetic: 22.9 us -> none  [the longest x3 12.4 us: local(): gram_factor = jnp.linalg.cholesky(gram_matrix)]
    ppermute x16, starting transfers between devices: 39.3 us -> 26.2 us  [the longest x8 21.7 us: swapped(): remote = lax.ppermute(to_remote, GX_GY, REMOTE)]
    all_to_all x5 -> x3, waiting for transfers between devices: 25.8 us -> 15.7 us  [exchange(): arrived = lax.all_to_all(sent, GX_GY, 0, 0, tiled=True)]
  transfers between devices with their start and end apart: 21 -> 19, of which waited for: 21 -> 5; matrix products, arithmetic and copies ran while one was open for 0% -> 3% of each run, Pallas kernels for 0% -> 2%
where the time goes in v2:
time: 218 us; the launch traced here: 217 us
  Pallas kernels  68.8 us (32%)
  starting transfers between devices  57.3 us (26%)
  blocking collectives  44.7 us (21%)
  waiting for transfers between devices  33.1 us (15%)
  local copies, waits for them, and re-layouts  8.71 us (4%)
  matrix products  3.01 us (1%)
    pallas_call x4, Pallas kernels, operator(): pl.pallas_call(kernel, grid=(STEPS,), in_specs=[pl.BlockSpec(memory_space...  62.3 us
    all_to_all x2, blocking collectives, exchange(): arrived = lax.all_to_all(sent, GX_GY, 0, 0, tiled=True)  44.7 us
    all_to_all x3, starting transfers between devices, exchange(): arrived = lax.all_to_all(sent, GX_GY, 0, 0, tiled=True)  31.1 us
    ppermute x8, starting transfers between devices, swapped(): remote = lax.ppermute(to_remote, GX_GY, REMOTE)  21.7 us
    ppermute x8, waiting for transfers between devices, swapped(): remote = lax.ppermute(to_remote, GX_GY, REMOTE)  17.3 us
    all_to_all x3, waiting for transfers between devices, exchange(): arrived = lax.all_to_all(sent, GX_GY, 0, 0, tiled=True)  15.7 us
    pallas_call x6, Pallas kernels, small_call(): pl.pallas_call(kernel, in_specs=[pl.BlockSpec(memory_space=pltpu.SMEM)] *...  6.51 us
    ppermute x8, starting transfers between devices, swapped(): partner = lax.ppermute(to_partner, 'gy_2', [(0, 1), (1, 0)])  4.52 us
  transfers between devices with their start and end apart: 19, of which 5 were waited for; matrix products, arithmetic and copies ran while one was open for 3% of the time, Pallas kernels for 2%

profile of v2, /device:TPU:1, one launch (start us, length us, event | category | flops | bytes accessed | tf_op | source)
XLA Modules:
  0.0 217.3 jit_solution(2142690931477888906)
XLA Ops:
  0.7 1.3 constant_dynamic-slice_fusion.2
  1.9 1.5 collective-permute-start
  3.4 3.2 %collective-permute-start.1 = (f32[768,128]{1,0:T(8,128)S(1)}, f32[768,128]{1,0:T(8,128)S(1)}, u32[]{:S(2)}, u32[]{:S(2)}) collective-permute-start(f32[768,128]{1,0:T(8,128)S(1)} %get-tuple-element.80), channel_id=1, source_target_pairs={{1,2},{3,4},{5,6},{7,8},{9,10},{11,12},{13,14},{15,16},{17,18},{19... | collective-permute-start | bytes 1179656 | tf_op jit(solution)/shard_map/ppermute | solution.py:394
  9.4 3.1 %collective-permute-done.1.remote.basis_remote = f32[768,128]{1,0:T(8,128)S(1)} collective-permute-done((f32[768,128]{1,0:T(8,128)S(1)}, f32[768,128]{1,0:T(8,128)S(1)}, u32[]{:S(2)}, u32[]{:S(2)}) %collective-permute-start.1) | collective-permute-done | bytes 393248 | tf_op jit(solution)/shard_map/ppermute | solution.py:394
  12.5 13.1 %shard_map.68 = (f32[1024,128]{1,0:T(8,128)S(1)}, f32[768,128]{1,0:T(8,128)}, f32[768,128]{1,0:T(8,128)}, f32[384,128]{1,0:T(8,128)}) custom-call(s32[2]{0:T(128)S(1)} %pad_add_fusion.place, f32[1024,128]{1,0:T(8,128)S(1)} %copy-done, f32[768,128]{1,0:T(8,128)S(1)} %collective-permute-done.partner.basis_partner, ...), custom_call_target="tpu_custom_call" | custom-call | flops 4294967296 | bytes 16777216 | tf_op jit(solution)/shard_map/pallas_call | solution.py:356
  25.6 3.7 %collective-permute-start.3 = (f32[768,128]{1,0:T(8,128)}, f32[768,128]{1,0:T(8,128)S(1)}, u32[]{:S(2)}, u32[]{:S(2)}) collective-permute-start(f32[768,128]{1,0:T(8,128)} %get-tuple-element.43), channel_id=1, source_target_pairs={{1,2},{3,4},{5,6},{7,8},{9,10},{11,12},{13,14},{15,16},{17,18},{19... | collective-permute-start | bytes 1179656 | tf_op jit(solution)/shard_map/ppermute | solution.py:394
  29.3 14.0 %all-to-all-start = ((f32[128,1,384]{2,1,0:T(1,128)}), f32[128,1,384]{2,1,0:T(1,128)S(1)}, u32[]{:S(2)}, u32[]{:S(2)}) async-start(f32[128,1,384]{2,1,0:T(1,128)} %bitcast.1), calls=%async_computation | async-start | bytes 393216 | tf_op jit(solution)/shard_map/all_to_all | solution.py:406
  44.3 1.1 collective-permute-start.4
  45.3 2.6 %collective-permute-start.5 = (f32[768,128]{1,0:T(8,128)}, f32[768,128]{1,0:T(8,128)S(1)}, u32[]{:S(2)}, u32[]{:S(2)}) collective-permute-start(f32[768,128]{1,0:T(8,128)} %get-tuple-element.78), channel_id=1, source_target_pairs={{1,2},{3,4},{5,6},{7,8},{9,10},{11,12},{13,14},{15,16},{17,18},{19... | collective-permute-start | bytes 1179656 | tf_op jit(solution)/shard_map/ppermute | solution.py:394
  49.7 1.6 shard_map.70
  51.3 3.5 %collective-permute-start.7 = (f32[768,128]{1,0:T(8,128)}, f32[768,128]{1,0:T(8,128)S(1)}, u32[]{:S(2)}, u32[]{:S(2)}) collective-permute-start(f32[768,128]{1,0:T(8,128)} %get-tuple-element.46), channel_id=1, source_target_pairs={{1,2},{3,4},{5,6},{7,8},{9,10},{11,12},{13,14},{15,16},{17,18},{19... | collective-permute-start | bytes 1179656 | tf_op jit(solution)/shard_map/ppermute | solution.py:394
  55.5 12.3 %all-to-all-start.1 = ((f32[128,1,384]{2,1,0:T(1,128)}), f32[128,1,384]{2,1,0:T(1,128)S(1)}, u32[]{:S(2)}, u32[]{:S(2)}) async-start(f32[128,1,384]{2,1,0:T(1,128)} %bitcast.3), calls=%async_computation.1 | async-start | bytes 393216 | tf_op jit(solution)/shard_map/all_to_all | solution.py:406
  68.8 9.3 %all-to-all-done.1 = f32[128,1,384]{2,1,0:T(1,128)S(1)} async-done(((f32[128,1,384]{2,1,0:T(1,128)}), f32[128,1,384]{2,1,0:T(1,128)S(1)}, u32[]{:S(2)}, u32[]{:S(2)}) %all-to-all-start.1) | async-done | bytes 196640 | tf_op jit(solution)/shard_map/all_to_all | solution.py:406
  78.1 20.1 %shard_map.71 = (f32[1024,128]{1,0:T(8,128)}, f32[768,128]{1,0:T(8,128)S(1)}, f32[768,128]{1,0:T(8,128)S(1)}, f32[640,128]{1,0:T(8,128)S(1)}, f32[2560,128]{1,0:...) custom-call(s32[2]{0:T(128)S(1)} %pad_add_fusion.place, ...), custom_call_target="tpu_custom_call" | custom-call | flops 4294967296 | bytes 16777216 | tf_op jit(solution)/shard_map/pallas_call | solution.py:356
  98.9 2.0 collective-permute-start.9
  100.9 7.1 %collective-permute-done.9.remote = f32[768,128]{1,0:T(8,128)S(1)} collective-permute-done((f32[768,128]{1,0:T(8,128)S(1)}, f32[768,128]{1,0:T(8,128)S(1)}, u32[]{:S(2)}, u32[]{:S(2)}) %collective-permute-start.9) | collective-permute-done | bytes 393248 | tf_op jit(solution)/shard_map/ppermute | solution.py:394
  108.0 1.0 copy-done.4
  109.8 2.5 %collective-permute-start.11 = (f32[768,128]{1,0:T(8,128)S(1)}, f32[768,128]{1,0:T(8,128)S(1)}, u32[]{:S(2)}, u32[]{:S(2)}) collective-permute-start(f32[768,128]{1,0:T(8,128)S(1)} %get-tuple-element.55), channel_id=1, source_target_pairs={{1,2},{3,4},{5,6},{7,8},{9,10},{11,12},{13,14},{15,16},{17,18},{19... | collective-permute-start | bytes 1179656 | tf_op jit(solution)/shard_map/ppermute | solution.py:394
  112.3 22.2 %all_to_all.25 = f32[128,1,640]{2,1,0:T(1,128)S(1)} all-to-all(f32[128,1,640]{2,1,0:T(1,128)S(1)} %bitcast.20), channel_id=1, replica_groups=mesh['gx'=4,'gy_0'=4,'gy_1'=4,'gy_2'=2] {'gx','gy_0','gy_1','gy_2'}, dimensions={0} | all-to-all | bytes 655360 | tf_op jit(solution)/shard_map/all_to_all | solution.py:406
  134.6 14.8 %shard_map.73 = (f32[1024,128]{1,0:T(8,128)S(1)}, f32[768,128]{1,0:T(8,128)S(1)}, f32[768,128]{1,0:T(8,128)S(1)}, f32[640,128]{1,0:T(8,128)S(1)}, f32[2560,128]{...) custom-call(s32[2]{0:T(128)S(1)} %pad_add_fusion.place, f32[640,128]{1,0:T(8,128)S(1)} %bitcast.18, ...), custom_call_target="tpu_custom_call" | custom-call | flops 4294967296 | bytes 16777216 | tf_op jit(solution)/shard_map/pallas_call | solution.py:356
  149.4 1.1 collective-permute-start.12
  150.5 1.9 collective-permute-start.13
  152.4 7.2 %collective-permute-done.13.remote = f32[768,128]{1,0:T(8,128)S(1)} collective-permute-done((f32[768,128]{1,0:T(8,128)S(1)}, f32[768,128]{1,0:T(8,128)S(1)}, u32[]{:S(2)}, u32[]{:S(2)}) %collective-permute-start.13) | collective-permute-done | bytes 393248 | tf_op jit(solution)/shard_map/ppermute | solution.py:394
  160.4 2.3 %collective-permute-start.15 = (f32[768,128]{1,0:T(8,128)S(1)}, f32[768,128]{1,0:T(8,128)S(1)}, u32[]{:S(2)}, u32[]{:S(2)}) collective-permute-start(f32[768,128]{1,0:T(8,128)S(1)} %get-tuple-element.65), channel_id=1, source_target_pairs={{1,2},{3,4},{5,6},{7,8},{9,10},{11,12},{13,14},{15,16},{17,18},{19... | collective-permute-start | bytes 1179656 | tf_op jit(solution)/shard_map/ppermute | solution.py:394
  162.7 22.5 %all_to_all.26 = f32[128,1,640]{2,1,0:T(1,128)S(1)} all-to-all(f32[128,1,640]{2,1,0:T(1,128)S(1)} %bitcast.21), channel_id=1, replica_groups=mesh['gx'=4,'gy_0'=4,'gy_1'=4,'gy_2'=2] {'gx','gy_0','gy_1','gy_2'}, dimensions={0} | all-to-all | bytes 655360 | tf_op jit(solution)/shard_map/all_to_all | solution.py:406
  185.1 14.4 %shard_map.75 = (f32[512,128]{1,0:T(8,128)}, f32[1024,128]{1,0:T(8,128)S(1)}, f32[8,128]{1,0:T(8,128)S(1)}, f32[4,128,128]{2,1,0:T(8,128)S(1)}) custom-call(s32[2]{0:T(128)S(1)} %pad_add_fusion.place, f32[640,128]{1,0:T(8,128)S(1)} %bitcast.17, f32[8,128]{1,0:T(8,128)S(1)} %get-tuple-element.57.scalars, f32[2560,128]{1,0:T(8,128)} %get-tuple-element.58.last, ...), custom_call_target="tpu_custom_call" | custom-call | flops 4294967296 | bytes 16777216 | tf_op jit(solution)/shard_map/pallas_call | solution.py:356
  199.5 4.8 %all-to-all-start.4 = ((f32[128,1,512]{2,1,0:T(1,128)}), f32[128,1,512]{2,1,0:T(1,128)S(1)}, u32[]{:S(2)}, u32[]{:S(2)}) async-start(f32[128,1,512]{2,1,0:T(1,128)} %bitcast.9), calls=%async_computation.4 | async-start | bytes 524288 | tf_op jit(solution)/shard_map/all_to_all | solution.py:406
  204.3 1.1 slice.6.r0
  205.4 1.1 slice.7.r1
  206.5 1.6 shard_map.76
  208.7 6.4 %all-to-all-done.4 = f32[128,1,512]{2,1,0:T(1,128)S(1)} async-done(((f32[128,1,512]{2,1,0:T(1,128)}), f32[128,1,512]{2,1,0:T(1,128)S(1)}, u32[]{:S(2)}, u32[]{:S(2)}) %all-to-all-start.4) | async-done | bytes 262176 | tf_op jit(solution)/shard_map/all_to_all | solution.py:406
  216.0 1.2 shard_map.77
  (46 shorter events, 10.4 us)
Async XLA Ops:
  0.6 6.0 %copy-start = (f32[1024,128]{1,0:T(8,128)S(1)}, f32[1024,128]{1,0:T(8,128)}, u32[]{:S(2)}) copy-start(f32[1024,128]{1,0:T(8,128)} %basis.1) | copy-start | bytes 1572868
  0.6 7.7 %copy-start.9 = (f32[1024,128]{1,0:T(8,128)S(1)}, f32[1024,128]{1,0:T(8,128)}, u32[]{:S(2)}) copy-start(f32[1024,128]{1,0:T(8,128)} %right_own.1) | copy-start | bytes 1572868
  1.9 7.4 %collective-permute-start = (f32[768,128]{1,0:T(8,128)S(1)}, f32[768,128]{1,0:T(8,128)S(1)}, u32[]{:S(2)}, u32[]{:S(2)}) collective-permute-start(f32[768,128]{1,0:T(8,128)S(1)} %get-tuple-element.81), channel_id=1, source_target_pairs={{0,1},{1,0},{2,3},{3,2},{4,5},{5,4},{6,7},{7,6},{8,9},{9,8},{10,11... | collective-permute-start | bytes 1179656 | tf_op jit(solution)/shard_map/ppermute | solution.py:395
  3.4 9.1 %collective-permute-start.1 = (f32[768,128]{1,0:T(8,128)S(1)}, f32[768,128]{1,0:T(8,128)S(1)}, u32[]{:S(2)}, u32[]{:S(2)}) collective-permute-start(f32[768,128]{1,0:T(8,128)S(1)} %get-tuple-element.80), channel_id=1, source_target_pairs={{1,2},{3,4},{5,6},{7,8},{9,10},{11,12},{13,14},{15,16},{17,18},{19... | collective-permute-start | bytes 1179656 | tf_op jit(solution)/shard_map/ppermute | solution.py:394
  25.6 22.4 %collective-permute-start.2 = (f32[768,128]{1,0:T(8,128)}, f32[768,128]{1,0:T(8,128)S(1)}, u32[]{:S(2)}, u32[]{:S(2)}) collective-permute-start(f32[768,128]{1,0:T(8,128)} %get-tuple-element.42), channel_id=1, source_target_pairs={{0,1},{1,0},{2,3},{3,2},{4,5},{5,4},{6,7},{7,6},{8,9},{9,8},{10,11... | collective-permute-start | bytes 1179656 | tf_op jit(solution)/shard_map/ppermute | solution.py:395
  25.6 22.4 %collective-permute-start.3 = (f32[768,128]{1,0:T(8,128)}, f32[768,128]{1,0:T(8,128)S(1)}, u32[]{:S(2)}, u32[]{:S(2)}) collective-permute-start(f32[768,128]{1,0:T(8,128)} %get-tuple-element.43), channel_id=1, source_target_pairs={{1,2},{3,4},{5,6},{7,8},{9,10},{11,12},{13,14},{15,16},{17,18},{19... | collective-permute-start | bytes 1179656 | tf_op jit(solution)/shard_map/ppermute | solution.py:394
  29.3 25.5 %all-to-all-start = ((f32[128,1,384]{2,1,0:T(1,128)}), f32[128,1,384]{2,1,0:T(1,128)S(1)}, u32[]{:S(2)}, u32[]{:S(2)}) async-start(f32[128,1,384]{2,1,0:T(1,128)} %bitcast.1), calls=%async_computation | async-start | bytes 393216 | tf_op jit(solution)/shard_map/all_to_all | solution.py:406
  44.3 24.5 %collective-permute-start.4 = (f32[768,128]{1,0:T(8,128)}, f32[768,128]{1,0:T(8,128)S(1)}, u32[]{:S(2)}, u32[]{:S(2)}) collective-permute-start(f32[768,128]{1,0:T(8,128)} %get-tuple-element.79), channel_id=1, source_target_pairs={{0,1},{1,0},{2,3},{3,2},{4,5},{5,4},{6,7},{7,6},{8,9},{9,8},{10,11... | collective-permute-start | bytes 1179656 | tf_op jit(solution)/shard_map/ppermute | solution.py:395
  45.3 23.4 %collective-permute-start.5 = (f32[768,128]{1,0:T(8,128)}, f32[768,128]{1,0:T(8,128)S(1)}, u32[]{:S(2)}, u32[]{:S(2)}) collective-permute-start(f32[768,128]{1,0:T(8,128)} %get-tuple-element.78), channel_id=1, source_target_pairs={{1,2},{3,4},{5,6},{7,8},{9,10},{11,12},{13,14},{15,16},{17,18},{19... | collective-permute-start | bytes 1179656 | tf_op jit(solution)/shard_map/ppermute | solution.py:394
  48.0 0.7 copy-start.5
  48.7 1.0 copy-start.6
  51.3 16.5 %copy-start.2 = (f32[1024,128]{1,0:T(8,128)}, f32[1024,128]{1,0:T(8,128)S(1)}, u32[]{:S(2)}) copy-start(f32[1024,128]{1,0:T(8,128)S(1)} %get-tuple-element.44.image_own) | copy-start | bytes 1572868
  51.3 26.9 %collective-permute-start.6 = (f32[768,128]{1,0:T(8,128)}, f32[768,128]{1,0:T(8,128)S(1)}, u32[]{:S(2)}, u32[]{:S(2)}) collective-permute-start(f32[768,128]{1,0:T(8,128)} %get-tuple-element.45), channel_id=1, source_target_pairs={{0,1},{1,0},{2,3},{3,2},{4,5},{5,4},{6,7},{7,6},{8,9},{9,8},{10,11... | collective-permute-start | bytes 1179656 | tf_op jit(solution)/shard_map/ppermute | solution.py:395
  51.3 26.9 %collective-permute-start.7 = (f32[768,128]{1,0:T(8,128)}, f32[768,128]{1,0:T(8,128)S(1)}, u32[]{:S(2)}, u32[]{:S(2)}) collective-permute-start(f32[768,128]{1,0:T(8,128)} %get-tuple-element.46), channel_id=1, source_target_pairs={{1,2},{3,4},{5,6},{7,8},{9,10},{11,12},{13,14},{15,16},{17,18},{19... | collective-permute-start | bytes 1179656 | tf_op jit(solution)/shard_map/ppermute | solution.py:394
  55.5 22.7 %copy-start.3 = (f32[128,128]{1,0:T(8,128)S(1)}, f32[128,128]{1,0:T(8,128)}, u32[]{:S(2)}) copy-start(f32[128,128]{1,0:T(8,128)} %load.1) | copy-start | bytes 196612
  55.5 22.7 %all-to-all-start.1 = ((f32[128,1,384]{2,1,0:T(1,128)}), f32[128,1,384]{2,1,0:T(1,128)S(1)}, u32[]{:S(2)}, u32[]{:S(2)}) async-start(f32[128,1,384]{2,1,0:T(1,128)} %bitcast.3), calls=%async_computation.1 | async-start | bytes 393216 | tf_op jit(solution)/shard_map/all_to_all | solution.py:406
  98.2 2.7 %collective-permute-start.8 = (f32[768,128]{1,0:T(8,128)S(1)}, f32[768,128]{1,0:T(8,128)S(1)}, u32[]{:S(2)}, u32[]{:S(2)}) collective-permute-start(f32[768,128]{1,0:T(8,128)S(1)} %get-tuple-element.51), channel_id=1, source_target_pairs={{0,1},{1,0},{2,3},{3,2},{4,5},{5,4},{6,7},{7,6},{8,9},{9,8},{10,11... | collective-permute-start | bytes 1179656 | tf_op jit(solution)/shard_map/ppermute | solution.py:395
  98.9 9.1 %collective-permute-start.9 = (f32[768,128]{1,0:T(8,128)S(1)}, f32[768,128]{1,0:T(8,128)S(1)}, u32[]{:S(2)}, u32[]{:S(2)}) collective-permute-start(f32[768,128]{1,0:T(8,128)S(1)} %get-tuple-element.52), channel_id=1, source_target_pairs={{1,2},{3,4},{5,6},{7,8},{9,10},{11,12},{13,14},{15,16},{17,18},{19... | collective-permute-start | bytes 1179656 | tf_op jit(solution)/shard_map/ppermute | solution.py:394
  108.0 1.0 copy-start.4
  109.7 24.8 %collective-permute-start.10 = (f32[768,128]{1,0:T(8,128)S(1)}, f32[768,128]{1,0:T(8,128)S(1)}, u32[]{:S(2)}, u32[]{:S(2)}) collective-permute-start(f32[768,128]{1,0:T(8,128)S(1)} %get-tuple-element.54), channel_id=1, source_target_pairs={{0,1},{1,0},{2,3},{3,2},{4,5},{5,4},{6,7},{7,6},{8,9},{9,8},{10,11... | collective-permute-start | bytes 1179656 | tf_op jit(solution)/shard_map/ppermute | solution.py:395
  109.8 24.7 %collective-permute-start.11 = (f32[768,128]{1,0:T(8,128)S(1)}, f32[768,128]{1,0:T(8,128)S(1)}, u32[]{:S(2)}, u32[]{:S(2)}) collective-permute-start(f32[768,128]{1,0:T(8,128)S(1)} %get-tuple-element.55), channel_id=1, source_target_pairs={{1,2},{3,4},{5,6},{7,8},{9,10},{11,12},{13,14},{15,16},{17,18},{19... | collective-permute-start | bytes 1179656 | tf_op jit(solution)/shard_map/ppermute | solution.py:394
  149.4 3.0 %collective-permute-start.12 = (f32[768,128]{1,0:T(8,128)S(1)}, f32[768,128]{1,0:T(8,128)S(1)}, u32[]{:S(2)}, u32[]{:S(2)}) collective-permute-start(f32[768,128]{1,0:T(8,128)S(1)} %get-tuple-element.61), channel_id=1, source_target_pairs={{0,1},{1,0},{2,3},{3,2},{4,5},{5,4},{6,7},{7,6},{8,9},{9,8},{10,11... | collective-permute-start | bytes 1179656 | tf_op jit(solution)/shard_map/ppermute | solution.py:395
  150.5 9.1 %collective-permute-start.13 = (f32[768,128]{1,0:T(8,128)S(1)}, f32[768,128]{1,0:T(8,128)S(1)}, u32[]{:S(2)}, u32[]{:S(2)}) collective-permute-start(f32[768,128]{1,0:T(8,128)S(1)} %get-tuple-element.62), channel_id=1, source_target_pairs={{1,2},{3,4},{5,6},{7,8},{9,10},{11,12},{13,14},{15,16},{17,18},{19... | collective-permute-start | bytes 1179656 | tf_op jit(solution)/shard_map/ppermute | solution.py:394
  160.3 24.9 %collective-permute-start.14 = (f32[768,128]{1,0:T(8,128)S(1)}, f32[768,128]{1,0:T(8,128)S(1)}, u32[]{:S(2)}, u32[]{:S(2)}) collective-permute-start(f32[768,128]{1,0:T(8,128)S(1)} %get-tuple-element.64), channel_id=1, source_target_pairs={{0,1},{1,0},{2,3},{3,2},{4,5},{5,4},{6,7},{7,6},{8,9},{9,8},{10,11... | collective-permute-start | bytes 1179656 | tf_op jit(solution)/shard_map/ppermute | solution.py:395
  160.4 24.8 %collective-permute-start.15 = (f32[768,128]{1,0:T(8,128)S(1)}, f32[768,128]{1,0:T(8,128)S(1)}, u32[]{:S(2)}, u32[]{:S(2)}) collective-permute-start(f32[768,128]{1,0:T(8,128)S(1)} %get-tuple-element.65), channel_id=1, source_target_pairs={{1,2},{3,4},{5,6},{7,8},{9,10},{11,12},{13,14},{15,16},{17,18},{19... | collective-permute-start | bytes 1179656 | tf_op jit(solution)/shard_map/ppermute | solution.py:394
  199.5 7.0 %copy-start.1 = (f32[1024,128]{1,0:T(8,128)S(1)}, f32[1024,128]{1,0:T(8,128)}, u32[]{:S(2)}) copy-start(f32[1024,128]{1,0:T(8,128)} %basis.1) | copy-start | bytes 1572868
  199.5 15.6 %all-to-all-start.4 = ((f32[128,1,512]{2,1,0:T(1,128)}), f32[128,1,512]{2,1,0:T(1,128)S(1)}, u32[]{:S(2)}, u32[]{:S(2)}) async-start(f32[128,1,512]{2,1,0:T(1,128)} %bitcast.9), calls=%async_computation.4 | async-start | bytes 524288 | tf_op jit(solution)/shard_map/all_to_all | solution.py:406
  208.1 0.6 copy-start.7
  215.1 0.9 copy-start.8

commit v3 on v2

v3 whole, which is shorter than its diff:
```python
import functools

import jax
import jax.numpy as jnp
from jax import lax
from jax.experimental import pallas as pl
from jax.experimental.pallas import tpu as pltpu
from jax.sharding import Mesh
from jax.sharding import PartitionSpec as P

GX_GY = ("gx", "gy_0", "gy_1", "gy_2")
HIGHEST = lax.Precision.HIGHEST
F32 = jnp.float32
BF16 = jnp.bfloat16

SLAB = 1024
WINDOW = 2048
REACH = 768
SKIP = SLAB - REACH
HIGH = REACH + SLAB
EXT = SLAB + 2 * REACH
R = 128
DEVICES = 128
CHUNK = 512
STEPS = WINDOW // CHUNK
PIECES = 8
PIECE = WINDOW // PIECES
OWN = slice(REACH, HIGH)

MATRIX = jax.ShapeDtypeStruct((R, R), F32)
EXTENDED = jax.ShapeDtypeStruct((EXT, R), F32)


def full_dot(a, b):
    return jnp.dot(a, b, precision=HIGHEST, preferred_element_type=F32)


def contract_rows(a, b):
    return lax.dot_general(
        a, b, (((0,), (0,)), ((), ())), precision=HIGHEST, preferred_element_type=F32
    )


def split_bf16(x):
    high = x.astype(BF16)
    return high, (x - high.astype(F32)).astype(BF16)


def column_sum(a, b):
    return jnp.sum(a * b, axis=0, keepdims=True)


def part(arrived, index, count):
    return arrived[pl.ds(index, DEVICES, stride=count), :]


def total(arrived, index, count):
    return jnp.sum(part(arrived, index, count), axis=0, keepdims=True)


def put(joined, index, count, value):
    joined[pl.ds(index, DEVICES, stride=count), :] = jnp.broadcast_to(value, (DEVICES, R))


def sides(parity, scale):
    partner = pl.multiple_of(scale * (1 - parity), 8)
    remote = pl.multiple_of(scale * parity, 8)
    return pl.ds(partner, REACH), pl.ds(remote, REACH)


def assemble(ext, pieces, parity):
    own, partner, remote = pieces
    at_partner, at_remote = sides(parity, HIGH)
    ext[OWN, :] = own[...]
    ext[at_partner, :] = partner[...]
    ext[at_remote, :] = remote[...]


def invert(gram, inverse):
    row = lax.broadcasted_iota(jnp.int32, (R, R), 0)
    column = lax.broadcasted_iota(jnp.int32, (R, R), 1)
    identity = jnp.where(row == column, 1.0, 0.0).astype(F32)
    diagonal = gram * identity
    across = lax.rsqrt(jnp.sum(diagonal, axis=0, keepdims=True))
    along = lax.rsqrt(jnp.sum(diagonal, axis=1, keepdims=True))
    scaled = gram * across * along
    bound = jnp.max(jnp.sum(jnp.abs(scaled), axis=0, keepdims=True), axis=1, keepdims=True)
    inverse[...] = identity / bound

    def refine():
        current = inverse[...]
        rest = identity - full_dot(scaled, current)
        inverse[...] = current + full_dot(current, rest)
        return jnp.max(jnp.abs(rest))

    def body(carry):
        return carry[0] + 1, refine()

    lax.while_loop(lambda c: (c[0] < 60) & (c[1] > 1e-3), body, (jnp.int32(0), jnp.float32(1.0)))
    refine()
    inverse[...] = inverse[...] * across * along


def packed(x):
    return jnp.concatenate(split_bf16(x), axis=1)


def close_dot(x, m):
    high, low = split_bf16(m)
    upper = jnp.concatenate([high, low], axis=1)
    lower = jnp.concatenate([high, jnp.zeros_like(high)], axis=1)
    out = jnp.dot(packed(x), jnp.concatenate([upper, lower], axis=0), preferred_element_type=F32)
    return out[:, :R] + out[:, R:]


def close_contract(x, y):
    out = lax.dot_general(
        packed(x), packed(y), (((0,), (0,)), ((), ())), preferred_element_type=F32
    )
    return (out[:R, :R] + out[R:, R:]) + (out[:R, R:] + out[R:, :R])


def piece_of(schur, buffer, arrivals, index):
    rows = pl.ds(pl.multiple_of(index * PIECE, PIECE), PIECE)
    return pltpu.make_async_copy(schur.at[0, rows, :], buffer.at[rows, :], arrivals.at[index])


def fetch(schur, buffer, arrivals):
    for index in range(PIECES):
        piece_of(schur, buffer, arrivals, index).start()


def multiply(start, ext, schur, buffer, arrivals, halves, use):
    high, low = split_bf16(ext[pl.ds(start, WINDOW), :])
    halves[:, :R] = high
    halves[:, R:] = low

    def body(step, carry):
        for index in range(PIECES // STEPS):
            piece_of(schur, buffer, arrivals, step * (PIECES // STEPS) + index).wait()
        at = pl.multiple_of(step * CHUNK, CHUNK)
        high, low = split_bf16(buffer[pl.ds(at, CHUNK), :])
        both = jnp.dot(high, halves[...], preferred_element_type=F32)
        rest = jnp.dot(low, halves[:, :R], preferred_element_type=F32)
        use(pl.ds(start + at, CHUNK), both[:, :R] + both[:, R:] + rest)
        return carry

    lax.fori_loop(0, STEPS, body, 0)


def add_form(form, ext, rows, product):
    form[...] += jnp.sum((ext[rows, :] * product).reshape(CHUNK // 8, 8, R), axis=0)


def clear(form, cross, image):
    form[...] = jnp.zeros_like(form)
    cross[...] = jnp.zeros_like(cross)
    image[: EXT - WINDOW, :] = jnp.zeros((EXT - WINDOW, R), F32)
    image[WINDOW:, :] = jnp.zeros((EXT - WINDOW, R), F32)


def deliver(image, parity, own, partner, remote):
    at_partner, at_remote = sides(parity, HIGH)
    own[...] = image[OWN, :]
    partner[...] = image[at_partner, :]
    remote[...] = image[at_remote, :]


def first_kernel(
    place, own, partner, remote, gram, coarse, schur,
    out_own, out_partner, out_remote, joined,
    buffer, arrivals, halves, ext, image, form, cross,
):
    start, parity = place[0] - SKIP, place[1]
    fetch(schur, buffer, arrivals)
    assemble(ext, (own, partner, remote), parity)
    clear(form, cross, image)
    put(joined, 0, 3, gram[...])
    put(joined, 1, 3, coarse[...])

    def use(rows, product):
        cross[...] += close_contract(ext[rows, :], product)
        image[rows, :] = product

    multiply(start, ext, schur, buffer, arrivals, halves, use)
    deliver(image, parity, out_own, out_partner, out_remote)
    put(joined, 2, 3, cross[...])


def start_kernel(
    place, arrived, load, square,
    right_own, right_partner, right_remote,
    basis_own, basis_partner, basis_remote,
    image_own, image_partner, image_remote, schur,
    out_own, out_partner, out_remote, joined,
    residual, z_ext, new_own, inverse, first, amp, stiff,
    buffer, arrivals, halves, image, form, cross,
):
    start, parity = place[0] - SKIP, place[1]
    fetch(schur, buffer, arrivals)
    invert(part(arrived, 0, 3), inverse)
    stiff[...] = part(arrived, 2, 3)
    first[...] = full_dot(inverse[...], load[...])
    amp[...] = full_dot(inverse[...], part(arrived, 1, 3) - full_dot(stiff[...], first[...]))
    assemble(z_ext, (image_own, image_partner, image_remote), parity)
    assemble(image, (basis_own, basis_partner, basis_remote), parity)
    assemble(residual, (right_own, right_partner, right_remote), parity)
    residual[...] = (
        residual[...] - close_dot(z_ext[...], first[...]) - close_dot(image[...], amp[...])
    )
    clear(form, cross, image)
    own = residual[OWN, :]
    new_own[...] = own
    put(joined, 0, 5, column_sum(own, own))
    put(joined, 4, 5, square[...])
    put(joined, 2, 5, close_contract(image_own[...], own))

    def use(rows, product):
        add_form(form, residual, rows, product)
        cross[...] += close_contract(z_ext[rows, :], product)
        image[rows, :] = product

    multiply(start, residual, schur, buffer, arrivals, halves, use)
    deliver(image, parity, out_own, out_partner, out_remote)
    put(joined, 1, 5, jnp.sum(form[...], axis=0, keepdims=True))
    put(joined, 3, 5, cross[...])


def middle_kernel(
    place, arrived, last, z_ext, own, partner, remote, schur,
    out_own, out_partner, out_remote, joined, residual, w_ext, new_own, scalars,
    buffer, arrivals, halves, image, form, cross,
):
    start, parity = place[0] - SKIP, place[1]
    fetch(schur, buffer, arrivals)
    energy = total(arrived, 0, 5)
    length = energy / total(arrived, 1, 5)
    assemble(w_ext, (own, partner, remote), parity)
    residual[...] = last[...] - length * w_ext[...]
    clear(form, cross, image)
    mine = residual[OWN, :]
    new_own[...] = mine
    put(joined, 0, 5, column_sum(mine, mine))
    put(joined, 2, 5, total(arrived, 2, 5))
    put(joined, 3, 5, total(arrived, 3, 5))
    scalars[...] = jnp.zeros_like(scalars)
    scalars[0:1, :] = energy
    scalars[1:2, :] = length
    scalars[2:3, :] = total(arrived, 4, 5)

    def use(rows, product):
        add_form(form, residual, rows, product)
        cross[...] += close_contract(z_ext[rows, :], product)
        image[rows, :] = product

    multiply(start, residual, schur, buffer, arrivals, halves, use)
    deliver(image, parity, out_own, out_partner, out_remote)
    put(joined, 1, 5, jnp.sum(form[...], axis=0, keepdims=True))
    put(joined, 4, 5, cross[...])


def last_kernel(
    place, arrived, scalars, last, w_last, z_ext, own, partner, remote, inverse, stiff, schur,
    joined, new_own, numbers, matrices,
    buffer, arrivals, halves, residual, form, w_ext,
):
    start, parity = place[0] - SKIP, place[1]
    fetch(schur, buffer, arrivals)
    energy0, length0 = scalars[0:1, :], scalars[1:2, :]
    e0, f0 = part(arrived, 2, 5), part(arrived, 3, 5)
    c1 = -length0 * e0
    a1 = full_dot(inverse[...], c1)
    e1 = e0 - length0 * f0
    energy1 = total(arrived, 0, 5) - column_sum(c1, a1)
    stiff_a1 = full_dot(stiff[...], a1)
    ratio0 = energy1 / energy0
    curve1 = (
        total(arrived, 1, 5)
        - 2.0 * column_sum(a1, e1)
        + column_sum(a1, stiff_a1)
        - ratio0 * energy1 / length0
    )
    length1 = energy1 / curve1
    assemble(w_ext, (own, partner, remote), parity)
    residual[...] = last[...] - length1 * (
        w_ext[...] - close_dot(z_ext[...], a1) + ratio0 * w_last[...]
    )
    mine = residual[OWN, :]
    new_own[...] = mine
    put(joined, 0, 4, column_sum(mine, mine))
    put(joined, 2, 4, total(arrived, 4, 5))
    put(joined, 3, 4, scalars[2:3, :])
    numbers[...] = jnp.zeros_like(numbers)
    numbers[0:1, :] = length0
    numbers[1:2, :] = length1
    numbers[2:3, :] = ratio0
    numbers[3:4, :] = energy1
    d_coarse = e1 - stiff_a1 + ratio0 * e0
    matrices[0] = a1
    matrices[1] = c1 - length1 * d_coarse
    matrices[2] = d_coarse
    matrices[3] = e1 - length1 * ratio0 * f0
    form[...] = jnp.zeros_like(form)

    def use(rows, product):
        add_form(form, residual, rows, product)

    multiply(start, residual, schur, buffer, arrivals, halves, use)
    put(joined, 1, 4, jnp.sum(form[...], axis=0, keepdims=True))


def direction_kernel(
    numbers, matrices, inverse, stiff, first, basis, r0, r1, r2,
    base, d1, p2, small,
):
    length0, length1, ratio0 = numbers[0:1, :], numbers[1:2, :], numbers[2:3, :]
    a1 = matrices[0]
    a2 = full_dot(inverse[...], matrices[1])
    d1[...] = r1[...] - full_dot(basis[...], a1) + ratio0 * r0[...]
    p2[...] = r2[...] - full_dot(basis[...], a2)
    base[...] = full_dot(basis[...], first[...]) + length0 * r0[...] + length1 * d1[...]
    small[0] = a2
    small[1] = full_dot(stiff[...], a2)


def final_kernel(
    arrived, numbers, matrices, small, inverse, amp, base, d1, p2,
    multipliers, amplitudes,
):
    length1, energy1 = numbers[1:2, :], numbers[3:4, :]
    a2, stiff_a2 = small[0], small[1]
    f1, square = part(arrived, 2, 4), part(arrived, 3, 4)
    e2 = matrices[3] - length1 * (f1 - full_dot(square, matrices[0]))
    energy2 = total(arrived, 0, 4) - column_sum(matrices[1], a2)
    ratio1 = energy2 / energy1
    curve2 = (
        total(arrived, 1, 4)
        - 2.0 * column_sum(a2, e2)
        + column_sum(a2, stiff_a2)
        - ratio1 * energy2 / length1
    )
    length2 = energy2 / curve2
    multipliers[...] = base[...] + length2 * (p2[...] + ratio1 * d1[...])
    c3 = matrices[1] - length2 * (e2 - stiff_a2 + ratio1 * matrices[2])
    amplitudes[...] = amp[...] + full_dot(inverse[...], c3)


def sum_kernel(place, own, partner, remote, total_own, to_partner, to_remote):
    at_partner, at_remote = sides(place[1], SKIP)
    total_own[...] = own[...]
    total_own[at_partner, :] += partner[...]
    total_own[at_remote, :] += remote[...]
    to_partner[...] = total_own[at_partner, :]
    to_remote[...] = total_own[at_remote, :]


def turn_kernel(arrived, joined, *, count):
    for i in range(count):
        put(joined, i, count, total(arrived, i, count))


def shape(rows):
    return jax.ShapeDtypeStruct((rows, R), F32)


def operator(kernel, place, arrays, schur, outs, scratch):
    vmem = pl.BlockSpec(memory_space=pltpu.VMEM)
    return pl.pallas_call(
        kernel,
        in_specs=[pl.BlockSpec(memory_space=pltpu.SMEM)]
        + [vmem] * len(arrays)
        + [pl.BlockSpec(memory_space=pl.ANY)],
        out_specs=[vmem] * len(outs),
        out_shape=outs,
        scratch_shapes=[
            pltpu.VMEM((WINDOW, WINDOW), F32),
            pltpu.SemaphoreType.DMA((PIECES,)),
            pltpu.VMEM((WINDOW, 2 * R), BF16),
        ]
        + scratch,
        compiler_params=pltpu.CompilerParams(vmem_limit_bytes=50 << 20),
        cost_estimate=pl.CostEstimate(
            flops=8 * WINDOW * WINDOW * R, bytes_accessed=4 * WINDOW * WINDOW, transcendentals=0
        ),
    )(place, *arrays, schur)


def small_call(kernel, arrays, outs, place=None):
    head = [] if place is None else [place]
    return pl.pallas_call(
        kernel,
        in_specs=[pl.BlockSpec(memory_space=pltpu.SMEM)] * len(head)
        + [pl.BlockSpec(memory_space=pltpu.VMEM)] * len(arrays),
        out_specs=[pl.BlockSpec(memory_space=pltpu.VMEM)] * len(outs),
        out_shape=outs,
        compiler_params=pltpu.CompilerParams(vmem_limit_bytes=24 << 20),
        cost_estimate=pl.CostEstimate(
            flops=1 << 30, bytes_accessed=1 << 22, transcendentals=0
        ),
    )(*head, *arrays)


REMOTE = [(i, i + 1) for i in range(1, DEVICES - 1, 2)]
REMOTE = REMOTE + [(b, a) for a, b in REMOTE]


def swapped(to_partner, to_remote):
    remote = lax.ppermute(to_remote, GX_GY, REMOTE)
    partner = lax.ppermute(to_partner, "gy_2", [(0, 1), (1, 0)])
    return partner, remote


def halves_of(own, parity):
    at = SKIP * (1 - parity), SKIP * parity
    return [lax.dynamic_slice_in_dim(own, a, REACH, 0) for a in at]


def exchange(joined, count):
    sent = joined.reshape(DEVICES, 1, count * R)
    arrived = lax.all_to_all(sent, GX_GY, 0, 0, tiled=True)
    return arrived.reshape(DEVICES * count, R)


def summed(ends, place):
    own, *rest = ends
    arrived = swapped(*rest)
    own, *rest = small_call(
        sum_kernel, (own, *arrived), [shape(SLAB), shape(REACH), shape(REACH)], place
    )
    return own, *swapped(*rest)


def local(schur, offsets, right_side, basis, load):
    parity = lax.axis_index("gy_2").astype(jnp.int32)
    place = jnp.concatenate([offsets, parity[None]])
    ends = [shape(SLAB), shape(REACH), shape(REACH)]
    ext = pltpu.VMEM((EXT, R), F32)
    rows = pltpu.VMEM((8, R), F32)
    square = pltpu.VMEM((R, R), F32)

    basis_sides = swapped(*halves_of(basis, parity))
    right_sides = swapped(*halves_of(right_side, parity))
    gram, coarse = contract_rows(basis, basis), contract_rows(basis, right_side)
    *image, joined = operator(
        first_kernel, place, (basis, *basis_sides, gram, coarse), schur,
        ends + [shape(3 * DEVICES)], [ext, ext, rows, square],
    )
    arrived = exchange(joined, 3)
    image = summed(image, place)
    (joined,) = small_call(
        functools.partial(turn_kernel, count=3), (arrived,), [shape(3 * DEVICES)]
    )
    arrived = exchange(joined, 3)

    *w0, joined, r0_ext, z_ext, r0, inverse, first, amp, stiff = operator(
        start_kernel, place,
        (
            arrived, load, contract_rows(image[0], image[0]),
            right_side, *right_sides, basis, *basis_sides, *image,
        ),
        schur,
        ends + [shape(5 * DEVICES), EXTENDED, EXTENDED, shape(SLAB)] + [MATRIX] * 4,
        [ext, rows, square],
    )
    arrived = exchange(joined, 5)
    w0 = summed(w0, place)

    *w1, joined, r1_ext, w0_ext, r1, scalars = operator(
        middle_kernel, place, (arrived, r0_ext, z_ext, *w0), schur,
        ends + [shape(5 * DEVICES), EXTENDED, EXTENDED, shape(SLAB), shape(8)],
        [ext, rows, square],
    )
    arrived = exchange(joined, 5)
    w1 = summed(w1, place)

    joined, r2, numbers, matrices = operator(
        last_kernel, place,
        (arrived, scalars, r1_ext, w0_ext, z_ext, *w1, inverse, stiff),
        schur,
        [shape(4 * DEVICES), shape(SLAB), shape(8), jax.ShapeDtypeStruct((4, R, R), F32)],
        [ext, rows, ext],
    )
    arrived = exchange(joined, 4)
    base, d1, p2, small = small_call(
        direction_kernel,
        (numbers, matrices, inverse, stiff, first, basis, r0, r1, r2),
        [shape(SLAB)] * 3 + [jax.ShapeDtypeStruct((2, R, R), F32)],
    )
    return tuple(
        small_call(
            final_kernel,
            (arrived, numbers, matrices, small, inverse, amp, base, d1, p2),
            [shape(SLAB), MATRIX],
        )
    )


def solution(mesh):
    split = Mesh(mesh.devices.reshape(mesh.shape["gx"], 4, 4, 2), GX_GY)
    in_specs = (P(GX_GY, None, None), P(GX_GY), P(GX_GY, None), P(GX_GY, None), P())
    out_specs = (P(GX_GY, None), P())
    return jax.shard_map(local, mesh=split, in_specs=in_specs, out_specs=out_specs, check_vma=False)
```

time: 218 us -> 201 us (0.922)
  Pallas kernels: 68.8 us -> 50.2 us
    pallas_call x4, Pallas kernels: 62.3 us -> 43.7 us  [operator(): pl.pallas_call(kernel, in_specs=[pl.BlockSpec(memory_space=pltpu.SMEM)] +...]
    unnamed x20 -> x30, local copies, waits for them, and re-layouts: 4.34 us -> 8.03 us
  transfers between devices with their start and end apart: 19 -> 19, of which waited for: 5 -> 5; matrix products, arithmetic and copies ran while one was open for 3% -> 2% of each run, Pallas kernels for 2% -> 2%
where the time goes in v3:
time: 201 us; the launch traced here: 200 us
  starting transfers between devices  57.3 us (29%)
  Pallas kernels  50.2 us (25%)
  blocking collectives  44.8 us (22%)
  waiting for transfers between devices  33.2 us (17%)
  local copies, waits for them, and re-layouts  10.2 us (5%)
  matrix products  3.01 us (1%)
    all_to_all x2, blocking collectives, exchange(): arrived = lax.all_to_all(sent, GX_GY, 0, 0, tiled=True)  44.8 us
    pallas_call x4, Pallas kernels, operator(): pl.pallas_call(kernel, in_specs=[pl.BlockSpec(memory_space=pltpu.SMEM)] +...  43.7 us
    all_to_all x3, starting transfers between devices, exchange(): arrived = lax.all_to_all(sent, GX_GY, 0, 0, tiled=True)  31.1 us
    ppermute x8, starting transfers between devices, swapped(): remote = lax.ppermute(to_remote, GX_GY, REMOTE)  23.3 us
    ppermute x8, waiting for transfers between devices, swapped(): remote = lax.ppermute(to_remote, GX_GY, REMOTE)  16.9 us
    all_to_all x3, waiting for transfers between devices, exchange(): arrived = lax.all_to_all(sent, GX_GY, 0, 0, tiled=True)  16.3 us
    unnamed x30, local copies, waits for them, and re-layouts  8.03 us
    pallas_call x6, Pallas kernels, small_call(): pl.pallas_call(kernel, in_specs=[pl.BlockSpec(memory_space=pltpu.SMEM)] *...  6.47 us
  transfers between devices with their start and end apart: 19, of which 5 were waited for; matrix products, arithmetic and copies ran while one was open for 2% of the time, Pallas kernels for 2%

profile of v3, /device:TPU:1, one launch (start us, length us, event | category | flops | bytes accessed | tf_op | source)
XLA Modules:
  0.0 200.5 jit_solution(16945145660361690077)
XLA Ops:
  0.7 1.3 constant_dynamic-slice_fusion.2
  1.9 4.6 %collective-permute-start.1 = (f32[768,128]{1,0:T(8,128)S(1)}, f32[768,128]{1,0:T(8,128)S(1)}, u32[]{:S(2)}, u32[]{:S(2)}) collective-permute-start(f32[768,128]{1,0:T(8,128)S(1)} %get-tuple-element.84), channel_id=1, source_target_pairs={{1,2},{3,4},{5,6},{7,8},{9,10},{11,12},{13,14},{15,16},{17,18},{19... | collective-permute-start | bytes 1179656 | tf_op jit(solution)/shard_map/ppermute | solution.py:408
  6.6 1.0 fusion.gram
  9.4 2.6 %collective-permute-done.1.remote.basis_remote = f32[768,128]{1,0:T(8,128)S(1)} collective-permute-done((f32[768,128]{1,0:T(8,128)S(1)}, f32[768,128]{1,0:T(8,128)S(1)}, u32[]{:S(2)}, u32[]{:S(2)}) %collective-permute-start.1) | collective-permute-done | bytes 393248 | tf_op jit(solution)/shard_map/ppermute | solution.py:408
  12.0 10.0 %shard_map.68 = (f32[1024,128]{1,0:T(8,128)S(1)}, f32[768,128]{1,0:T(8,128)}, f32[768,128]{1,0:T(8,128)}, f32[384,128]{1,0:T(8,128)}) custom-call(s32[2]{0:T(128)S(1)} %pad_add_fusion.place, f32[1024,128]{1,0:T(8,128)S(1)} %copy-done, f32[768,128]{1,0:T(8,128)S(1)} %collective-permute-done.partner.basis_partner, ...), custom_call_target="tpu_custom_call" | custom-call | flops 4294967296 | bytes 16777216 | tf_op jit(solution)/shard_map/pallas_call | solution.py:368
  22.1 3.7 %collective-permute-start.3 = (f32[768,128]{1,0:T(8,128)}, f32[768,128]{1,0:T(8,128)S(1)}, u32[]{:S(2)}, u32[]{:S(2)}) collective-permute-start(f32[768,128]{1,0:T(8,128)} %get-tuple-element.45), channel_id=1, source_target_pairs={{1,2},{3,4},{5,6},{7,8},{9,10},{11,12},{13,14},{15,16},{17,18},{19... | collective-permute-start | bytes 1179656 | tf_op jit(solution)/shard_map/ppermute | solution.py:408
  25.7 13.8 %all-to-all-start = ((f32[128,1,384]{2,1,0:T(1,128)}), f32[128,1,384]{2,1,0:T(1,128)S(1)}, u32[]{:S(2)}, u32[]{:S(2)}) async-start(f32[128,1,384]{2,1,0:T(1,128)} %bitcast.1), calls=%async_computation | async-start | bytes 393216 | tf_op jit(solution)/shard_map/all_to_all | solution.py:420
  40.5 3.5 %collective-permute-start.5 = (f32[768,128]{1,0:T(8,128)}, f32[768,128]{1,0:T(8,128)S(1)}, u32[]{:S(2)}, u32[]{:S(2)}) collective-permute-start(f32[768,128]{1,0:T(8,128)} %get-tuple-element.82), channel_id=1, source_target_pairs={{1,2},{3,4},{5,6},{7,8},{9,10},{11,12},{13,14},{15,16},{17,18},{19... | collective-permute-start | bytes 1179656 | tf_op jit(solution)/shard_map/ppermute | solution.py:408
  45.9 1.6 shard_map.70
  47.9 3.0 %collective-permute-start.7 = (f32[768,128]{1,0:T(8,128)}, f32[768,128]{1,0:T(8,128)S(1)}, u32[]{:S(2)}, u32[]{:S(2)}) collective-permute-start(f32[768,128]{1,0:T(8,128)} %get-tuple-element.48), channel_id=1, source_target_pairs={{1,2},{3,4},{5,6},{7,8},{9,10},{11,12},{13,14},{15,16},{17,18},{19... | collective-permute-start | bytes 1179656 | tf_op jit(solution)/shard_map/ppermute | solution.py:408
  51.6 12.5 %all-to-all-start.1 = ((f32[128,1,384]{2,1,0:T(1,128)}), f32[128,1,384]{2,1,0:T(1,128)S(1)}, u32[]{:S(2)}, u32[]{:S(2)}) async-start(f32[128,1,384]{2,1,0:T(1,128)} %bitcast.3), calls=%async_computation.1 | async-start | bytes 393216 | tf_op jit(solution)/shard_map/all_to_all | solution.py:420
  64.1 1.0 fusion.2.square
  65.2 9.3 %all-to-all-done.1 = f32[128,1,384]{2,1,0:T(1,128)S(1)} async-done(((f32[128,1,384]{2,1,0:T(1,128)}), f32[128,1,384]{2,1,0:T(1,128)S(1)}, u32[]{:S(2)}, u32[]{:S(2)}) %all-to-all-start.1) | async-done | bytes 196640 | tf_op jit(solution)/shard_map/all_to_all | solution.py:420
  74.5 12.9 %shard_map.71 = (f32[1024,128]{1,0:T(8,128)}, f32[768,128]{1,0:T(8,128)S(1)}, f32[768,128]{1,0:T(8,128)S(1)}, f32[640,128]{1,0:T(8,128)S(1)}, f32[2560,128]{1,0:...) custom-call(s32[2]{0:T(128)S(1)} %pad_add_fusion.place, ...), custom_call_target="tpu_custom_call" | custom-call | flops 4294967296 | bytes 16777216 | tf_op jit(solution)/shard_map/pallas_call | solution.py:368
  88.2 1.9 collective-permute-start.9
  90.2 7.1 %collective-permute-done.9.remote = f32[768,128]{1,0:T(8,128)S(1)} collective-permute-done((f32[768,128]{1,0:T(8,128)S(1)}, f32[768,128]{1,0:T(8,128)S(1)}, u32[]{:S(2)}, u32[]{:S(2)}) %collective-permute-start.9) | collective-permute-done | bytes 393248 | tf_op jit(solution)/shard_map/ppermute | solution.py:408
  97.3 1.0 copy-done.5
  99.2 2.4 %collective-permute-start.11 = (f32[768,128]{1,0:T(8,128)S(1)}, f32[768,128]{1,0:T(8,128)S(1)}, u32[]{:S(2)}, u32[]{:S(2)}) collective-permute-start(f32[768,128]{1,0:T(8,128)S(1)} %get-tuple-element.57), channel_id=1, source_target_pairs={{1,2},{3,4},{5,6},{7,8},{9,10},{11,12},{13,14},{15,16},{17,18},{19... | collective-permute-start | bytes 1179656 | tf_op jit(solution)/shard_map/ppermute | solution.py:408
  101.6 22.3 %all_to_all.25 = f32[128,1,640]{2,1,0:T(1,128)S(1)} all-to-all(f32[128,1,640]{2,1,0:T(1,128)S(1)} %bitcast.20), channel_id=1, replica_groups=mesh['gx'=4,'gy_0'=4,'gy_1'=4,'gy_2'=2] {'gx','gy_0','gy_1','gy_2'}, dimensions={0} | all-to-all | bytes 655360 | tf_op jit(solution)/shard_map/all_to_all | solution.py:420
  123.9 10.3 %shard_map.73 = (f32[1024,128]{1,0:T(8,128)S(1)}, f32[768,128]{1,0:T(8,128)S(1)}, f32[768,128]{1,0:T(8,128)S(1)}, f32[640,128]{1,0:T(8,128)S(1)}, f32[2560,128]{...) custom-call(s32[2]{0:T(128)S(1)} %pad_add_fusion.place, ...), custom_call_target="tpu_custom_call" | custom-call | flops 4294967296 | bytes 16777216 | tf_op jit(solution)/shard_map/pallas_call | solution.py:368
  134.2 1.2 collective-permute-start.12
  135.4 1.9 collective-permute-start.13
  137.3 7.2 %collective-permute-done.13.remote = f32[768,128]{1,0:T(8,128)S(1)} collective-permute-done((f32[768,128]{1,0:T(8,128)S(1)}, f32[768,128]{1,0:T(8,128)S(1)}, u32[]{:S(2)}, u32[]{:S(2)}) %collective-permute-start.13) | collective-permute-done | bytes 393248 | tf_op jit(solution)/shard_map/ppermute | solution.py:408
  145.2 2.3 %collective-permute-start.15 = (f32[768,128]{1,0:T(8,128)S(1)}, f32[768,128]{1,0:T(8,128)S(1)}, u32[]{:S(2)}, u32[]{:S(2)}) collective-permute-start(f32[768,128]{1,0:T(8,128)S(1)} %get-tuple-element.67), channel_id=1, source_target_pairs={{1,2},{3,4},{5,6},{7,8},{9,10},{11,12},{13,14},{15,16},{17,18},{19... | collective-permute-start | bytes 1179656 | tf_op jit(solution)/shard_map/ppermute | solution.py:408
  147.5 22.5 %all_to_all.26 = f32[128,1,640]{2,1,0:T(1,128)S(1)} all-to-all(f32[128,1,640]{2,1,0:T(1,128)S(1)} %bitcast.21), channel_id=1, replica_groups=mesh['gx'=4,'gy_0'=4,'gy_1'=4,'gy_2'=2] {'gx','gy_0','gy_1','gy_2'}, dimensions={0} | all-to-all | bytes 655360 | tf_op jit(solution)/shard_map/all_to_all | solution.py:420
  170.1 10.5 %shard_map.75 = (f32[512,128]{1,0:T(8,128)}, f32[1024,128]{1,0:T(8,128)S(1)}, f32[8,128]{1,0:T(8,128)S(1)}, f32[4,128,128]{2,1,0:T(8,128)S(1)}) custom-call(s32[2]{0:T(128)S(1)} %pad_add_fusion.place, f32[640,128]{1,0:T(8,128)S(1)} %bitcast.18, f32[8,128]{1,0:T(8,128)S(1)} %get-tuple-element.59.scalars, f32[2560,128]{1,0:T(8,128)} %get-tuple-element.60.last, ...), custom_call_target="tpu_custom_call" | custom-call | flops 4294967296 | bytes 16777216 | tf_op jit(solution)/shard_map/pallas_call | solution.py:368
  180.6 4.8 %all-to-all-start.4 = ((f32[128,1,512]{2,1,0:T(1,128)}), f32[128,1,512]{2,1,0:T(1,128)S(1)}, u32[]{:S(2)}, u32[]{:S(2)}) async-start(f32[128,1,512]{2,1,0:T(1,128)} %bitcast.9), calls=%async_computation.4 | async-start | bytes 524288 | tf_op jit(solution)/shard_map/all_to_all | solution.py:420
  185.4 1.5 shard_map.76
  189.3 7.0 %all-to-all-done.4 = f32[128,1,512]{2,1,0:T(1,128)S(1)} async-done(((f32[128,1,512]{2,1,0:T(1,128)}), f32[128,1,512]{2,1,0:T(1,128)S(1)}, u32[]{:S(2)}, u32[]{:S(2)}) %all-to-all-start.4) | async-done | bytes 262176 | tf_op jit(solution)/shard_map/all_to_all | solution.py:420
  196.2 1.0 copy-done.9
  197.3 1.0 copy-done.11
  199.2 1.2 shard_map.77
  (54 shorter events, 10.8 us)
Async XLA Ops:
  0.6 6.0 %copy-start = (f32[1024,128]{1,0:T(8,128)S(1)}, f32[1024,128]{1,0:T(8,128)}, u32[]{:S(2)}) copy-start(f32[1024,128]{1,0:T(8,128)} %basis.1) | copy-start | bytes 1572868
  0.6 7.7 %copy-start.14 = (f32[1024,128]{1,0:T(8,128)S(1)}, f32[1024,128]{1,0:T(8,128)}, u32[]{:S(2)}) copy-start(f32[1024,128]{1,0:T(8,128)} %right_own.1) | copy-start | bytes 1572868
  1.9 10.0 %collective-permute-start.1 = (f32[768,128]{1,0:T(8,128)S(1)}, f32[768,128]{1,0:T(8,128)S(1)}, u32[]{:S(2)}, u32[]{:S(2)}) collective-permute-start(f32[768,128]{1,0:T(8,128)S(1)} %get-tuple-element.84), channel_id=1, source_target_pairs={{1,2},{3,4},{5,6},{7,8},{9,10},{11,12},{13,14},{15,16},{17,18},{19... | collective-permute-start | bytes 1179656 | tf_op jit(solution)/shard_map/ppermute | solution.py:408
  6.5 5.4 %collective-permute-start = (f32[768,128]{1,0:T(8,128)S(1)}, f32[768,128]{1,0:T(8,128)S(1)}, u32[]{:S(2)}, u32[]{:S(2)}) collective-permute-start(f32[768,128]{1,0:T(8,128)S(1)} %get-tuple-element.85), channel_id=1, source_target_pairs={{0,1},{1,0},{2,3},{3,2},{4,5},{5,4},{6,7},{7,6},{8,9},{9,8},{10,11... | collective-permute-start | bytes 1179656 | tf_op jit(solution)/shard_map/ppermute | solution.py:409
  22.0 22.1 %collective-permute-start.2 = (f32[768,128]{1,0:T(8,128)}, f32[768,128]{1,0:T(8,128)S(1)}, u32[]{:S(2)}, u32[]{:S(2)}) collective-permute-start(f32[768,128]{1,0:T(8,128)} %get-tuple-element.44), channel_id=1, source_target_pairs={{0,1},{1,0},{2,3},{3,2},{4,5},{5,4},{6,7},{7,6},{8,9},{9,8},{10,11... | collective-permute-start | bytes 1179656 | tf_op jit(solution)/shard_map/ppermute | solution.py:409
  22.1 22.0 %collective-permute-start.3 = (f32[768,128]{1,0:T(8,128)}, f32[768,128]{1,0:T(8,128)S(1)}, u32[]{:S(2)}, u32[]{:S(2)}) collective-permute-start(f32[768,128]{1,0:T(8,128)} %get-tuple-element.45), channel_id=1, source_target_pairs={{1,2},{3,4},{5,6},{7,8},{9,10},{11,12},{13,14},{15,16},{17,18},{19... | collective-permute-start | bytes 1179656 | tf_op jit(solution)/shard_map/ppermute | solution.py:408
  25.7 25.2 %all-to-all-start = ((f32[128,1,384]{2,1,0:T(1,128)}), f32[128,1,384]{2,1,0:T(1,128)S(1)}, u32[]{:S(2)}, u32[]{:S(2)}) async-start(f32[128,1,384]{2,1,0:T(1,128)} %bitcast.1), calls=%async_computation | async-start | bytes 393216 | tf_op jit(solution)/shard_map/all_to_all | solution.py:420
  40.5 24.7 %collective-permute-start.5 = (f32[768,128]{1,0:T(8,128)}, f32[768,128]{1,0:T(8,128)S(1)}, u32[]{:S(2)}, u32[]{:S(2)}) collective-permute-start(f32[768,128]{1,0:T(8,128)} %get-tuple-element.82), channel_id=1, source_target_pairs={{1,2},{3,4},{5,6},{7,8},{9,10},{11,12},{13,14},{15,16},{17,18},{19... | collective-permute-start | bytes 1179656 | tf_op jit(solution)/shard_map/ppermute | solution.py:408
  44.0 21.2 %collective-permute-start.4 = (f32[768,128]{1,0:T(8,128)}, f32[768,128]{1,0:T(8,128)S(1)}, u32[]{:S(2)}, u32[]{:S(2)}) collective-permute-start(f32[768,128]{1,0:T(8,128)} %get-tuple-element.83), channel_id=1, source_target_pairs={{0,1},{1,0},{2,3},{3,2},{4,5},{5,4},{6,7},{7,6},{8,9},{9,8},{10,11... | collective-permute-start | bytes 1179656 | tf_op jit(solution)/shard_map/ppermute | solution.py:409
  44.9 1.0 copy-start.7
  47.4 16.7 %copy-start.2 = (f32[1024,128]{1,0:T(8,128)}, f32[1024,128]{1,0:T(8,128)S(1)}, u32[]{:S(2)}) copy-start(f32[1024,128]{1,0:T(8,128)S(1)} %get-tuple-element.46.image_own) | copy-start | bytes 1572868
  47.4 27.1 %collective-permute-start.6 = (f32[768,128]{1,0:T(8,128)}, f32[768,128]{1,0:T(8,128)S(1)}, u32[]{:S(2)}, u32[]{:S(2)}) collective-permute-start(f32[768,128]{1,0:T(8,128)} %get-tuple-element.47), channel_id=1, source_target_pairs={{0,1},{1,0},{2,3},{3,2},{4,5},{5,4},{6,7},{7,6},{8,9},{9,8},{10,11... | collective-permute-start | bytes 1179656 | tf_op jit(solution)/shard_map/ppermute | solution.py:409
  47.9 26.6 %collective-permute-start.7 = (f32[768,128]{1,0:T(8,128)}, f32[768,128]{1,0:T(8,128)S(1)}, u32[]{:S(2)}, u32[]{:S(2)}) collective-permute-start(f32[768,128]{1,0:T(8,128)} %get-tuple-element.48), channel_id=1, source_target_pairs={{1,2},{3,4},{5,6},{7,8},{9,10},{11,12},{13,14},{15,16},{17,18},{19... | collective-permute-start | bytes 1179656 | tf_op jit(solution)/shard_map/ppermute | solution.py:408
  51.6 22.9 %copy-start.3 = (f32[128,128]{1,0:T(8,128)S(1)}, f32[128,128]{1,0:T(8,128)}, u32[]{:S(2)}) copy-start(f32[128,128]{1,0:T(8,128)} %load.1) | copy-start | bytes 196612
  51.6 22.9 %all-to-all-start.1 = ((f32[128,1,384]{2,1,0:T(1,128)}), f32[128,1,384]{2,1,0:T(1,128)S(1)}, u32[]{:S(2)}, u32[]{:S(2)}) async-start(f32[128,1,384]{2,1,0:T(1,128)} %bitcast.3), calls=%async_computation.1 | async-start | bytes 393216 | tf_op jit(solution)/shard_map/all_to_all | solution.py:420
  87.4 2.8 %collective-permute-start.8 = (f32[768,128]{1,0:T(8,128)S(1)}, f32[768,128]{1,0:T(8,128)S(1)}, u32[]{:S(2)}, u32[]{:S(2)}) collective-permute-start(f32[768,128]{1,0:T(8,128)S(1)} %get-tuple-element.53), channel_id=1, source_target_pairs={{0,1},{1,0},{2,3},{3,2},{4,5},{5,4},{6,7},{7,6},{8,9},{9,8},{10,11... | collective-permute-start | bytes 1179656 | tf_op jit(solution)/shard_map/ppermute | solution.py:409
  88.2 9.1 %collective-permute-start.9 = (f32[768,128]{1,0:T(8,128)S(1)}, f32[768,128]{1,0:T(8,128)S(1)}, u32[]{:S(2)}, u32[]{:S(2)}) collective-permute-start(f32[768,128]{1,0:T(8,128)S(1)} %get-tuple-element.54), channel_id=1, source_target_pairs={{1,2},{3,4},{5,6},{7,8},{9,10},{11,12},{13,14},{15,16},{17,18},{19... | collective-permute-start | bytes 1179656 | tf_op jit(solution)/shard_map/ppermute | solution.py:408
  97.3 1.0 copy-start.5
  99.1 24.8 %collective-permute-start.10 = (f32[768,128]{1,0:T(8,128)S(1)}, f32[768,128]{1,0:T(8,128)S(1)}, u32[]{:S(2)}, u32[]{:S(2)}) collective-permute-start(f32[768,128]{1,0:T(8,128)S(1)} %get-tuple-element.56), channel_id=1, source_target_pairs={{0,1},{1,0},{2,3},{3,2},{4,5},{5,4},{6,7},{7,6},{8,9},{9,8},{10,11... | collective-permute-start | bytes 1179656 | tf_op jit(solution)/shard_map/ppermute | solution.py:409
  99.2 24.7 %collective-permute-start.11 = (f32[768,128]{1,0:T(8,128)S(1)}, f32[768,128]{1,0:T(8,128)S(1)}, u32[]{:S(2)}, u32[]{:S(2)}) collective-permute-start(f32[768,128]{1,0:T(8,128)S(1)} %get-tuple-element.57), channel_id=1, source_target_pairs={{1,2},{3,4},{5,6},{7,8},{9,10},{11,12},{13,14},{15,16},{17,18},{19... | collective-permute-start | bytes 1179656 | tf_op jit(solution)/shard_map/ppermute | solution.py:408
  134.2 3.1 %collective-permute-start.12 = (f32[768,128]{1,0:T(8,128)S(1)}, f32[768,128]{1,0:T(8,128)S(1)}, u32[]{:S(2)}, u32[]{:S(2)}) collective-permute-start(f32[768,128]{1,0:T(8,128)S(1)} %get-tuple-element.63), channel_id=1, source_target_pairs={{0,1},{1,0},{2,3},{3,2},{4,5},{5,4},{6,7},{7,6},{8,9},{9,8},{10,11... | collective-permute-start | bytes 1179656 | tf_op jit(solution)/shard_map/ppermute | solution.py:409
  135.4 9.1 %collective-permute-start.13 = (f32[768,128]{1,0:T(8,128)S(1)}, f32[768,128]{1,0:T(8,128)S(1)}, u32[]{:S(2)}, u32[]{:S(2)}) collective-permute-start(f32[768,128]{1,0:T(8,128)S(1)} %get-tuple-element.64), channel_id=1, source_target_pairs={{1,2},{3,4},{5,6},{7,8},{9,10},{11,12},{13,14},{15,16},{17,18},{19... | collective-permute-start | bytes 1179656 | tf_op jit(solution)/shard_map/ppermute | solution.py:408
  145.1 24.9 %collective-permute-start.14 = (f32[768,128]{1,0:T(8,128)S(1)}, f32[768,128]{1,0:T(8,128)S(1)}, u32[]{:S(2)}, u32[]{:S(2)}) collective-permute-start(f32[768,128]{1,0:T(8,128)S(1)} %get-tuple-element.66), channel_id=1, source_target_pairs={{0,1},{1,0},{2,3},{3,2},{4,5},{5,4},{6,7},{7,6},{8,9},{9,8},{10,11... | collective-permute-start | bytes 1179656 | tf_op jit(solution)/shard_map/ppermute | solution.py:409
  145.2 24.8 %collective-permute-start.15 = (f32[768,128]{1,0:T(8,128)S(1)}, f32[768,128]{1,0:T(8,128)S(1)}, u32[]{:S(2)}, u32[]{:S(2)}) collective-permute-start(f32[768,128]{1,0:T(8,128)S(1)} %get-tuple-element.67), channel_id=1, source_target_pairs={{1,2},{3,4},{5,6},{7,8},{9,10},{11,12},{13,14},{15,16},{17,18},{19... | collective-permute-start | bytes 1179656 | tf_op jit(solution)/shard_map/ppermute | solution.py:408
  170.1 15.4 %copy-start.1 = (f32[1024,128]{1,0:T(8,128)S(1)}, f32[1024,128]{1,0:T(8,128)}, u32[]{:S(2)}) copy-start(f32[1024,128]{1,0:T(8,128)} %basis.1) | copy-start | bytes 1572868
  170.1 15.4 %copy-start.4 = (f32[1024,128]{1,0:T(8,128)S(1)}, f32[1024,128]{1,0:T(8,128)}, u32[]{:S(2)}) copy-start(f32[1024,128]{1,0:T(8,128)} %get-tuple-element.74.r0) | copy-start | bytes 1572868
  180.6 15.6 %all-to-all-start.4 = ((f32[128,1,512]{2,1,0:T(1,128)}), f32[128,1,512]{2,1,0:T(1,128)S(1)}, u32[]{:S(2)}, u32[]{:S(2)}) async-start(f32[128,1,512]{2,1,0:T(1,128)} %bitcast.9), calls=%async_computation.4 | async-start | bytes 524288 | tf_op jit(solution)/shard_map/all_to_all | solution.py:420
  187.0 0.8 copy-start.8
  187.8 0.8 copy-start.10
  196.2 1.0 copy-start.9
  197.3 1.0 copy-start.11
  198.3 0.9 copy-start.13
  (2 other events, 1.4 us)

commit v4 on v3

--- a/solution.py
+++ b/solution.py
@@ -167,7 +167,7 @@
 
 
 def first_kernel(
-    place, own, partner, remote, gram, coarse, schur,
+    place, own, partner, remote, right, schur,
     out_own, out_partner, out_remote, joined,
     buffer, arrivals, halves, ext, image, form, cross,
 ):
@@ -175,8 +175,8 @@
     fetch(schur, buffer, arrivals)
     assemble(ext, (own, partner, remote), parity)
     clear(form, cross, image)
-    put(joined, 0, 3, gram[...])
-    put(joined, 1, 3, coarse[...])
+    put(joined, 0, 3, contract_rows(own[...], own[...]))
+    put(joined, 1, 3, contract_rows(own[...], right[...]))
 
     def use(rows, product):
         cross[...] += close_contract(ext[rows, :], product)
@@ -188,31 +188,34 @@
 
 
 def start_kernel(
-    place, arrived, load, square,
+    place, arrived, load,
     right_own, right_partner, right_remote,
     basis_own, basis_partner, basis_remote,
     image_own, image_partner, image_remote, schur,
     out_own, out_partner, out_remote, joined,
-    residual, z_ext, new_own, inverse, first, amp, stiff,
-    buffer, arrivals, halves, image, form, cross,
+    out_residual, out_z, inverse, first, amp, stiff,
+    buffer, arrivals, halves, residual, z_ext, image, form, cross, saved,
 ):
     start, parity = place[0] - SKIP, place[1]
     fetch(schur, buffer, arrivals)
+    assemble(z_ext, (image_own, image_partner, image_remote), parity)
+    save_z = pltpu.make_async_copy(z_ext, out_z, saved.at[0])
+    save_z.start()
+    put(joined, 4, 5, close_contract(image_own[...], image_own[...]))
     invert(part(arrived, 0, 3), inverse)
     stiff[...] = part(arrived, 2, 3)
     first[...] = full_dot(inverse[...], load[...])
     amp[...] = full_dot(inverse[...], part(arrived, 1, 3) - full_dot(stiff[...], first[...]))
-    assemble(z_ext, (image_own, image_partner, image_remote), parity)
     assemble(image, (basis_own, basis_partner, basis_remote), parity)
     assemble(residual, (right_own, right_partner, right_remote), parity)
     residual[...] = (
         residual[...] - close_dot(z_ext[...], first[...]) - close_dot(image[...], amp[...])
     )
+    save = pltpu.make_async_copy(residual, out_residual, saved.at[1])
+    save.start()
     clear(form, cross, image)
     own = residual[OWN, :]
-    new_own[...] = own
     put(joined, 0, 5, column_sum(own, own))
-    put(joined, 4, 5, square[...])
     put(joined, 2, 5, close_contract(image_own[...], own))
 
     def use(rows, product):
@@ -224,22 +227,32 @@
     deliver(image, parity, out_own, out_partner, out_remote)
     put(joined, 1, 5, jnp.sum(form[...], axis=0, keepdims=True))
     put(joined, 3, 5, cross[...])
+    save_z.wait()
+    save.wait()
 
 
 def middle_kernel(
-    place, arrived, last, z_ext, own, partner, remote, schur,
-    out_own, out_partner, out_remote, joined, residual, w_ext, new_own, scalars,
-    buffer, arrivals, halves, image, form, cross,
+    place, arrived, own, partner, remote, last, z_last, schur,
+    out_own, out_partner, out_remote, joined, out_residual, out_w, scalars,
+    buffer, arrivals, halves, residual, z_ext, w_ext, image, form, cross, saved,
 ):
     start, parity = place[0] - SKIP, place[1]
+    load = pltpu.make_async_copy(last, residual, saved.at[0])
+    load_z = pltpu.make_async_copy(z_last, z_ext, saved.at[1])
+    load.start()
+    load_z.start()
     fetch(schur, buffer, arrivals)
     energy = total(arrived, 0, 5)
     length = energy / total(arrived, 1, 5)
     assemble(w_ext, (own, partner, remote), parity)
-    residual[...] = last[...] - length * w_ext[...]
+    save_w = pltpu.make_async_copy(w_ext, out_w, saved.at[2])
+    save_w.start()
+    load.wait()
+    residual[...] = residual[...] - length * w_ext[...]
+    save = pltpu.make_async_copy(residual, out_residual, saved.at[3])
+    save.start()
     clear(form, cross, image)
     mine = residual[OWN, :]
-    new_own[...] = mine
     put(joined, 0, 5, column_sum(mine, mine))
     put(joined, 2, 5, total(arrived, 2, 5))
     put(joined, 3, 5, total(arrived, 3, 5))
@@ -247,6 +260,7 @@
     scalars[0:1, :] = energy
     scalars[1:2, :] = length
     scalars[2:3, :] = total(arrived, 4, 5)
+    load_z.wait()
 
     def use(rows, product):
         add_form(form, residual, rows, product)
@@ -257,14 +271,25 @@
     deliver(image, parity, out_own, out_partner, out_remote)
     put(joined, 1, 5, jnp.sum(form[...], axis=0, keepdims=True))
     put(joined, 4, 5, cross[...])
+    save_w.wait()
+    save.wait()
 
 
 def last_kernel(
-    place, arrived, scalars, last, w_last, z_ext, own, partner, remote, inverse, stiff, schur,
-    joined, new_own, numbers, matrices,
-    buffer, arrivals, halves, residual, form, w_ext,
+    place, arrived, scalars, own, partner, remote, inverse, stiff, first, basis,
+    last, w_last, z_last, schur,
+    joined, base, d1, p2, numbers, matrices,
+    buffer, arrivals, halves, residual, z_ext, w_ext, w_old, form, saved,
 ):
     start, parity = place[0] - SKIP, place[1]
+    loads = [
+        pltpu.make_async_copy(here, there, saved.at[index])
+        for index, (here, there) in enumerate(
+            ((z_last, z_ext), (last, residual), (w_last, w_old))
+        )
+    ]
+    for load in loads:
+        load.start()
     fetch(schur, buffer, arrivals)
     energy0, length0 = scalars[0:1, :], scalars[1:2, :]
     e0, f0 = part(arrived, 2, 5), part(arrived, 3, 5)
@@ -282,11 +307,16 @@
     )
     length1 = energy1 / curve1
     assemble(w_ext, (own, partner, remote), parity)
-    residual[...] = last[...] - length1 * (
-        w_ext[...] - close_dot(z_ext[...], a1) + ratio0 * w_last[...]
+    for load in loads:
+        load.wait()
+    r1 = residual[OWN, :]
+    r0 = r1 + length0 * w_old[OWN, :]
+    d1[...] = r1 - close_dot(basis[...], a1) + ratio0 * r0
+    base[...] = close_dot(basis[...], first[...]) + length0 * r0 + length1 * d1[...]
+    residual[...] = residual[...] - length1 * (
+        w_ext[...] - close_dot(z_ext[...], a1) + ratio0 * w_old[...]
     )
     mine = residual[OWN, :]
-    new_own[...] = mine
     put(joined, 0, 4, column_sum(mine, mine))
     put(joined, 2, 4, total(arrived, 4, 5))
     put(joined, 3, 4, scalars[2:3, :])
@@ -296,10 +326,15 @@
     numbers[2:3, :] = ratio0
     numbers[3:4, :] = energy1
     d_coarse = e1 - stiff_a1 + ratio0 * e0
+    c2 = c1 - length1 * d_coarse
+    a2 = full_dot(inverse[...], c2)
+    p2[...] = mine - close_dot(basis[...], a2)
     matrices[0] = a1
-    matrices[1] = c1 - length1 * d_coarse
+    matrices[1] = c2
     matrices[2] = d_coarse
     matrices[3] = e1 - length1 * ratio0 * f0
+    matrices[4] = a2
+    matrices[5] = full_dot(stiff[...], a2)
     form[...] = jnp.zeros_like(form)
 
     def use(rows, product):
@@ -309,26 +344,12 @@
     put(joined, 1, 4, jnp.sum(form[...], axis=0, keepdims=True))
 
 
-def direction_kernel(
-    numbers, matrices, inverse, stiff, first, basis, r0, r1, r2,
-    base, d1, p2, small,
-):
-    length0, length1, ratio0 = numbers[0:1, :], numbers[1:2, :], numbers[2:3, :]
-    a1 = matrices[0]
-    a2 = full_dot(inverse[...], matrices[1])
-    d1[...] = r1[...] - full_dot(basis[...], a1) + ratio0 * r0[...]
-    p2[...] = r2[...] - full_dot(basis[...], a2)
-    base[...] = full_dot(basis[...], first[...]) + length0 * r0[...] + length1 * d1[...]
-    small[0] = a2
-    small[1] = full_dot(stiff[...], a2)
-
-
 def final_kernel(
-    arrived, numbers, matrices, small, inverse, amp, base, d1, p2,
+    arrived, numbers, matrices, inverse, amp, base, d1, p2,
     multipliers, amplitudes,
 ):
     length1, energy1 = numbers[1:2, :], numbers[3:4, :]
-    a2, stiff_a2 = small[0], small[1]
+    a2, stiff_a2 = matrices[4], matrices[5]
     f1, square = part(arrived, 2, 4), part(arrived, 3, 4)
     e2 = matrices[3] - length1 * (f1 - full_dot(square, matrices[0]))
     energy2 = total(arrived, 0, 4) - column_sum(matrices[1], a2)
@@ -363,14 +384,15 @@
     return jax.ShapeDtypeStruct((rows, R), F32)
 
 
-def operator(kernel, place, arrays, schur, outs, scratch):
+def operator(kernel, place, arrays, kept, schur, outs, scratch):
     vmem = pl.BlockSpec(memory_space=pltpu.VMEM)
+    free = pl.BlockSpec(memory_space=pl.ANY)
     return pl.pallas_call(
         kernel,
         in_specs=[pl.BlockSpec(memory_space=pltpu.SMEM)]
         + [vmem] * len(arrays)
-        + [pl.BlockSpec(memory_space=pl.ANY)],
-        out_specs=[vmem] * len(outs),
+        + [free] * (len(kept) + 1),
+        out_specs=[free if o is EXTENDED else vmem for o in outs],
         out_shape=outs,
         scratch_shapes=[
             pltpu.VMEM((WINDOW, WINDOW), F32),
@@ -382,7 +404,7 @@
         cost_estimate=pl.CostEstimate(
             flops=8 * WINDOW * WINDOW * R, bytes_accessed=4 * WINDOW * WINDOW, transcendentals=0
         ),
-    )(place, *arrays, schur)
+    )(place, *arrays, *kept, schur)
 
 
 def small_call(kernel, arrays, outs, place=None):
@@ -437,12 +459,12 @@
     ext = pltpu.VMEM((EXT, R), F32)
     rows = pltpu.VMEM((8, R), F32)
     square = pltpu.VMEM((R, R), F32)
+    waits = pltpu.SemaphoreType.DMA((4,))
 
     basis_sides = swapped(*halves_of(basis, parity))
     right_sides = swapped(*halves_of(right_side, parity))
-    gram, coarse = contract_rows(basis, basis), contract_rows(basis, right_side)
     *image, joined = operator(
-        first_kernel, place, (basis, *basis_sides, gram, coarse), schur,
+        first_kernel, place, (basis, *basis_sides, right_side), (), schur,
         ends + [shape(3 * DEVICES)], [ext, ext, rows, square],
     )
     arrived = exchange(joined, 3)
@@ -452,44 +474,35 @@
     )
     arrived = exchange(joined, 3)
 
-    *w0, joined, r0_ext, z_ext, r0, inverse, first, amp, stiff = operator(
+    *w0, joined, r0, z_ext, inverse, first, amp, stiff = operator(
         start_kernel, place,
-        (
-            arrived, load, contract_rows(image[0], image[0]),
-            right_side, *right_sides, basis, *basis_sides, *image,
-        ),
-        schur,
-        ends + [shape(5 * DEVICES), EXTENDED, EXTENDED, shape(SLAB)] + [MATRIX] * 4,
-        [ext, rows, square],
+        (arrived, load, right_side, *right_sides, basis, *basis_sides, *image), (), schur,
+        ends + [shape(5 * DEVICES), EXTENDED, EXTENDED] + [MATRIX] * 4,
+        [ext, ext, ext, rows, square, waits],
     )
     arrived = exchange(joined, 5)
     w0 = summed(w0, place)
 
-    *w1, joined, r1_ext, w0_ext, r1, scalars = operator(
-        middle_kernel, place, (arrived, r0_ext, z_ext, *w0), schur,
-        ends + [shape(5 * DEVICES), EXTENDED, EXTENDED, shape(SLAB), shape(8)],
-        [ext, rows, square],
+    *w1, joined, r1, w0, scalars = operator(
+        middle_kernel, place, (arrived, *w0), (r0, z_ext), schur,
+        ends + [shape(5 * DEVICES), EXTENDED, EXTENDED, shape(8)],
+        [ext, ext, ext, ext, rows, square, waits],
     )
     arrived = exchange(joined, 5)
     w1 = summed(w1, place)
 
-    joined, r2, numbers, matrices = operator(
+    joined, base, d1, p2, numbers, matrices = operator(
         last_kernel, place,
-        (arrived, scalars, r1_ext, w0_ext, z_ext, *w1, inverse, stiff),
-        schur,
-        [shape(4 * DEVICES), shape(SLAB), shape(8), jax.ShapeDtypeStruct((4, R, R), F32)],
-        [ext, rows, ext],
+        (arrived, scalars, *w1, inverse, stiff, first, basis), (r1, w0, z_ext), schur,
+        [shape(4 * DEVICES)] + [shape(SLAB)] * 3
+        + [shape(8), jax.ShapeDtypeStruct((6, R, R), F32)],
+        [ext, ext, ext, ext, rows, waits],
     )
     arrived = exchange(joined, 4)
-    base, d1, p2, small = small_call(
-        direction_kernel,
-        (numbers, matrices, inverse, stiff, first, basis, r0, r1, r2),
-        [shape(SLAB)] * 3 + [jax.ShapeDtypeStruct((2, R, R), F32)],
-    )
     return tuple(
         small_call(
             final_kernel,
-            (arrived, numbers, matrices, small, inverse, amp, base, d1, p2),
+            (arrived, numbers, matrices, inverse, amp, base, d1, p2),
             [shape(SLAB), MATRIX],
         )
     )

time: 201 us -> 205 us (1.020)
  blocking collectives: 44.8 us -> 60.3 us
  starting transfers between devices: 57.3 us -> 49.6 us
  local copies, waits for them, and re-layouts: 10.2 us -> 5.79 us
  Pallas kernels: 50.2 us -> 54.5 us
  matrix products: 3.01 us -> 0 us
    all_to_all x2 -> x3, blocking collectives: 44.8 us -> 60.3 us  [exchange(): arrived = lax.all_to_all(sent, GX_GY, 0, 0, tiled=True)]
    all_to_all x3 -> x2, starting transfers between devices: 31.1 us -> 24.7 us  [exchange(): arrived = lax.all_to_all(sent, GX_GY, 0, 0, tiled=True)]
    pallas_call x4, Pallas kernels: 43.7 us -> 50 us  [operator(): pl.pallas_call(kernel, in_specs=[pl.BlockSpec(memory_space=pltpu.SMEM)] +...]
    unnamed x30 -> x14, local copies, waits for them, and re-layouts: 8.03 us -> 3.58 us
    dot_general x3 -> x0, matrix products: 3.01 us -> none  [contract_rows(): lax.dot_general(a, b, (((0,), (0,)), ((), ())), precision=HIGHEST, prefer...]
    all_to_all x3 -> x2, waiting for transfers between devices: 16.3 us -> 13.4 us  [exchange(): arrived = lax.all_to_all(sent, GX_GY, 0, 0, tiled=True)]
    pallas_call x6 -> x5, Pallas kernels: 6.47 us -> 4.55 us  [small_call(): pl.pallas_call(kernel, in_specs=[pl.BlockSpec(memory_space=pltpu.SMEM)] *...]
  transfers between devices with their start and end apart: 19 -> 18, of which waited for: 5 -> 5; matrix products, arithmetic and copies ran while one was open for 2% -> 1% of each run, Pallas kernels for 2% -> 1%
where the time goes in v4:
time: 205 us; the launch traced here: 204 us
  blocking collectives  60.3 us (29%)
  Pallas kernels  54.5 us (27%)
  starting transfers between devices  49.6 us (24%)
  waiting for transfers between devices  32.2 us (16%)
  local copies, waits for them, and re-layouts  5.79 us (3%)
    all_to_all x3, blocking collectives, exchange(): arrived = lax.all_to_all(sent, GX_GY, 0, 0, tiled=True)  60.3 us
    pallas_call x4, Pallas kernels, operator(): pl.pallas_call(kernel, in_specs=[pl.BlockSpec(memory_space=pltpu.SMEM)] +...  50 us
    all_to_all x2, starting transfers between devices, exchange(): arrived = lax.all_to_all(sent, GX_GY, 0, 0, tiled=True)  24.7 us
    ppermute x8, starting transfers between devices, swapped(): remote = lax.ppermute(to_remote, GX_GY, REMOTE)  21.5 us
    ppermute x8, waiting for transfers between devices, swapped(): remote = lax.ppermute(to_remote, GX_GY, REMOTE)  18.9 us
    all_to_all x2, waiting for transfers between devices, exchange(): arrived = lax.all_to_all(sent, GX_GY, 0, 0, tiled=True)  13.4 us
    pallas_call x5, Pallas kernels, small_call(): pl.pallas_call(kernel, in_specs=[pl.BlockSpec(memory_space=pltpu.SMEM)] *...  4.55 us
  transfers between devices with their start and end apart: 18, of which 5 were waited for; matrix products, arithmetic and copies ran while one was open for 1% of the time, Pallas kernels for 1%

profile of v4, /device:TPU:1, one launch (start us, length us, event | category | flops | bytes accessed | tf_op | source)
XLA Modules:
  0.0 204.1 jit_solution(6291167843316438305)
XLA Ops:
  0.7 1.3 constant_dynamic-slice_fusion.2
  1.9 4.6 %collective-permute-start.1 = (f32[768,128]{1,0:T(8,128)S(1)}, f32[768,128]{1,0:T(8,128)S(1)}, u32[]{:S(2)}, u32[]{:S(2)}) collective-permute-start(f32[768,128]{1,0:T(8,128)S(1)} %get-tuple-element.76), channel_id=1, source_target_pairs={{1,2},{3,4},{5,6},{7,8},{9,10},{11,12},{13,14},{15,16},{17,18},{19... | collective-permute-start | bytes 1179656 | tf_op jit(solution)/shard_map/ppermute | solution.py:430
  7.3 4.6 %collective-permute-done.1.remote.basis_remote = f32[768,128]{1,0:T(8,128)S(1)} collective-permute-done((f32[768,128]{1,0:T(8,128)S(1)}, f32[768,128]{1,0:T(8,128)S(1)}, u32[]{:S(2)}, u32[]{:S(2)}) %collective-permute-start.1) | collective-permute-done | bytes 393248 | tf_op jit(solution)/shard_map/ppermute | solution.py:430
  12.0 9.8 %shard_map.68 = (f32[1024,128]{1,0:T(8,128)S(1)}, f32[768,128]{1,0:T(8,128)}, f32[768,128]{1,0:T(8,128)S(1)}, f32[384,128]{1,0:T(8,128)}) custom-call(s32[2]{0:T(128)S(1)} %pad_add_fusion.place, f32[1024,128]{1,0:T(8,128)S(1)} %copy-done, f32[768,128]{1,0:T(8,128)S(1)} %collective-permute-done.partner.basis_partner, ...), custom_call_target="tpu_custom_call" | custom-call | flops 4294967296 | bytes 16777216 | tf_op jit(solution)/shard_map/pallas_call | solution.py:390
  21.9 3.7 %collective-permute-start.5 = (f32[768,128]{1,0:T(8,128)S(1)}, f32[768,128]{1,0:T(8,128)}, u32[]{:S(2)}, u32[]{:S(2)}) collective-permute-start(f32[768,128]{1,0:T(8,128)S(1)} %get-tuple-element.41), channel_id=1, source_target_pairs={{1,2},{3,4},{5,6},{7,8},{9,10},{11,12},{13,14},{15,16},{17,18},{19... | collective-permute-start | bytes 1179656 | tf_op jit(solution)/shard_map/ppermute | solution.py:430
  25.6 1.0 constant_dynamic-slice_fusion
  26.5 1.9 collective-permute-start.3
  28.5 18.6 %all-to-all-start = ((f32[128,1,384]{2,1,0:T(1,128)}), f32[128,1,384]{2,1,0:T(1,128)S(1)}, u32[]{:S(2)}, u32[]{:S(2)}) async-start(f32[128,1,384]{2,1,0:T(1,128)} %bitcast.1), calls=%async_computation | async-start | bytes 393216 | tf_op jit(solution)/shard_map/all_to_all | solution.py:442
  47.2 0.7 copy-done.5
  47.9 1.0 copy-done.6
  48.9 1.2 shard_map.70
  50.1 0.8 copy-done.2
  50.9 1.1 collective-permute-start.6
  51.9 2.6 %collective-permute-start.7 = (f32[768,128]{1,0:T(8,128)S(1)}, f32[768,128]{1,0:T(8,128)S(1)}, u32[]{:S(2)}, u32[]{:S(2)}) collective-permute-start(f32[768,128]{1,0:T(8,128)S(1)} %get-tuple-element.44), channel_id=1, source_target_pairs={{1,2},{3,4},{5,6},{7,8},{9,10},{11,12},{13,14},{15,16},{17,18},{19... | collective-permute-start | bytes 1179656 | tf_op jit(solution)/shard_map/ppermute | solution.py:430
  54.5 3.0 %all-to-all-done = f32[128,1,384]{2,1,0:T(1,128)S(1)} async-done(((f32[128,1,384]{2,1,0:T(1,128)}), f32[128,1,384]{2,1,0:T(1,128)S(1)}, u32[]{:S(2)}, u32[]{:S(2)}) %all-to-all-start) | async-done | bytes 196640 | tf_op jit(solution)/shard_map/all_to_all | solution.py:442
  58.2 6.1 %all-to-all-start.1 = ((f32[128,1,384]{2,1,0:T(1,128)}), f32[128,1,384]{2,1,0:T(1,128)S(1)}, u32[]{:S(2)}, u32[]{:S(2)}) async-start(f32[128,1,384]{2,1,0:T(1,128)} %bitcast.3), calls=%async_computation.1 | async-start | bytes 393216 | tf_op jit(solution)/shard_map/all_to_all | solution.py:442
  64.4 10.4 %all-to-all-done.1 = f32[128,1,384]{2,1,0:T(1,128)S(1)} async-done(((f32[128,1,384]{2,1,0:T(1,128)}), f32[128,1,384]{2,1,0:T(1,128)S(1)}, u32[]{:S(2)}, u32[]{:S(2)}) %all-to-all-start.1) | async-done | bytes 196640 | tf_op jit(solution)/shard_map/all_to_all | solution.py:442
  74.8 13.1 %shard_map.71 = (f32[1024,128]{1,0:T(8,128)}, f32[768,128]{1,0:T(8,128)S(1)}, f32[768,128]{1,0:T(8,128)S(1)}, f32[640,128]{1,0:T(8,128)S(1)}, f32[2560,128]{1,0:...) custom-call(s32[2]{0:T(128)S(1)} %pad_add_fusion.place, ...), custom_call_target="tpu_custom_call" | custom-call | flops 4294967296 | bytes 16777216 | tf_op jit(solution)/shard_map/pallas_call | solution.py:390
  88.6 2.0 collective-permute-start.9
  90.7 7.1 %collective-permute-done.9.remote = f32[768,128]{1,0:T(8,128)S(1)} collective-permute-done((f32[768,128]{1,0:T(8,128)S(1)}, f32[768,128]{1,0:T(8,128)S(1)}, u32[]{:S(2)}, u32[]{:S(2)}) %collective-permute-start.9) | collective-permute-done | bytes 393248 | tf_op jit(solution)/shard_map/ppermute | solution.py:430
  97.7 1.0 copy-done.4
  99.6 2.5 %collective-permute-start.11 = (f32[768,128]{1,0:T(8,128)S(1)}, f32[768,128]{1,0:T(8,128)S(1)}, u32[]{:S(2)}, u32[]{:S(2)}) collective-permute-start(f32[768,128]{1,0:T(8,128)S(1)} %get-tuple-element.51), channel_id=1, source_target_pairs={{1,2},{3,4},{5,6},{7,8},{9,10},{11,12},{13,14},{15,16},{17,18},{19... | collective-permute-start | bytes 1179656 | tf_op jit(solution)/shard_map/ppermute | solution.py:430
  102.0 22.3 %all_to_all.25 = f32[128,1,640]{2,1,0:T(1,128)S(1)} all-to-all(f32[128,1,640]{2,1,0:T(1,128)S(1)} %bitcast.14), channel_id=1, replica_groups=mesh['gx'=4,'gy_0'=4,'gy_1'=4,'gy_2'=2] {'gx','gy_0','gy_1','gy_2'}, dimensions={0} | all-to-all | bytes 655360 | tf_op jit(solution)/shard_map/all_to_all | solution.py:442
  124.4 12.9 %shard_map.73 = (f32[1024,128]{1,0:T(8,128)S(1)}, f32[768,128]{1,0:T(8,128)S(1)}, f32[768,128]{1,0:T(8,128)S(1)}, f32[640,128]{1,0:T(8,128)S(1)}, f32[2560,128]{...) custom-call(s32[2]{0:T(128)S(1)} %pad_add_fusion.place, f32[640,128]{1,0:T(8,128)S(1)} %bitcast.12, ...), custom_call_target="tpu_custom_call" | custom-call | flops 4294967296 | bytes 16777216 | tf_op jit(solution)/shard_map/pallas_call | solution.py:390
  137.3 1.2 collective-permute-start.12
  138.5 1.9 collective-permute-start.13
  140.4 7.2 %collective-permute-done.13.remote = f32[768,128]{1,0:T(8,128)S(1)} collective-permute-done((f32[768,128]{1,0:T(8,128)S(1)}, f32[768,128]{1,0:T(8,128)S(1)}, u32[]{:S(2)}, u32[]{:S(2)}) %collective-permute-start.13) | collective-permute-done | bytes 393248 | tf_op jit(solution)/shard_map/ppermute | solution.py:430
  148.4 2.3 %collective-permute-start.15 = (f32[768,128]{1,0:T(8,128)S(1)}, f32[768,128]{1,0:T(8,128)S(1)}, u32[]{:S(2)}, u32[]{:S(2)}) collective-permute-start(f32[768,128]{1,0:T(8,128)S(1)} %get-tuple-element.61), channel_id=1, source_target_pairs={{1,2},{3,4},{5,6},{7,8},{9,10},{11,12},{13,14},{15,16},{17,18},{19... | collective-permute-start | bytes 1179656 | tf_op jit(solution)/shard_map/ppermute | solution.py:430
  150.7 22.5 %all_to_all.26 = f32[128,1,640]{2,1,0:T(1,128)S(1)} all-to-all(f32[128,1,640]{2,1,0:T(1,128)S(1)} %bitcast.15), channel_id=1, replica_groups=mesh['gx'=4,'gy_0'=4,'gy_1'=4,'gy_2'=2] {'gx','gy_0','gy_1','gy_2'}, dimensions={0} | all-to-all | bytes 655360 | tf_op jit(solution)/shard_map/all_to_all | solution.py:442
  173.2 14.1 %shard_map.75 = (f32[512,128]{1,0:T(8,128)S(1)}, f32[1024,128]{1,0:T(8,128)S(1)}, f32[1024,128]{1,0:T(8,128)S(1)}, f32[1024,128]{1,0:T(8,128)S(1)}, f32[8,128]{1,0:T(8,128)S(1)}, /*index=5*/f32[6,128,128]{2,1,0:T(8,128)S(1)}) custom-call(s32[2]{0:T(128)S(1)} %pad_add_fusion.place, f32[640,128]{1,0:T(8,128)S(1)} %bitcast.11, ...), custom_call_target="tpu_custom_call" | custom-call | flops 4294967296 | bytes 16777216 | tf_op jit(solution)/shard_map/pallas_call | solution.py:390
  187.3 15.5 %all_to_all.27 = f32[128,1,512]{2,1,0:T(1,128)S(1)} all-to-all(f32[128,1,512]{2,1,0:T(1,128)S(1)} %bitcast.16), channel_id=1, replica_groups=mesh['gx'=4,'gy_0'=4,'gy_1'=4,'gy_2'=2] {'gx','gy_0','gy_1','gy_2'}, dimensions={0} | all-to-all | bytes 524288 | tf_op jit(solution)/shard_map/all_to_all | solution.py:442
  202.8 1.3 shard_map.76
  (33 shorter events, 3.4 us)
Async XLA Ops:
  0.6 11.3 %copy-start = (f32[1024,128]{1,0:T(8,128)S(1)}, f32[1024,128]{1,0:T(8,128)}, u32[]{:S(2)}) copy-start(f32[1024,128]{1,0:T(8,128)} %basis.1) | copy-start | bytes 1572868
  0.6 11.3 %copy-start.1 = (f32[1024,128]{1,0:T(8,128)S(1)}, f32[1024,128]{1,0:T(8,128)}, u32[]{:S(2)}) copy-start(f32[1024,128]{1,0:T(8,128)} %right_own.1) | copy-start | bytes 1572868
  1.9 10.0 %collective-permute-start.1 = (f32[768,128]{1,0:T(8,128)S(1)}, f32[768,128]{1,0:T(8,128)S(1)}, u32[]{:S(2)}, u32[]{:S(2)}) collective-permute-start(f32[768,128]{1,0:T(8,128)S(1)} %get-tuple-element.76), channel_id=1, source_target_pairs={{1,2},{3,4},{5,6},{7,8},{9,10},{11,12},{13,14},{15,16},{17,18},{19... | collective-permute-start | bytes 1179656 | tf_op jit(solution)/shard_map/ppermute | solution.py:430
  6.5 5.4 %collective-permute-start = (f32[768,128]{1,0:T(8,128)S(1)}, f32[768,128]{1,0:T(8,128)S(1)}, u32[]{:S(2)}, u32[]{:S(2)}) collective-permute-start(f32[768,128]{1,0:T(8,128)S(1)} %get-tuple-element.77), channel_id=1, source_target_pairs={{0,1},{1,0},{2,3},{3,2},{4,5},{5,4},{6,7},{7,6},{8,9},{9,8},{10,11... | collective-permute-start | bytes 1179656 | tf_op jit(solution)/shard_map/ppermute | solution.py:431
  21.8 25.4 %collective-permute-start.4 = (f32[768,128]{1,0:T(8,128)}, f32[768,128]{1,0:T(8,128)S(1)}, u32[]{:S(2)}, u32[]{:S(2)}) collective-permute-start(f32[768,128]{1,0:T(8,128)} %get-tuple-element.40), channel_id=1, source_target_pairs={{0,1},{1,0},{2,3},{3,2},{4,5},{5,4},{6,7},{7,6},{8,9},{9,8},{10,11... | collective-permute-start | bytes 1179656 | tf_op jit(solution)/shard_map/ppermute | solution.py:431
  21.9 26.0 %collective-permute-start.5 = (f32[768,128]{1,0:T(8,128)S(1)}, f32[768,128]{1,0:T(8,128)}, u32[]{:S(2)}, u32[]{:S(2)}) collective-permute-start(f32[768,128]{1,0:T(8,128)S(1)} %get-tuple-element.41), channel_id=1, source_target_pairs={{1,2},{3,4},{5,6},{7,8},{9,10},{11,12},{13,14},{15,16},{17,18},{19... | collective-permute-start | bytes 1179656 | tf_op jit(solution)/shard_map/ppermute | solution.py:430
  26.5 37.8 %collective-permute-start.3 = (f32[768,128]{1,0:T(8,128)}, f32[768,128]{1,0:T(8,128)S(1)}, u32[]{:S(2)}, u32[]{:S(2)}) collective-permute-start(f32[768,128]{1,0:T(8,128)} %get-tuple-element.74), channel_id=1, source_target_pairs={{1,2},{3,4},{5,6},{7,8},{9,10},{11,12},{13,14},{15,16},{17,18},{19... | collective-permute-start | bytes 1179656 | tf_op jit(solution)/shard_map/ppermute | solution.py:430
  28.5 35.9 %collective-permute-start.2 = (f32[768,128]{1,0:T(8,128)}, f32[768,128]{1,0:T(8,128)S(1)}, u32[]{:S(2)}, u32[]{:S(2)}) collective-permute-start(f32[768,128]{1,0:T(8,128)} %get-tuple-element.75), channel_id=1, source_target_pairs={{0,1},{1,0},{2,3},{3,2},{4,5},{5,4},{6,7},{7,6},{8,9},{9,8},{10,11... | collective-permute-start | bytes 1179656 | tf_op jit(solution)/shard_map/ppermute | solution.py:431
  28.5 29.0 %all-to-all-start = ((f32[128,1,384]{2,1,0:T(1,128)}), f32[128,1,384]{2,1,0:T(1,128)S(1)}, u32[]{:S(2)}, u32[]{:S(2)}) async-start(f32[128,1,384]{2,1,0:T(1,128)} %bitcast.1), calls=%async_computation | async-start | bytes 393216 | tf_op jit(solution)/shard_map/all_to_all | solution.py:442
  47.1 0.7 copy-start.5
  47.9 1.0 copy-start.6
  50.1 0.8 copy-start.2
  50.9 23.9 %collective-permute-start.6 = (f32[768,128]{1,0:T(8,128)S(1)}, f32[768,128]{1,0:T(8,128)S(1)}, u32[]{:S(2)}, u32[]{:S(2)}) collective-permute-start(f32[768,128]{1,0:T(8,128)S(1)} %get-tuple-element.43), channel_id=1, source_target_pairs={{0,1},{1,0},{2,3},{3,2},{4,5},{5,4},{6,7},{7,6},{8,9},{9,8},{10,11... | collective-permute-start | bytes 1179656 | tf_op jit(solution)/shard_map/ppermute | solution.py:431
  51.9 22.8 %collective-permute-start.7 = (f32[768,128]{1,0:T(8,128)S(1)}, f32[768,128]{1,0:T(8,128)S(1)}, u32[]{:S(2)}, u32[]{:S(2)}) collective-permute-start(f32[768,128]{1,0:T(8,128)S(1)} %get-tuple-element.44), channel_id=1, source_target_pairs={{1,2},{3,4},{5,6},{7,8},{9,10},{11,12},{13,14},{15,16},{17,18},{19... | collective-permute-start | bytes 1179656 | tf_op jit(solution)/shard_map/ppermute | solution.py:430
  57.5 17.2 %copy-start.3 = (f32[128,128]{1,0:T(8,128)S(1)}, f32[128,128]{1,0:T(8,128)}, u32[]{:S(2)}) copy-start(f32[128,128]{1,0:T(8,128)} %load.1) | copy-start | bytes 196612
  58.2 16.5 %all-to-all-start.1 = ((f32[128,1,384]{2,1,0:T(1,128)}), f32[128,1,384]{2,1,0:T(1,128)S(1)}, u32[]{:S(2)}, u32[]{:S(2)}) async-start(f32[128,1,384]{2,1,0:T(1,128)} %bitcast.3), calls=%async_computation.1 | async-start | bytes 393216 | tf_op jit(solution)/shard_map/all_to_all | solution.py:442
  87.9 2.8 %collective-permute-start.8 = (f32[768,128]{1,0:T(8,128)S(1)}, f32[768,128]{1,0:T(8,128)S(1)}, u32[]{:S(2)}, u32[]{:S(2)}) collective-permute-start(f32[768,128]{1,0:T(8,128)S(1)} %get-tuple-element.47), channel_id=1, source_target_pairs={{0,1},{1,0},{2,3},{3,2},{4,5},{5,4},{6,7},{7,6},{8,9},{9,8},{10,11... | collective-permute-start | bytes 1179656 | tf_op jit(solution)/shard_map/ppermute | solution.py:431
  88.6 9.1 %collective-permute-start.9 = (f32[768,128]{1,0:T(8,128)S(1)}, f32[768,128]{1,0:T(8,128)S(1)}, u32[]{:S(2)}, u32[]{:S(2)}) collective-permute-start(f32[768,128]{1,0:T(8,128)S(1)} %get-tuple-element.48), channel_id=1, source_target_pairs={{1,2},{3,4},{5,6},{7,8},{9,10},{11,12},{13,14},{15,16},{17,18},{19... | collective-permute-start | bytes 1179656 | tf_op jit(solution)/shard_map/ppermute | solution.py:430
  97.7 1.0 copy-start.4
  99.5 24.9 %collective-permute-start.10 = (f32[768,128]{1,0:T(8,128)S(1)}, f32[768,128]{1,0:T(8,128)S(1)}, u32[]{:S(2)}, u32[]{:S(2)}) collective-permute-start(f32[768,128]{1,0:T(8,128)S(1)} %get-tuple-element.50), channel_id=1, source_target_pairs={{0,1},{1,0},{2,3},{3,2},{4,5},{5,4},{6,7},{7,6},{8,9},{9,8},{10,11... | collective-permute-start | bytes 1179656 | tf_op jit(solution)/shard_map/ppermute | solution.py:431
  99.6 24.8 %collective-permute-start.11 = (f32[768,128]{1,0:T(8,128)S(1)}, f32[768,128]{1,0:T(8,128)S(1)}, u32[]{:S(2)}, u32[]{:S(2)}) collective-permute-start(f32[768,128]{1,0:T(8,128)S(1)} %get-tuple-element.51), channel_id=1, source_target_pairs={{1,2},{3,4},{5,6},{7,8},{9,10},{11,12},{13,14},{15,16},{17,18},{19... | collective-permute-start | bytes 1179656 | tf_op jit(solution)/shard_map/ppermute | solution.py:430
  137.3 3.1 %collective-permute-start.12 = (f32[768,128]{1,0:T(8,128)S(1)}, f32[768,128]{1,0:T(8,128)S(1)}, u32[]{:S(2)}, u32[]{:S(2)}) collective-permute-start(f32[768,128]{1,0:T(8,128)S(1)} %get-tuple-element.57), channel_id=1, source_target_pairs={{0,1},{1,0},{2,3},{3,2},{4,5},{5,4},{6,7},{7,6},{8,9},{9,8},{10,11... | collective-permute-start | bytes 1179656 | tf_op jit(solution)/shard_map/ppermute | solution.py:431
  138.5 9.1 %collective-permute-start.13 = (f32[768,128]{1,0:T(8,128)S(1)}, f32[768,128]{1,0:T(8,128)S(1)}, u32[]{:S(2)}, u32[]{:S(2)}) collective-permute-start(f32[768,128]{1,0:T(8,128)S(1)} %get-tuple-element.58), channel_id=1, source_target_pairs={{1,2},{3,4},{5,6},{7,8},{9,10},{11,12},{13,14},{15,16},{17,18},{19... | collective-permute-start | bytes 1179656 | tf_op jit(solution)/shard_map/ppermute | solution.py:430
  148.3 24.9 %collective-permute-start.14 = (f32[768,128]{1,0:T(8,128)S(1)}, f32[768,128]{1,0:T(8,128)S(1)}, u32[]{:S(2)}, u32[]{:S(2)}) collective-permute-start(f32[768,128]{1,0:T(8,128)S(1)} %get-tuple-element.60), channel_id=1, source_target_pairs={{0,1},{1,0},{2,3},{3,2},{4,5},{5,4},{6,7},{7,6},{8,9},{9,8},{10,11... | collective-permute-start | bytes 1179656 | tf_op jit(solution)/shard_map/ppermute | solution.py:431
  148.4 24.8 %collective-permute-start.15 = (f32[768,128]{1,0:T(8,128)S(1)}, f32[768,128]{1,0:T(8,128)S(1)}, u32[]{:S(2)}, u32[]{:S(2)}) collective-permute-start(f32[768,128]{1,0:T(8,128)S(1)} %get-tuple-element.61), channel_id=1, source_target_pairs={{1,2},{3,4},{5,6},{7,8},{9,10},{11,12},{13,14},{15,16},{17,18},{19... | collective-permute-start | bytes 1179656 | tf_op jit(solution)/shard_map/ppermute | solution.py:430

commit v5 on v4

--- a/solution.py
+++ b/solution.py
@@ -25,6 +25,7 @@
 STEPS = WINDOW // CHUNK
 PIECES = 8
 PIECE = WINDOW // PIECES
+AHEAD = 4
 OWN = slice(REACH, HIGH)
 
 MATRIX = jax.ShapeDtypeStruct((R, R), F32)
@@ -125,8 +126,8 @@
     return pltpu.make_async_copy(schur.at[0, rows, :], buffer.at[rows, :], arrivals.at[index])
 
 
-def fetch(schur, buffer, arrivals):
-    for index in range(PIECES):
+def fetch(schur, buffer, arrivals, first, last):
+    for index in range(first, last):
         piece_of(schur, buffer, arrivals, index).start()
 
 
@@ -138,6 +139,13 @@
     def body(step, carry):
         for index in range(PIECES // STEPS):
             piece_of(schur, buffer, arrivals, step * (PIECES // STEPS) + index).wait()
+
+        @pl.when(step < (PIECES - AHEAD) // (PIECES // STEPS))
+        def _():
+            for index in range(PIECES // STEPS):
+                at = AHEAD + step * (PIECES // STEPS) + index
+                piece_of(schur, buffer, arrivals, at).start()
+
         at = pl.multiple_of(step * CHUNK, CHUNK)
         high, low = split_bf16(buffer[pl.ds(at, CHUNK), :])
         both = jnp.dot(high, halves[...], preferred_element_type=F32)
@@ -172,7 +180,7 @@
     buffer, arrivals, halves, ext, image, form, cross,
 ):
     start, parity = place[0] - SKIP, place[1]
-    fetch(schur, buffer, arrivals)
+    fetch(schur, buffer, arrivals, 0, AHEAD)
     assemble(ext, (own, partner, remote), parity)
     clear(form, cross, image)
     put(joined, 0, 3, contract_rows(own[...], own[...]))
@@ -197,7 +205,7 @@
     buffer, arrivals, halves, residual, z_ext, image, form, cross, saved,
 ):
     start, parity = place[0] - SKIP, place[1]
-    fetch(schur, buffer, arrivals)
+    fetch(schur, buffer, arrivals, 0, AHEAD)
     assemble(z_ext, (image_own, image_partner, image_remote), parity)
     save_z = pltpu.make_async_copy(z_ext, out_z, saved.at[0])
     save_z.start()
@@ -241,13 +249,14 @@
     load_z = pltpu.make_async_copy(z_last, z_ext, saved.at[1])
     load.start()
     load_z.start()
-    fetch(schur, buffer, arrivals)
+    fetch(schur, buffer, arrivals, 0, 2)
     energy = total(arrived, 0, 5)
     length = energy / total(arrived, 1, 5)
     assemble(w_ext, (own, partner, remote), parity)
     save_w = pltpu.make_async_copy(w_ext, out_w, saved.at[2])
     save_w.start()
     load.wait()
+    fetch(schur, buffer, arrivals, 2, AHEAD)
     residual[...] = residual[...] - length * w_ext[...]
     save = pltpu.make_async_copy(residual, out_residual, saved.at[3])
     save.start()
@@ -290,7 +299,7 @@
     ]
     for load in loads:
         load.start()
-    fetch(schur, buffer, arrivals)
+    fetch(schur, buffer, arrivals, 0, 1)
     energy0, length0 = scalars[0:1, :], scalars[1:2, :]
     e0, f0 = part(arrived, 2, 5), part(arrived, 3, 5)
     c1 = -length0 * e0
@@ -309,6 +318,7 @@
     assemble(w_ext, (own, partner, remote), parity)
     for load in loads:
         load.wait()
+    fetch(schur, buffer, arrivals, 1, AHEAD)
     r1 = residual[OWN, :]
     r0 = r1 + length0 * w_old[OWN, :]
     d1[...] = r1 - close_dot(basis[...], a1) + ratio0 * r0

time: 205 us -> 200 us (0.976)
  Pallas kernels: 54.5 us -> 49.5 us
    pallas_call x4, Pallas kernels: 50 us -> 45 us  [operator(): pl.pallas_call(kernel, in_specs=[pl.BlockSpec(memory_space=pltpu.SMEM)] +...]
where the time goes in v5:
time: 200 us; the launch traced here: 199 us
  blocking collectives  60.3 us (30%)
  starting transfers between devices  49.6 us (25%)
  Pallas kernels  49.5 us (25%)
  waiting for transfers between devices  32.2 us (16%)
  local copies, waits for them, and re-layouts  5.79 us (3%)
    all_to_all x3, blocking collectives, exchange(): arrived = lax.all_to_all(sent, GX_GY, 0, 0, tiled=True)  60.3 us
    pallas_call x4, Pallas kernels, operator(): pl.pallas_call(kernel, in_specs=[pl.BlockSpec(memory_space=pltpu.SMEM)] +...  45 us
    all_to_all x2, starting transfers between devices, exchange(): arrived = lax.all_to_all(sent, GX_GY, 0, 0, tiled=True)  24.7 us
    ppermute x8, starting transfers between devices, swapped(): remote = lax.ppermute(to_remote, GX_GY, REMOTE)  21.6 us
    ppermute x8, waiting for transfers between devices, swapped(): remote = lax.ppermute(to_remote, GX_GY, REMOTE)  18.8 us
    all_to_all x2, waiting for transfers between devices, exchange(): arrived = lax.all_to_all(sent, GX_GY, 0, 0, tiled=True)  13.4 us
    pallas_call x5, Pallas kernels, small_call(): pl.pallas_call(kernel, in_specs=[pl.BlockSpec(memory_space=pltpu.SMEM)] *...  4.55 us
  transfers between devices with their start and end apart: 18, of which 5 were waited for; matrix products, arithmetic and copies ran while one was open for 1% of the time, Pallas kernels for 1%

profile of v5, /device:TPU:1, one launch (start us, length us, event | category | flops | bytes accessed | tf_op | source)
XLA Modules:
  0.0 199.0 jit_solution(7885714377453147046)
XLA Ops:
  0.7 1.3 constant_dynamic-slice_fusion.2
  1.9 4.6 %collective-permute-start.1 = (f32[768,128]{1,0:T(8,128)S(1)}, f32[768,128]{1,0:T(8,128)S(1)}, u32[]{:S(2)}, u32[]{:S(2)}) collective-permute-start(f32[768,128]{1,0:T(8,128)S(1)} %get-tuple-element.76), channel_id=1, source_target_pairs={{1,2},{3,4},{5,6},{7,8},{9,10},{11,12},{13,14},{15,16},{17,18},{19... | collective-permute-start | bytes 1179656 | tf_op jit(solution)/shard_map/ppermute | solution.py:440
  7.3 4.6 %collective-permute-done.1.remote.basis_remote = f32[768,128]{1,0:T(8,128)S(1)} collective-permute-done((f32[768,128]{1,0:T(8,128)S(1)}, f32[768,128]{1,0:T(8,128)S(1)}, u32[]{:S(2)}, u32[]{:S(2)}) %collective-permute-start.1) | collective-permute-done | bytes 393248 | tf_op jit(solution)/shard_map/ppermute | solution.py:440
  12.0 9.8 %shard_map.68 = (f32[1024,128]{1,0:T(8,128)S(1)}, f32[768,128]{1,0:T(8,128)}, f32[768,128]{1,0:T(8,128)S(1)}, f32[384,128]{1,0:T(8,128)}) custom-call(s32[2]{0:T(128)S(1)} %pad_add_fusion.place, f32[1024,128]{1,0:T(8,128)S(1)} %copy-done, f32[768,128]{1,0:T(8,128)S(1)} %collective-permute-done.partner.basis_partner, ...), custom_call_target="tpu_custom_call" | custom-call | flops 4294967296 | bytes 16777216 | tf_op jit(solution)/shard_map/pallas_call | solution.py:400
  21.9 3.7 %collective-permute-start.5 = (f32[768,128]{1,0:T(8,128)S(1)}, f32[768,128]{1,0:T(8,128)}, u32[]{:S(2)}, u32[]{:S(2)}) collective-permute-start(f32[768,128]{1,0:T(8,128)S(1)} %get-tuple-element.41), channel_id=1, source_target_pairs={{1,2},{3,4},{5,6},{7,8},{9,10},{11,12},{13,14},{15,16},{17,18},{19... | collective-permute-start | bytes 1179656 | tf_op jit(solution)/shard_map/ppermute | solution.py:440
  25.6 1.0 constant_dynamic-slice_fusion
  26.5 1.9 collective-permute-start.3
  28.6 18.6 %all-to-all-start = ((f32[128,1,384]{2,1,0:T(1,128)}), f32[128,1,384]{2,1,0:T(1,128)S(1)}, u32[]{:S(2)}, u32[]{:S(2)}) async-start(f32[128,1,384]{2,1,0:T(1,128)} %bitcast.1), calls=%async_computation | async-start | bytes 393216 | tf_op jit(solution)/shard_map/all_to_all | solution.py:452
  47.9 1.0 copy-done.6
  48.9 1.2 shard_map.70
  50.1 0.8 copy-done.2
  50.8 1.1 collective-permute-start.6
  51.9 2.6 %collective-permute-start.7 = (f32[768,128]{1,0:T(8,128)S(1)}, f32[768,128]{1,0:T(8,128)S(1)}, u32[]{:S(2)}, u32[]{:S(2)}) collective-permute-start(f32[768,128]{1,0:T(8,128)S(1)} %get-tuple-element.44), channel_id=1, source_target_pairs={{1,2},{3,4},{5,6},{7,8},{9,10},{11,12},{13,14},{15,16},{17,18},{19... | collective-permute-start | bytes 1179656 | tf_op jit(solution)/shard_map/ppermute | solution.py:440
  54.5 3.0 %all-to-all-done = f32[128,1,384]{2,1,0:T(1,128)S(1)} async-done(((f32[128,1,384]{2,1,0:T(1,128)}), f32[128,1,384]{2,1,0:T(1,128)S(1)}, u32[]{:S(2)}, u32[]{:S(2)}) %all-to-all-start) | async-done | bytes 196640 | tf_op jit(solution)/shard_map/all_to_all | solution.py:452
  58.2 6.1 %all-to-all-start.1 = ((f32[128,1,384]{2,1,0:T(1,128)}), f32[128,1,384]{2,1,0:T(1,128)S(1)}, u32[]{:S(2)}, u32[]{:S(2)}) async-start(f32[128,1,384]{2,1,0:T(1,128)} %bitcast.3), calls=%async_computation.1 | async-start | bytes 393216 | tf_op jit(solution)/shard_map/all_to_all | solution.py:452
  64.4 10.4 %all-to-all-done.1 = f32[128,1,384]{2,1,0:T(1,128)S(1)} async-done(((f32[128,1,384]{2,1,0:T(1,128)}), f32[128,1,384]{2,1,0:T(1,128)S(1)}, u32[]{:S(2)}, u32[]{:S(2)}) %all-to-all-start.1) | async-done | bytes 196640 | tf_op jit(solution)/shard_map/all_to_all | solution.py:452
  74.7 13.1 %shard_map.71 = (f32[1024,128]{1,0:T(8,128)}, f32[768,128]{1,0:T(8,128)S(1)}, f32[768,128]{1,0:T(8,128)S(1)}, f32[640,128]{1,0:T(8,128)S(1)}, f32[2560,128]{1,0:...) custom-call(s32[2]{0:T(128)S(1)} %pad_add_fusion.place, ...), custom_call_target="tpu_custom_call" | custom-call | flops 4294967296 | bytes 16777216 | tf_op jit(solution)/shard_map/pallas_call | solution.py:400
  87.8 0.7 collective-permute-start.8
  88.6 2.0 %collective-permute-start.9 = (f32[768,128]{1,0:T(8,128)S(1)}, f32[768,128]{1,0:T(8,128)S(1)}, u32[]{:S(2)}, u32[]{:S(2)}) collective-permute-start(f32[768,128]{1,0:T(8,128)S(1)} %get-tuple-element.48), channel_id=1, source_target_pairs={{1,2},{3,4},{5,6},{7,8},{9,10},{11,12},{13,14},{15,16},{17,18},{19... | collective-permute-start | bytes 1179656 | tf_op jit(solution)/shard_map/ppermute | solution.py:440
  90.7 7.0 %collective-permute-done.9.remote = f32[768,128]{1,0:T(8,128)S(1)} collective-permute-done((f32[768,128]{1,0:T(8,128)S(1)}, f32[768,128]{1,0:T(8,128)S(1)}, u32[]{:S(2)}, u32[]{:S(2)}) %collective-permute-start.9) | collective-permute-done | bytes 393248 | tf_op jit(solution)/shard_map/ppermute | solution.py:440
  97.7 1.0 copy-done.4
  99.5 2.5 %collective-permute-start.11 = (f32[768,128]{1,0:T(8,128)S(1)}, f32[768,128]{1,0:T(8,128)S(1)}, u32[]{:S(2)}, u32[]{:S(2)}) collective-permute-start(f32[768,128]{1,0:T(8,128)S(1)} %get-tuple-element.51), channel_id=1, source_target_pairs={{1,2},{3,4},{5,6},{7,8},{9,10},{11,12},{13,14},{15,16},{17,18},{19... | collective-permute-start | bytes 1179656 | tf_op jit(solution)/shard_map/ppermute | solution.py:440
  102.0 22.3 %all_to_all.25 = f32[128,1,640]{2,1,0:T(1,128)S(1)} all-to-all(f32[128,1,640]{2,1,0:T(1,128)S(1)} %bitcast.14), channel_id=1, replica_groups=mesh['gx'=4,'gy_0'=4,'gy_1'=4,'gy_2'=2] {'gx','gy_0','gy_1','gy_2'}, dimensions={0} | all-to-all | bytes 655360 | tf_op jit(solution)/shard_map/all_to_all | solution.py:452
  124.3 10.9 %shard_map.73 = (f32[1024,128]{1,0:T(8,128)S(1)}, f32[768,128]{1,0:T(8,128)S(1)}, f32[768,128]{1,0:T(8,128)S(1)}, f32[640,128]{1,0:T(8,128)S(1)}, f32[2560,128]{...) custom-call(s32[2]{0:T(128)S(1)} %pad_add_fusion.place, f32[640,128]{1,0:T(8,128)S(1)} %bitcast.12, ...), custom_call_target="tpu_custom_call" | custom-call | flops 4294967296 | bytes 16777216 | tf_op jit(solution)/shard_map/pallas_call | solution.py:400
  135.2 1.1 collective-permute-start.12
  136.4 1.9 collective-permute-start.13
  138.3 7.2 %collective-permute-done.13.remote = f32[768,128]{1,0:T(8,128)S(1)} collective-permute-done((f32[768,128]{1,0:T(8,128)S(1)}, f32[768,128]{1,0:T(8,128)S(1)}, u32[]{:S(2)}, u32[]{:S(2)}) %collective-permute-start.13) | collective-permute-done | bytes 393248 | tf_op jit(solution)/shard_map/ppermute | solution.py:440
  146.3 2.3 %collective-permute-start.15 = (f32[768,128]{1,0:T(8,128)S(1)}, f32[768,128]{1,0:T(8,128)S(1)}, u32[]{:S(2)}, u32[]{:S(2)}) collective-permute-start(f32[768,128]{1,0:T(8,128)S(1)} %get-tuple-element.61), channel_id=1, source_target_pairs={{1,2},{3,4},{5,6},{7,8},{9,10},{11,12},{13,14},{15,16},{17,18},{19... | collective-permute-start | bytes 1179656 | tf_op jit(solution)/shard_map/ppermute | solution.py:440
  148.6 22.5 %all_to_all.26 = f32[128,1,640]{2,1,0:T(1,128)S(1)} all-to-all(f32[128,1,640]{2,1,0:T(1,128)S(1)} %bitcast.15), channel_id=1, replica_groups=mesh['gx'=4,'gy_0'=4,'gy_1'=4,'gy_2'=2] {'gx','gy_0','gy_1','gy_2'}, dimensions={0} | all-to-all | bytes 655360 | tf_op jit(solution)/shard_map/all_to_all | solution.py:452
  171.1 11.1 %shard_map.75 = (f32[512,128]{1,0:T(8,128)S(1)}, f32[1024,128]{1,0:T(8,128)S(1)}, f32[1024,128]{1,0:T(8,128)S(1)}, f32[1024,128]{1,0:T(8,128)S(1)}, f32[8,128]{1,0:T(8,128)S(1)}, /*index=5*/f32[6,128,128]{2,1,0:T(8,128)S(1)}) custom-call(s32[2]{0:T(128)S(1)} %pad_add_fusion.place, f32[640,128]{1,0:T(8,128)S(1)} %bitcast.11, ...), custom_call_target="tpu_custom_call" | custom-call | flops 4294967296 | bytes 16777216 | tf_op jit(solution)/shard_map/pallas_call | solution.py:400
  182.3 15.5 %all_to_all.27 = f32[128,1,512]{2,1,0:T(1,128)S(1)} all-to-all(f32[128,1,512]{2,1,0:T(1,128)S(1)} %bitcast.16), channel_id=1, replica_groups=mesh['gx'=4,'gy_0'=4,'gy_1'=4,'gy_2'=2] {'gx','gy_0','gy_1','gy_2'}, dimensions={0} | all-to-all | bytes 524288 | tf_op jit(solution)/shard_map/all_to_all | solution.py:452
  197.8 1.3 shard_map.76
  (33 shorter events, 3.4 us)
Async XLA Ops:
  0.6 11.3 %copy-start = (f32[1024,128]{1,0:T(8,128)S(1)}, f32[1024,128]{1,0:T(8,128)}, u32[]{:S(2)}) copy-start(f32[1024,128]{1,0:T(8,128)} %basis.1) | copy-start | bytes 1572868
  0.6 11.3 %copy-start.1 = (f32[1024,128]{1,0:T(8,128)S(1)}, f32[1024,128]{1,0:T(8,128)}, u32[]{:S(2)}) copy-start(f32[1024,128]{1,0:T(8,128)} %right_own.1) | copy-start | bytes 1572868
  1.9 10.0 %collective-permute-start.1 = (f32[768,128]{1,0:T(8,128)S(1)}, f32[768,128]{1,0:T(8,128)S(1)}, u32[]{:S(2)}, u32[]{:S(2)}) collective-permute-start(f32[768,128]{1,0:T(8,128)S(1)} %get-tuple-element.76), channel_id=1, source_target_pairs={{1,2},{3,4},{5,6},{7,8},{9,10},{11,12},{13,14},{15,16},{17,18},{19... | collective-permute-start | bytes 1179656 | tf_op jit(solution)/shard_map/ppermute | solution.py:440
  6.5 5.4 %collective-permute-start = (f32[768,128]{1,0:T(8,128)S(1)}, f32[768,128]{1,0:T(8,128)S(1)}, u32[]{:S(2)}, u32[]{:S(2)}) collective-permute-start(f32[768,128]{1,0:T(8,128)S(1)} %get-tuple-element.77), channel_id=1, source_target_pairs={{0,1},{1,0},{2,3},{3,2},{4,5},{5,4},{6,7},{7,6},{8,9},{9,8},{10,11... | collective-permute-start | bytes 1179656 | tf_op jit(solution)/shard_map/ppermute | solution.py:441
  21.8 25.3 %collective-permute-start.4 = (f32[768,128]{1,0:T(8,128)}, f32[768,128]{1,0:T(8,128)S(1)}, u32[]{:S(2)}, u32[]{:S(2)}) collective-permute-start(f32[768,128]{1,0:T(8,128)} %get-tuple-element.40), channel_id=1, source_target_pairs={{0,1},{1,0},{2,3},{3,2},{4,5},{5,4},{6,7},{7,6},{8,9},{9,8},{10,11... | collective-permute-start | bytes 1179656 | tf_op jit(solution)/shard_map/ppermute | solution.py:441
  21.9 26.0 %collective-permute-start.5 = (f32[768,128]{1,0:T(8,128)S(1)}, f32[768,128]{1,0:T(8,128)}, u32[]{:S(2)}, u32[]{:S(2)}) collective-permute-start(f32[768,128]{1,0:T(8,128)S(1)} %get-tuple-element.41), channel_id=1, source_target_pairs={{1,2},{3,4},{5,6},{7,8},{9,10},{11,12},{13,14},{15,16},{17,18},{19... | collective-permute-start | bytes 1179656 | tf_op jit(solution)/shard_map/ppermute | solution.py:440
  26.5 37.8 %collective-permute-start.3 = (f32[768,128]{1,0:T(8,128)}, f32[768,128]{1,0:T(8,128)S(1)}, u32[]{:S(2)}, u32[]{:S(2)}) collective-permute-start(f32[768,128]{1,0:T(8,128)} %get-tuple-element.74), channel_id=1, source_target_pairs={{1,2},{3,4},{5,6},{7,8},{9,10},{11,12},{13,14},{15,16},{17,18},{19... | collective-permute-start | bytes 1179656 | tf_op jit(solution)/shard_map/ppermute | solution.py:440
  28.5 35.9 %collective-permute-start.2 = (f32[768,128]{1,0:T(8,128)}, f32[768,128]{1,0:T(8,128)S(1)}, u32[]{:S(2)}, u32[]{:S(2)}) collective-permute-start(f32[768,128]{1,0:T(8,128)} %get-tuple-element.75), channel_id=1, source_target_pairs={{0,1},{1,0},{2,3},{3,2},{4,5},{5,4},{6,7},{7,6},{8,9},{9,8},{10,11... | collective-permute-start | bytes 1179656 | tf_op jit(solution)/shard_map/ppermute | solution.py:441
  28.6 28.9 %all-to-all-start = ((f32[128,1,384]{2,1,0:T(1,128)}), f32[128,1,384]{2,1,0:T(1,128)S(1)}, u32[]{:S(2)}, u32[]{:S(2)}) async-start(f32[128,1,384]{2,1,0:T(1,128)} %bitcast.1), calls=%async_computation | async-start | bytes 393216 | tf_op jit(solution)/shard_map/all_to_all | solution.py:452
  47.1 0.7 copy-start.5
  47.9 1.0 copy-start.6
  50.0 0.8 copy-start.2
  50.8 23.9 %collective-permute-start.6 = (f32[768,128]{1,0:T(8,128)S(1)}, f32[768,128]{1,0:T(8,128)S(1)}, u32[]{:S(2)}, u32[]{:S(2)}) collective-permute-start(f32[768,128]{1,0:T(8,128)S(1)} %get-tuple-element.43), channel_id=1, source_target_pairs={{0,1},{1,0},{2,3},{3,2},{4,5},{5,4},{6,7},{7,6},{8,9},{9,8},{10,11... | collective-permute-start | bytes 1179656 | tf_op jit(solution)/shard_map/ppermute | solution.py:441
  51.9 22.8 %collective-permute-start.7 = (f32[768,128]{1,0:T(8,128)S(1)}, f32[768,128]{1,0:T(8,128)S(1)}, u32[]{:S(2)}, u32[]{:S(2)}) collective-permute-start(f32[768,128]{1,0:T(8,128)S(1)} %get-tuple-element.44), channel_id=1, source_target_pairs={{1,2},{3,4},{5,6},{7,8},{9,10},{11,12},{13,14},{15,16},{17,18},{19... | collective-permute-start | bytes 1179656 | tf_op jit(solution)/shard_map/ppermute | solution.py:440
  57.5 17.2 %copy-start.3 = (f32[128,128]{1,0:T(8,128)S(1)}, f32[128,128]{1,0:T(8,128)}, u32[]{:S(2)}) copy-start(f32[128,128]{1,0:T(8,128)} %load.1) | copy-start | bytes 196612
  58.2 16.5 %all-to-all-start.1 = ((f32[128,1,384]{2,1,0:T(1,128)}), f32[128,1,384]{2,1,0:T(1,128)S(1)}, u32[]{:S(2)}, u32[]{:S(2)}) async-start(f32[128,1,384]{2,1,0:T(1,128)} %bitcast.3), calls=%async_computation.1 | async-start | bytes 393216 | tf_op jit(solution)/shard_map/all_to_all | solution.py:452
  87.8 2.8 %collective-permute-start.8 = (f32[768,128]{1,0:T(8,128)S(1)}, f32[768,128]{1,0:T(8,128)S(1)}, u32[]{:S(2)}, u32[]{:S(2)}) collective-permute-start(f32[768,128]{1,0:T(8,128)S(1)} %get-tuple-element.47), channel_id=1, source_target_pairs={{0,1},{1,0},{2,3},{3,2},{4,5},{5,4},{6,7},{7,6},{8,9},{9,8},{10,11... | collective-permute-start | bytes 1179656 | tf_op jit(solution)/shard_map/ppermute | solution.py:441
  88.6 9.1 %collective-permute-start.9 = (f32[768,128]{1,0:T(8,128)S(1)}, f32[768,128]{1,0:T(8,128)S(1)}, u32[]{:S(2)}, u32[]{:S(2)}) collective-permute-start(f32[768,128]{1,0:T(8,128)S(1)} %get-tuple-element.48), channel_id=1, source_target_pairs={{1,2},{3,4},{5,6},{7,8},{9,10},{11,12},{13,14},{15,16},{17,18},{19... | collective-permute-start | bytes 1179656 | tf_op jit(solution)/shard_map/ppermute | solution.py:440
  97.7 1.0 copy-start.4
  99.4 24.9 %collective-permute-start.10 = (f32[768,128]{1,0:T(8,128)S(1)}, f32[768,128]{1,0:T(8,128)S(1)}, u32[]{:S(2)}, u32[]{:S(2)}) collective-permute-start(f32[768,128]{1,0:T(8,128)S(1)} %get-tuple-element.50), channel_id=1, source_target_pairs={{0,1},{1,0},{2,3},{3,2},{4,5},{5,4},{6,7},{7,6},{8,9},{9,8},{10,11... | collective-permute-start | bytes 1179656 | tf_op jit(solution)/shard_map/ppermute | solution.py:441
  99.5 24.8 %collective-permute-start.11 = (f32[768,128]{1,0:T(8,128)S(1)}, f32[768,128]{1,0:T(8,128)S(1)}, u32[]{:S(2)}, u32[]{:S(2)}) collective-permute-start(f32[768,128]{1,0:T(8,128)S(1)} %get-tuple-element.51), channel_id=1, source_target_pairs={{1,2},{3,4},{5,6},{7,8},{9,10},{11,12},{13,14},{15,16},{17,18},{19... | collective-permute-start | bytes 1179656 | tf_op jit(solution)/shard_map/ppermute | solution.py:440
  135.2 3.1 %collective-permute-start.12 = (f32[768,128]{1,0:T(8,128)S(1)}, f32[768,128]{1,0:T(8,128)S(1)}, u32[]{:S(2)}, u32[]{:S(2)}) collective-permute-start(f32[768,128]{1,0:T(8,128)S(1)} %get-tuple-element.57), channel_id=1, source_target_pairs={{0,1},{1,0},{2,3},{3,2},{4,5},{5,4},{6,7},{7,6},{8,9},{9,8},{10,11... | collective-permute-start | bytes 1179656 | tf_op jit(solution)/shard_map/ppermute | solution.py:441
  136.4 9.1 %collective-permute-start.13 = (f32[768,128]{1,0:T(8,128)S(1)}, f32[768,128]{1,0:T(8,128)S(1)}, u32[]{:S(2)}, u32[]{:S(2)}) collective-permute-start(f32[768,128]{1,0:T(8,128)S(1)} %get-tuple-element.58), channel_id=1, source_target_pairs={{1,2},{3,4},{5,6},{7,8},{9,10},{11,12},{13,14},{15,16},{17,18},{19... | collective-permute-start | bytes 1179656 | tf_op jit(solution)/shard_map/ppermute | solution.py:440
  146.2 24.9 %collective-permute-start.14 = (f32[768,128]{1,0:T(8,128)S(1)}, f32[768,128]{1,0:T(8,128)S(1)}, u32[]{:S(2)}, u32[]{:S(2)}) collective-permute-start(f32[768,128]{1,0:T(8,128)S(1)} %get-tuple-element.60), channel_id=1, source_target_pairs={{0,1},{1,0},{2,3},{3,2},{4,5},{5,4},{6,7},{7,6},{8,9},{9,8},{10,11... | collective-permute-start | bytes 1179656 | tf_op jit(solution)/shard_map/ppermute | solution.py:441
  146.3 24.8 %collective-permute-start.15 = (f32[768,128]{1,0:T(8,128)S(1)}, f32[768,128]{1,0:T(8,128)S(1)}, u32[]{:S(2)}, u32[]{:S(2)}) collective-permute-start(f32[768,128]{1,0:T(8,128)S(1)} %get-tuple-element.61), channel_id=1, source_target_pairs={{1,2},{3,4},{5,6},{7,8},{9,10},{11,12},{13,14},{15,16},{17,18},{19... | collective-permute-start | bytes 1179656 | tf_op jit(solution)/shard_map/ppermute | solution.py:440
